TPU v7x, 64 devices: a 2x2x8 block of a 4x4x8 slice. The times are simulated.
64 devices in a mesh: rep: 8 (over x, y, core), dp: 8 (over z).
Axes of the slice: x: 2, y: 2, z: 8, core: 2. Of those that a mesh axis runs over, the one named last changes fastest.
The devices are a block of a 4x4x8 slice.
Arguments:
- x: bfloat16 [64, 4096, 512], P(('rep', 'dp')), parts along dimension 0
- dy: bfloat16 [64, 4096, 512], P(('rep', 'dp')), parts along dimension 0
- w_gate: bfloat16 [2, 512, 1792], replicated
- w_up: bfloat16 [2, 512, 1792], replicated
- w_down: bfloat16 [2, 1792, 512], replicated
- m_w_gate: float32 [2, 512, 1792], replicated
- m_w_up: float32 [2, 512, 1792], replicated
- m_w_down: float32 [2, 1792, 512], replicated
- v_w_gate: float32 [2, 512, 1792], replicated
- v_w_up: float32 [2, 512, 1792], replicated
- v_w_down: float32 [2, 1792, 512], replicated
Outputs:
- output 1: bfloat16 [16, 512, 1792], P('rep'), parts along dimension 0
- output 2: bfloat16 [16, 512, 1792], P('rep'), parts along dimension 0
- output 3: bfloat16 [16, 1792, 512], P('rep'), parts along dimension 0
- output 4: float32 [16, 512, 1792], P('rep'), parts along dimension 0
- output 5: float32 [16, 512, 1792], P('rep'), parts along dimension 0
- output 6: float32 [16, 1792, 512], P('rep'), parts along dimension 0
- output 7: float32 [16, 512, 1792], P('rep'), parts along dimension 0
- output 8: float32 [16, 512, 1792], P('rep'), parts along dimension 0
- output 9: float32 [16, 1792, 512], P('rep'), parts along dimension 0
There are 8 independent parts. A program takes and returns all parts, laid end to end along the dimension named above; an argument that names none is the same for every part.
All inputs are finite; a program needn't handle non-finite values.
Results may differ from a plain program's by a relative error of at most 0.02.
Values are sent between devices in bfloat16 or wider.
A program may use at most 768 MiB of HBM per device.

v0:
```python
import jax
import jax.numpy as jnp
from jax import lax
from jax.sharding import PartitionSpec as P

NAMES = ("w_gate", "w_up", "w_down")


def matmul(a, w):
    return jnp.dot(a, w, preferred_element_type=jnp.float32).astype(jnp.bfloat16)


def normed(h):
    wide = h.astype(jnp.float32)
    scale = lax.rsqrt(jnp.mean(wide**2, -1, keepdims=True) + 1e-6)
    return (wide * scale).astype(jnp.bfloat16)


def layer(h, w):
    a = normed(h)
    gate = jnp.dot(a, w["w_gate"], preferred_element_type=jnp.float32)
    up = jnp.dot(a, w["w_up"], preferred_element_type=jnp.float32)
    return h + matmul((jax.nn.silu(gate) * up).astype(jnp.bfloat16), w["w_down"])


def adamw(w, m, v, g):
    m = 0.9 * m + 0.1 * g
    v = 0.95 * v + 0.05 * g * g
    step = m * lax.rsqrt(v + 1e-8) + 0.1 * w
    return (w - 0.02 * step).astype(jnp.bfloat16), m, v


def solution(mesh):
    def step(x, dy, *arrays):
        weights, m, v = (arrays[i : i + 3] for i in (0, 3, 6))
        layers = weights[0].shape[0]
        h, kept = x[0], []
        for number in range(layers):
            kept.append(h)
            h = layer(h, {name: w[number] for name, w in zip(NAMES, weights, strict=True)})
        by_h, summed = dy[0], [None] * layers
        for number in reversed(range(layers)):
            _, back = jax.vjp(lambda w, h: layer(h, w), {name: w[number] for name, w in zip(NAMES, weights, strict=True)}, kept[number])
            by_w, by_h = back(by_h)
            summed[number] = [lax.psum(by_w[name], "dp") for name in NAMES]
        gradients = [jnp.stack([summed[number][i] for number in range(layers)]).astype(jnp.float32) for i in range(3)]
        new = [adamw(w.astype(jnp.float32), m, v, g) for w, m, v, g in zip(weights, m, v, gradients, strict=True)]
        return tuple(one[which] for which in range(3) for one in new)

    return jax.shard_map(
        step,
        mesh=mesh,
        in_specs=(P(("rep", "dp"), None, None),) * 2 + (P(None, None, None),) * 9,
        out_specs=(P("rep", None, None),) * 9,
        check_vma=False,
    )
```

profile of v0, /device:TPU:21, one launch (start us, length us, event | category | flops | bytes accessed | tf_op | source)
XLA Modules:
  0.0 589.9 jit_solution(1022923379184718878)
XLA Ops:
  7.2 0.1 all-reduce.3.cloned.1.call-start
  7.3 6.3 %copy.20 = bf16[1,4096,512]{1,2,0:T(8,128)(2,1)} copy(bf16[1,4096,512]{2,1,0:T(8,128)(2,1)} %param.11) | data formatting | bytes 8388608 | tf_op args[0]
  13.6 3.1 fusion.15
  16.7 0.0 copy-start.15
  16.7 6.3 %copy.21 = bf16[1,4096,512]{1,2,0:T(8,128)(2,1)} copy(bf16[1,4096,512]{2,1,0:T(8,128)(2,1)} %param.12) | data formatting | bytes 8388608 | tf_op args[1]
  23.0 0.0 copy-start.2
  23.0 0.0 copy-start.7
  23.0 13.3 %convolution_convert_fusion.1 = bf16[4096,1792]{1,0:T(8,128)(2,1)} fusion(bf16[1,4096,512]{2,1,0:T(8,128)(2,1)} %param.12, bf16[2,1792,512]{2,1,0:T(8,128)(2,1)} %param.15), kind=kOutput, calls=%fused_computation.23 | convolution fusion | flops 7523532800 | bytes 20709376 | tf_op jit(solution)/shard_map/transpose(jvp())/dot_general | solution.py:10
  36.3 0.0 copy-done.2
  36.3 0.0 copy-done.7
  36.3 13.4 %fusion.88 = f32[4096,1792]{1,0:T(8,128)} fusion(bf16[2,512,1792]{2,1,0:T(8,128)(2,1)S(1)} %copy-done.7, bf16[1,4096,512]{2,1,0:T(8,128)(2,1)S(1)} %copy-done.2, f32[4096]{0:T(1024)S(1)} %add_rsqrt_fusion), kind=kOutput, calls=%fused_computation.103 | convolution fusion | flops 7522484224 | bytes 35405824 | tf_op jit(solution)/shard_map/dot_general | solution.py:21
  49.6 0.0 copy-done.15
  49.6 29.1 %multiply_convert_fusion.1 = (bf16[4096,1792]{1,0:T(8,128)(2,1)}, f32[4096,1792]{1,0:T(8,128)}) fusion(f32[4096,1792]{1,0:T(8,128)} %fusion.88, bf16[2,512,1792]{2,1,0:T(8,128)(2,1)} %param.14, bf16[1,4096,512]{2,1,0:T(8,128)(2,1)} %param.11, f32[4096]{0:T(1024)S(1)} %add_rsqrt_fusion), kind=kOutput, calls=%fused_computation.17 | convolution fusion | flops 7566524416 | bytes 79446016 | tf_op jit(solution)/shard_map/dot_general | solution.py:22
  78.7 0.0 copy-start.10
  78.7 13.2 %fusion.19 = (f32[4096]{0:T(1024)S(1)}, bf16[4096,512]{0,1:T(8,128)(2,1)S(1)}) fusion(bf16[4096,1792]{1,0:T(8,128)(2,1)} %get-tuple-element.24, bf16[2,1792,512]{2,1,0:T(8,128)(2,1)} %param.15, bf16[1,4096,512]{1,2,0:T(8,128)(2,1)} %copy.20), kind=kOutput, calls=%fused_computation.49 | convolution fusion | flops 7526674432 | bytes 24920064 | tf_op jit(solution)/shard_map/dot_general | solution.py:10
  91.9 0.0 copy-start.13
  91.9 0.0 copy-start.3
  92.0 0.6 copy-done.13
  92.5 0.0 copy-done.10
  92.6 13.6 %fusion.75 = f32[4096,1792]{1,0:T(8,128)} fusion(bf16[4096,512]{0,1:T(8,128)(2,1)S(1)} %get-tuple-element.27, f32[4096]{0:T(1024)S(1)} %fusion.101, bf16[2,512,1792]{2,1,0:T(8,128)(2,1)S(1)} %copy-done.10), kind=kOutput, calls=%fused_computation.92 | convolution fusion | flops 7522484224 | bytes 35405824 | tf_op jit(solution)/shard_map/jvp()/dot_general | solution.py:22
  106.1 0.0 copy-done.3
  106.1 33.8 %fusion.2 = (bf16[4096,1792]{1,0:T(8,128)(2,1)}, f32[4096,1792]{1,0:T(8,128)}) fusion(f32[4096,1792]{1,0:T(8,128)} %fusion.75, bf16[4096,1792]{1,0:T(8,128)(2,1)} %convolution_convert_fusion.1, bf16[2,512,1792]{2,1,0:T(8,128)(2,1)} %param.13, bf16[4096,512]{0,1:T(8,128)(2,1)S(1)} %get-tuple-element.27, f32[4096]{0:T(1024)S(1)} %fusion.101), kind=kOutput, calls=%fused_computation.8 | convolution fusion | flops 7610564608 | bytes 94126080 | tf_op jit(solution)/shard_map/jvp()/dot_general | solution.py:21
  139.9 23.4 %fusion.59 = bf16[1,1792,512]{2,1,0:T(8,128)(2,1)} fusion(bf16[1,4096,512]{2,1,0:T(8,128)(2,1)} %param.12, f32[4096,1792]{1,0:T(8,128)} %fusion.75, f32[4096,1792]{1,0:T(8,128)} %get-tuple-element.29), kind=kOutput, calls=%fused_computation.86 | convolution fusion | flops 7561150464 | bytes 64749568 | tf_op jit(solution)/shard_map/transpose(jvp())/dot_general | solution.py:10
  163.3 0.0 copy-start.11
  163.3 21.2 %fusion.72 = bf16[1,512,1792]{2,1,0:T(8,128)(2,1)} fusion(bf16[4096,1792]{1,0:T(8,128)(2,1)} %convolution_convert_fusion.1, bf16[4096,512]{0,1:T(8,128)(2,1)} %copy-done.3, f32[4096]{0:T(1024)S(1)} %fusion.101, f32[4096,1792]{1,0:T(8,128)} %get-tuple-element.29), kind=kOutput, calls=%fused_computation.91 | convolution fusion | flops 7567441920 | bytes 50085888 | tf_op jit(solution)/shard_map/transpose(jvp())/dot_general | solution.py:22
  184.6 0.0 copy-done.11
  184.6 0.0 copy-start.4
  184.6 19.1 %fusion.37 = bf16[4096,512]{0,1:T(8,128)(2,1)} fusion(bf16[4096,1792]{1,0:T(8,128)(2,1)} %convolution_convert_fusion.1, bf16[2,512,1792]{2,1,0:T(8,128)(2,1)S(1)} %copy-done.11, f32[4096,1792]{1,0:T(8,128)} %get-tuple-element.29), kind=kOutput, calls=%fused_computation.68 | convolution fusion | flops 7562330112 | bytes 50069504 | tf_op jit(solution)/shard_map/transpose(jvp())/dot_general | solution.py:22
  203.7 0.0 copy-done.4
  203.7 0.0 copy-start.8
  203.7 13.2 %fusion.71 = bf16[1,512,1792]{2,1,0:T(8,128)(2,1)} fusion(bf16[4096,1792]{1,0:T(8,128)(2,1)} %get-tuple-element.28, bf16[4096,512]{0,1:T(8,128)(2,1)S(1)} %copy-done.4, f32[4096]{0:T(1024)S(1)} %fusion.101), kind=kOutput, calls=%fused_computation.90 | convolution fusion | flops 7522484224 | bytes 20725760 | tf_op jit(solution)/shard_map/transpose(jvp())/dot_general | solution.py:21
  216.9 0.0 copy-done.8
  216.9 0.0 copy-start.14
  216.9 0.0 copy-start.1
  216.9 12.3 %fusion.21 = (f32[4096]{0:T(1024)S(1)}, bf16[4096,512]{0,1:T(8,128)(2,1)S(1)}) fusion(bf16[4096,512]{0,1:T(8,128)(2,1)S(1)} %copy-done.4, bf16[4096,512]{0,1:T(8,128)(2,1)} %fusion.37, bf16[4096,1792]{1,0:T(8,128)(2,1)} %get-tuple-element.28, bf16[2,512,1792]{2,1,0:T(8,128)(2,1)S(1)} %copy-done.8), kind=kOutput, calls=%fused_computation.51 | convolution fusion | flops 7526674432 | bytes 29114368 | tf_op jit(solution)/shard_map/transpose(jvp())/dot_general | solution.py:21
  229.2 0.0 copy-done.14
  229.2 0.0 copy-done.1
  229.3 2.9 fusion.42
  232.1 0.0 copy-start.5
  232.1 2.0 copy-done.5
  234.1 0.0 copy-start.6
  234.1 12.5 %fusion.65 = bf16[1,1792,512]{2,1,0:T(8,128)(2,1)} fusion(bf16[4096,1792]{1,0:T(8,128)(2,1)} %get-tuple-element.24, bf16[4096,512]{0,1:T(8,128)(2,1)S(1)} %fusion.42), kind=kOutput, calls=%fused_computation.88 | convolution fusion | flops 7517110272 | bytes 20709376 | tf_op jit(solution)/shard_map/transpose(jvp())/dot_general | solution.py:10
  246.6 0.0 copy-done.6
  246.6 0.0 copy-start
  246.6 0.0 copy-start.16
  246.6 14.7 %convolution_convert_fusion = bf16[4096,1792]{1,0:T(8,128)(2,1)} fusion(bf16[4096,512]{0,1:T(8,128)(2,1)} %copy-done.5, bf16[2,1792,512]{2,1,0:T(8,128)(2,1)S(1)} %copy-done.6), kind=kOutput, calls=%fused_computation.22 | convolution fusion | flops 7523532800 | bytes 20709376 | tf_op jit(solution)/shard_map/transpose(jvp())/dot_general | solution.py:10
  261.3 0.0 copy-done
  261.4 0.0 copy-done.16
  261.4 18.3 %fusion.62 = bf16[1,512,1792]{2,1,0:T(8,128)(2,1)} fusion(bf16[4096,1792]{1,0:T(8,128)(2,1)} %convolution_convert_fusion, f32[4096,1792]{1,0:T(8,128)} %fusion.88, bf16[1,4096,512]{1,2,0:T(8,128)(2,1)S(1)} %copy-done, f32[4096]{0:T(1024)S(1)} %copy-done.16), kind=kOutput, calls=%fused_computation.87 | convolution fusion | flops 7567441920 | bytes 50085888 | tf_op jit(solution)/shard_map/transpose(jvp())/dot_general | solution.py:22
  279.7 27.7 %fusion.66 = bf16[1,512,1792]{2,1,0:T(8,128)(2,1)} fusion(f32[4096,1792]{1,0:T(8,128)} %fusion.88, f32[4096,1792]{1,0:T(8,128)} %get-tuple-element.25, bf16[4096,1792]{1,0:T(8,128)(2,1)} %convolution_convert_fusion, bf16[1,4096,512]{1,2,0:T(8,128)(2,1)S(1)} %copy-done, f32[4096]{0:T(1024)S(1)} %copy-done.16), kind=kOutput, calls=%fused_computation.89 | convolution fusion | flops 7604142080 | bytes 79446016 | tf_op jit(solution)/shard_map/transpose(jvp())/dot_general | solution.py:21
  307.4 0.0 slice-start
  307.4 0.1 all-reduce.3.cloned.1.call-update
  307.5 235.3 %all-reduce.3.cloned.1.call-done = (bf16[1,512,1792]{2,1,0:T(8,128)(2,1)}, bf16[1,512,1792]{2,1,0:T(8,128)(2,1)}, bf16[1,512,1792]{2,1,0:T(8,128)(2,1)}, bf16[1,...) async-done(((bf16[1,512,1792]{2,1,0:T(8,128)(2,1)}, bf16[1,512,1792]{2,1,0:T(8,128)(2,1)}, bf16[1,512,1792]{2,1,0:T(8,128)(2,1)}, ...) | async-done | bytes 11010064 | tf_op jit(solution)/shard_map/psum | solution.py:45
  542.8 0.0 slice-start.1
  542.8 0.0 copy-start.9
  542.8 0.0 copy-start.12
  542.8 15.3 %fusion.32 = (bf16[2,1792,512]{2,1,0:T(8,128)(2,1)}, f32[2,1792,512]{2,1,0:T(8,128)}, f32[2,1792,512]{2,1,0:T(8,128)}) fusion(bf16[2,1792,512]{2,1,0:T(8,128)(2,1)} %param.15, bf16[1,1792,512]{2,1,0:T(8,128)(2,1)} %get-tuple-element.13, bf16[1,1792,512]{2,1,0:T(8,128)(2,1)} %get-tuple-element.14, f32[2,1792,512]{2,1,0:T(8,128)} %param.21, ...), kind=kLoop, calls=%fused_computation.63 | loop fusion | flops 34865152 | bytes 40370176 | tf_op jit(solution)/shard_map/convert_element_type | solution.py:30
  558.1 0.0 slice-done
  558.1 0.0 slice-done.1
  558.1 0.0 copy-done.9
  558.1 1.6 copy-done.12
  559.8 22.8 %fusion.24 = (bf16[2,512,1792]{2,1,0:T(8,128)(2,1)}, f32[2,512,1792]{2,1,0:T(8,128)}, f32[2,512,1792]{2,1,0:T(8,128)}, bf16[2,512,1792]{2,1,0:T(8,128)(2,1)}, f3...) fusion(bf16[2,512,1792]{2,1,0:T(8,128)(2,1)S(1)} %copy-done.9, bf16[1,512,1792]{2,1,0:T(8,128)(2,1)} %get-tuple-element.9, ...), kind=kLoop, calls=%fused_computation.55 | loop fusion | flops 69730304 | bytes 80740352 | tf_op jit(solution)/shard_map/convert_element_type | solution.py:30
  (4 shorter events, 0.0 us)
Async XLA Ops:
  7.2 535.6 %all-reduce.3.cloned.1.call-start = ((), (), s32[]{:S(2)}) async-start(), calls=%async_computation | async-start | bytes 22020096 | tf_op jit(solution)/shard_map/psum | solution.py:45
  16.7 33.0 %copy-start.15 = (f32[4096]{0:T(1024)}, f32[4096]{0:T(1024)S(1)}, u32[]{:S(2)}) copy-start(f32[4096]{0:T(1024)S(1)} %add_rsqrt_fusion) | copy-start | bytes 49156
  23.0 13.3 %copy-start.2 = (bf16[1,4096,512]{2,1,0:T(8,128)(2,1)S(1)}, bf16[1,4096,512]{2,1,0:T(8,128)(2,1)}, u32[]{:S(2)}) copy-start(bf16[1,4096,512]{2,1,0:T(8,128)(2,1)} %param.11) | copy-start | bytes 12582916
  23.0 13.3 %copy-start.7 = (bf16[2,512,1792]{2,1,0:T(8,128)(2,1)S(1)}, bf16[2,512,1792]{2,1,0:T(8,128)(2,1)}, u32[]{:S(2)}) copy-start(bf16[2,512,1792]{2,1,0:T(8,128)(2,1)} %param.13) | copy-start | bytes 11010052
  78.7 13.9 %copy-start.10 = (bf16[2,512,1792]{2,1,0:T(8,128)(2,1)S(1)}, bf16[2,512,1792]{2,1,0:T(8,128)(2,1)}, u32[]{:S(2)}) copy-start(bf16[2,512,1792]{2,1,0:T(8,128)(2,1)} %param.14) | copy-start | bytes 11010052
  91.9 0.6 copy-start.13
  91.9 14.2 %copy-start.3 = (bf16[4096,512]{0,1:T(8,128)(2,1)}, bf16[4096,512]{0,1:T(8,128)(2,1)S(1)}, u32[]{:S(2)}) copy-start(bf16[4096,512]{0,1:T(8,128)(2,1)S(1)} %get-tuple-element.27) | copy-start | bytes 12582916
  163.3 21.2 %copy-start.11 = (bf16[2,512,1792]{2,1,0:T(8,128)(2,1)S(1)}, bf16[2,512,1792]{2,1,0:T(8,128)(2,1)}, u32[]{:S(2)}) copy-start(bf16[2,512,1792]{2,1,0:T(8,128)(2,1)} %param.14) | copy-start | bytes 11010052
  184.6 19.1 %copy-start.4 = (bf16[4096,512]{0,1:T(8,128)(2,1)S(1)}, bf16[4096,512]{0,1:T(8,128)(2,1)}, u32[]{:S(2)}) copy-start(bf16[4096,512]{0,1:T(8,128)(2,1)} %copy-done.3) | copy-start | bytes 12582916
  203.7 13.2 %copy-start.8 = (bf16[2,512,1792]{2,1,0:T(8,128)(2,1)S(1)}, bf16[2,512,1792]{2,1,0:T(8,128)(2,1)}, u32[]{:S(2)}) copy-start(bf16[2,512,1792]{2,1,0:T(8,128)(2,1)} %param.13) | copy-start | bytes 11010052
  216.9 12.4 %copy-start.14 = (f32[4096]{0:T(1024)S(1)}, f32[4096]{0:T(1024)}, u32[]{:S(2)}) copy-start(f32[4096]{0:T(1024)} %copy-done.13) | copy-start | bytes 49156
  216.9 12.4 %copy-start.1 = (bf16[1,4096,512]{1,2,0:T(8,128)(2,1)S(1)}, bf16[1,4096,512]{1,2,0:T(8,128)(2,1)}, u32[]{:S(2)}) copy-start(bf16[1,4096,512]{1,2,0:T(8,128)(2,1)} %copy.21) | copy-start | bytes 12582916
  232.1 2.0 copy-start.5
  234.1 12.5 %copy-start.6 = (bf16[2,1792,512]{2,1,0:T(8,128)(2,1)S(1)}, bf16[2,1792,512]{2,1,0:T(8,128)(2,1)}, u32[]{:S(2)}) copy-start(bf16[2,1792,512]{2,1,0:T(8,128)(2,1)} %param.15) | copy-start | bytes 11010052
  246.6 14.7 %copy-start = (bf16[1,4096,512]{1,2,0:T(8,128)(2,1)S(1)}, bf16[1,4096,512]{1,2,0:T(8,128)(2,1)}, u32[]{:S(2)}) copy-start(bf16[1,4096,512]{1,2,0:T(8,128)(2,1)} %copy.20) | copy-start | bytes 12582916
  246.6 14.7 %copy-start.16 = (f32[4096]{0:T(1024)S(1)}, f32[4096]{0:T(1024)}, u32[]{:S(2)}) copy-start(f32[4096]{0:T(1024)} %copy-done.15) | copy-start | bytes 49156
  307.4 250.7 %slice-start = ((s8[7340032]{0:T(1024)(128)(4,1)}), s8[3145728]{0:T(1024)(128)(4,1)S(1)}, s32[]{:S(2)}) async-start(s8[7340032]{0:T(1024)(128)(4,1)} %bitcast.82), calls=%async_computation.1 | async-start | bytes 6291456
  542.8 15.4 %slice-start.1 = ((s8[7340032]{0:T(1024)(128)(4,1)}), s8[4194304]{0:T(1024)(128)(4,1)S(1)}, s32[]{:S(2)}) async-start(s8[7340032]{0:T(1024)(128)(4,1)} %bitcast.82), calls=%async_computation.2 | async-start | bytes 8388608
  542.8 15.4 %copy-start.9 = (bf16[2,512,1792]{2,1,0:T(8,128)(2,1)S(1)}, bf16[2,512,1792]{2,1,0:T(8,128)(2,1)}, u32[]{:S(2)}) copy-start(bf16[2,512,1792]{2,1,0:T(8,128)(2,1)} %param.13) | copy-start | bytes 11010052
  542.8 17.0 %copy-start.12 = (bf16[2,512,1792]{2,1,0:T(8,128)(2,1)S(1)}, bf16[2,512,1792]{2,1,0:T(8,128)(2,1)}, u32[]{:S(2)}) copy-start(bf16[2,512,1792]{2,1,0:T(8,128)(2,1)} %param.14) | copy-start | bytes 11010052
Sparse Core Ops, SparseCore 0:
  307.6 235.1 all-reduce.2
where the time goes:
time: 598 us; the launch traced here: 590 us
  matrix products  279 us (47%)
  waiting for transfers between devices  235 us (39%)
  other arithmetic  44.1 us (7%)
  local copies, waits for them, and re-layouts  16.9 us (3%)
  between operations  14.6 us (2%)
    psum x1, waiting for transfers between devices, step(): summed[number] = [lax.psum(by_w[name], 'dp') for name in NAMES]  235 us
    dot_general x5, matrix products, layer(): up = jnp.dot(a, w['w_up'], preferred_element_type=jnp.float32)  101 us
    dot_general x5, matrix products, layer(): gate = jnp.dot(a, w['w_gate'], preferred_element_type=jnp.float32)  100 us
    dot_general x5, matrix products, matmul(): jnp.dot(a, w, preferred_element_type=jnp.float32).astype(jnp.bfloat16)  77.1 us
    convert_element_type x2, other arithmetic, adamw(): return ((w - 0.02 * step).astype(jnp.bfloat16), m, v)  38.2 us
    unnamed x40, local copies, waits for them, and re-layouts  16.9 us
  transfers between devices with their start and end apart: 1, of which 1 were waited for; matrix products, arithmetic and copies ran while one was open for 0% of the time, Pallas kernels for 0%

commit v1 on v0

v1 whole, which is shorter than its diff:
```python
import functools

import jax
import jax.numpy as jnp
from jax import lax
from jax.experimental import pallas as pl
from jax.experimental.pallas import tpu as pltpu
from jax.sharding import PartitionSpec as P

TM = 512
FS = 256
F32, BF16 = jnp.float32, jnp.bfloat16
VMEM_LIMIT = 67_000_000


def dot(a, b):
    return jnp.dot(a, b, preferred_element_type=F32)


def dot_t(a, b):
    return lax.dot_general(a, b, (((1,), (1,)), ((), ())), preferred_element_type=F32)


def scale_of(wide):
    return lax.rsqrt(jnp.mean(wide * wide, -1, keepdims=True) + 1e-6)


def normed(h):
    wide = h.astype(F32)
    return (wide * scale_of(wide)).astype(BF16)


def sigmoid(g):
    return 0.5 * jnp.tanh(0.5 * g) + 0.5


def forward_tile(x, w_gu, w_d, act_ref):
    slices = w_gu.shape[0]
    a = normed(x)
    for j in range(slices):
        gu = dot(a, w_gu[j])
        g, u = gu[:, :FS], gu[:, FS:]
        act_ref[:, j * FS : (j + 1) * FS] = (g * sigmoid(g) * u).astype(BF16)
    y = dot(act_ref[...], w_d[...].reshape(slices * FS, -1)).astype(BF16)
    return a, (x.astype(F32) + y.astype(F32)).astype(BF16)


def slice_tile(a, a_t, dy, dy_t, wgu, wd, acc_ref):
    gu = dot(a, wgu)
    g, u = gu[:, :FS], gu[:, FS:]
    dact = dot_t(dy, wd).astype(BF16).astype(F32)
    s = sigmoid(g)
    silu = g * s
    act = (silu * u).astype(BF16)
    du = (dact * silu).astype(BF16)
    dg = (dact * u * (s + silu * (1.0 - s))).astype(BF16)
    acc_ref[:, 2 * FS :] += dot(dy_t, act)
    dgu = jnp.concatenate([dg, du], axis=1)
    acc_ref[:, : 2 * FS] += dot(a_t, dgu)
    return dgu


def norm_back(da, h, dy):
    d = h.shape[-1]
    da = da.astype(BF16).astype(F32)
    h = h.astype(F32)
    r = scale_of(h)
    along = jnp.sum(da * h, -1, keepdims=True)
    dh = (da * r - h * (along * r * r * r * (1.0 / d))).astype(BF16)
    return (dy.astype(F32) + dh.astype(F32)).astype(BF16)


class Ring:
    def __init__(self, n, rows, own, got, out, g_hbm, send, recv, out_sem):
        self.n, self.half, self.rows = n, n // 2, rows // n
        self.own, self.got, self.out, self.g_hbm = own, got, out, g_hbm
        self.send, self.recv, self.out_sem = send, recv, out_sem
        self.me = lax.axis_index("dp")
        self.to = ({"dp": lax.rem(self.me + n - 1, n)}, {"dp": lax.rem(self.me + 1, n)})

    def part(self, offset, way, halved):
        owner = lax.rem(self.me + offset + self.n, self.n)
        size = self.rows // 2 if halved else self.rows
        start = owner * self.rows + (size if halved and way == 1 else 0)
        return pl.ds(pl.multiple_of(start, size), size)

    def landing(self, way, halved):
        size = self.rows // 2 if halved else self.rows
        return pl.ds(size if halved and way == 1 else 0, size)

    def sign(self, way):
        return 1 if way == 0 else -1

    def copy(self, slot, k, way):
        h = self.half
        if k < h:
            halved = k == 0
            rows = self.part(self.sign(way) * (k - h), way, halved)
            src = self.own.at[slot, rows]
            dst = self.got.at[slot, k, way, self.landing(way, halved)]
        else:
            rows = self.part(self.sign(way) * (k - h), way, k == 2 * h - 1)
            src = dst = self.out.at[slot, rows]
        return pltpu.make_async_remote_copy(
            src_ref=src,
            dst_ref=dst,
            send_sem=self.send.at[slot, k, way],
            recv_sem=self.recv.at[slot, k, way],
            device_id=self.to[way],
            device_id_type=pl.DeviceIdType.MESH,
        )

    def write_out(self, slot, t):
        return pltpu.make_async_copy(self.out.at[slot], self.g_hbm.at[t], self.out_sem.at[slot])

    def event(self, slot, t, k):
        h = self.half
        if 0 < k <= 2 * h:
            for way in (0, 1):
                self.copy(slot, k - 1, way).wait_recv()
        if 0 < k < h:
            for way in (0, 1):
                rows = self.part(self.sign(way) * (k - h), way, k == 1)
                came = self.got[slot, k - 1, way, self.landing(way, k == 1)].astype(F32)
                self.own[slot, rows] = (self.own[slot, rows].astype(F32) + came).astype(BF16)
        if k == h:
            rows = self.part(0, 0, False)
            total = self.own[slot, rows].astype(F32) + self.got[slot, h - 1, 0].astype(F32) + self.got[slot, h - 1, 1].astype(F32)
            self.out[slot, rows] = total.astype(BF16)
        if k < 2 * h:
            for way in (0, 1):
                self.copy(slot, k, way).start()
        if k == 2 * h:
            self.write_out(slot, t).start()
            for sent in range(2 * h):
                for way in (0, 1):
                    self.copy(slot, sent, way).wait_send()
        if k == 2 * h + 1:
            self.write_out(slot, t).wait()


SLOTS = 4
EVERY = 3


def train_kernel(n, x, dy, wg, wu, wd, g_out, w_gu, w_d, a1, a2, at, dyv, dyt, h1, da, act, acc, own, got, out, sem, wsem, send, recv, out_sem):
    layers, slices = w_gu.shape[:2]
    tiles = x.shape[0]
    total = layers * slices
    barrier = pltpu.get_barrier_semaphore()
    ring = Ring(n, acc.shape[0], own, got, out, g_out, send, recv, out_sem)
    for device in ring.to:
        pl.semaphore_signal(barrier, inc=1, device_id=device, device_id_type=pl.DeviceIdType.MESH)

    def weights(l):
        return [
            copy
            for j in range(slices)
            for copy in (
                pltpu.make_async_copy(wg.at[l, :, pl.ds(j * FS, FS)], w_gu.at[l, j, :, pl.ds(0, FS)], wsem.at[l, j, 0]),
                pltpu.make_async_copy(wu.at[l, :, pl.ds(j * FS, FS)], w_gu.at[l, j, :, pl.ds(FS, FS)], wsem.at[l, j, 1]),
                pltpu.make_async_copy(wd.at[l, pl.ds(j * FS, FS), :], w_d.at[l, j], wsem.at[l, j, 2]),
            )
        ]

    def state(m):
        return pltpu.make_async_copy(x.at[m], a1.at[m], sem.at[m])

    all_dy = pltpu.make_async_copy(dy, dyv, sem.at[tiles])
    state(0).start()
    for c in weights(0):
        c.start()
    for m in range(1, tiles):
        state(m).start()
    all_dy.start()
    for c in weights(1):
        c.start()
    for c in weights(0):
        c.wait()

    def forward(m, _):
        state(m).wait()
        a, h = forward_tile(a1[m], w_gu.at[0], w_d.at[0], act)
        a1[m] = a
        h1[m] = h
        a = normed(h)
        a2[m] = a
        at[m] = a.T
        da[m] = jnp.zeros(da.shape[1:], F32)

        @pl.when(m == 0)
        def _():
            all_dy.wait()

        dyt[m] = dyv[m].T
        return 0

    lax.fori_loop(0, tiles, forward, 0)
    for c in weights(1):
        c.wait()
    pl.semaphore_wait(barrier, 2)

    offsets = [EVERY * k for k in range(2 * ring.half + 2)]

    def events(s, m):
        for k in reversed(range(len(offsets))):
            ago, at_tile = divmod(offsets[k], tiles)
            t = s - 1 - ago

            @pl.when((m == at_tile) & (t >= 0) & (t < total))
            def _():
                ring.event(lax.rem(t, SLOTS), t, k)

    def one_slice(s, _):
        second = s < slices
        l = jnp.where(second, 1, 0)
        j = jnp.where(second, s, s - slices)
        acc[...] = jnp.zeros_like(acc)

        def one_tile(m, _):
            events(s, m)

            @pl.when(s == slices)
            def _():
                back = norm_back(da[m], h1[m], dyv[m])
                dyv[m] = back
                dyt[m] = back.T
                a = a1[m]
                a2[m] = a
                at[m] = a.T

            dgu = slice_tile(a2[m], at[m], dyv[m], dyt[m], w_gu[l, j], w_d[l, j], acc)

            @pl.when(second)
            def _():
                da[m] += dot_t(dgu, w_gu[l, j])

            return 0

        lax.fori_loop(0, tiles, one_tile, 0)
        own[lax.rem(s, SLOTS)] = acc[...].astype(BF16)
        return 0

    lax.fori_loop(0, total, one_slice, 0)

    def drain(s, _):
        def one(m, _):
            events(s, m)
            return 0

        return lax.fori_loop(0, tiles, one, 0)

    lax.fori_loop(total, total + 1 + offsets[-1] // tiles, drain, 0)


def adam_math(w, m, v, g):
    m = 0.9 * m + 0.1 * g
    v = 0.95 * v + 0.05 * g * g
    step = m * lax.rsqrt(v + 1e-8) + 0.1 * w
    return (w - 0.02 * step).astype(BF16), m, v


def adam_kernel(g_ref, *refs):
    ins, outs = refs[:9], refs[9:]
    for i in range(3):
        g = g_ref[0, :, i * FS : (i + 1) * FS].astype(F32)
        if i == 2:
            g = g.T
        w, m, v = (ins[k * 3 + i] for k in range(3))
        new = adam_math(w[0].astype(F32), m[0], v[0], g)
        for k in range(3):
            outs[k * 3 + i][0] = new[k]


def adam(g, arrays):
    layers, d, ff = arrays[0].shape
    slices = ff // FS
    wide = pl.BlockSpec((1, d, FS), lambda s: (layers - 1 - s // slices, 0, s % slices))
    tall = pl.BlockSpec((1, FS, d), lambda s: (layers - 1 - s // slices, s % slices, 0))
    specs = [wide, wide, tall] * 3
    return pl.pallas_call(
        adam_kernel,
        grid=(layers * slices,),
        in_specs=[pl.BlockSpec((1, d, 3 * FS), lambda s: (s, 0, 0))] + specs,
        out_specs=specs,
        out_shape=[jax.ShapeDtypeStruct(a.shape, a.dtype) for a in arrays],
        compiler_params=pltpu.CompilerParams(vmem_limit_bytes=60_000_000),
        cost_estimate=pl.CostEstimate(flops=10**9, bytes_accessed=120 * 10**6, transcendentals=0),
    )(g, *arrays)


def solution(mesh):
    n = mesh.shape["dp"]

    def step(x, dy, *arrays):
        wg, wu, wd = arrays[:3]
        tokens, d = x.shape[1:]
        layers, _, ff = wg.shape
        tiles, slices = tokens // TM, ff // FS
        x, dy = x.reshape(tiles, TM, d), dy.reshape(tiles, TM, d)
        hbm = pl.BlockSpec(memory_space=pl.ANY)
        half = n // 2
        mm = 2 * tokens * d * ff
        g = pl.pallas_call(
            functools.partial(train_kernel, n),
            in_specs=[hbm] * 5,
            out_specs=hbm,
            out_shape=jax.ShapeDtypeStruct((layers * slices, d, 3 * FS), BF16),
            scratch_shapes=[
                pltpu.VMEM((layers, slices, d, 2 * FS), BF16),
                pltpu.VMEM((layers, slices, FS, d), BF16),
                pltpu.VMEM((tiles, TM, d), BF16),
                pltpu.VMEM((tiles, TM, d), BF16),
                pltpu.VMEM((tiles, d, TM), BF16),
                pltpu.VMEM((tiles, TM, d), BF16),
                pltpu.VMEM((tiles, d, TM), BF16),
                pltpu.VMEM((tiles, TM, d), BF16),
                pltpu.VMEM((tiles, TM, d), F32),
                pltpu.VMEM((TM, ff), BF16),
                pltpu.VMEM((d, 3 * FS), F32),
                pltpu.VMEM((SLOTS, d, 3 * FS), BF16),
                pltpu.VMEM((SLOTS, half, 2, d // n, 3 * FS), BF16),
                pltpu.VMEM((SLOTS, d, 3 * FS), BF16),
                pltpu.SemaphoreType.DMA((tiles + 1,)),
                pltpu.SemaphoreType.DMA((layers, slices, 3)),
                pltpu.SemaphoreType.DMA((SLOTS, 2 * half, 2)),
                pltpu.SemaphoreType.DMA((SLOTS, 2 * half, 2)),
                pltpu.SemaphoreType.DMA((SLOTS,)),
            ],
            compiler_params=pltpu.CompilerParams(vmem_limit_bytes=VMEM_LIMIT, collective_id=0, has_side_effects=True),
            cost_estimate=pl.CostEstimate(flops=17 * mm, bytes_accessed=30 * 10**6, transcendentals=0),
        )(x, dy, wg, wu, wd)
        return tuple(adam(g, arrays))

    return jax.shard_map(
        step,
        mesh=mesh,
        in_specs=(P(("rep", "dp"), None, None),) * 2 + (P(None, None, None),) * 9,
        out_specs=(P("rep", None, None),) * 9,
        check_vma=False,
    )
```

time: 598 us -> 327 us (0.55)
  Pallas kernels: 0 us -> 320 us
  matrix products: 279 us -> 0 us
  waiting for transfers between devices: 235 us -> 0 us
  other arithmetic: 44.1 us -> 0 us
  local copies, waits for them, and re-layouts: 16.9 us -> 0 us
  between operations: 14.6 us -> 0.65 us
    pallas_call x0 -> x2, Pallas kernels: none -> 320 us  [the longest x1 278 us: step(): pl.pallas_call(functools.partial(train_kernel, n), in_specs=[hbm] * 5, ou...]
    dot_general x15 -> x0, matrix products: 279 us -> none  [the longest x5 101 us: layer(): up = jnp.dot(a, w['w_up'], preferred_element_type=jnp.float32)]
    psum x1 -> x0, waiting for transfers between devices: 235 us -> none  [step(): summed[number] = [lax.psum(by_w[name], 'dp') for name in NAMES]]
    convert_element_type x2 -> x0, other arithmetic: 38.2 us -> none  [adamw(): return ((w - 0.02 * step).astype(jnp.bfloat16), m, v)]
    unnamed x40 -> x0, local copies, waits for them, and re-layouts: 16.9 us -> none
  transfers between devices with their start and end apart: 1 -> 0, of which waited for: 1 -> 0; matrix products, arithmetic and copies ran while one was open for 0% -> 0% of each run, Pallas kernels for 0% -> 0%
where the time goes in v1:
time: 327 us; the launch traced here: 320 us
  Pallas kernels  320 us (98%)
    pallas_call x1, Pallas kernels, step(): pl.pallas_call(functools.partial(train_kernel, n), in_specs=[hbm] * 5, ou...  278 us
    pallas_call x1, Pallas kernels, adam(): pl.pallas_call(adam_kernel, grid=(layers * slices,), in_specs=[pl.BlockSp...  41.9 us

profile of v1, /device:TPU:21, one launch (start us, length us, event | category | flops | bytes accessed | tf_op | source)
XLA Modules:
  0.0 320.3 jit_solution(9923046591377489236)
XLA Ops:
  0.6 277.7 %shard_map.178.g_ref = bf16[14,512,768]{2,1,0:T(8,128)(2,1)} custom-call(bf16[8,512,512]{2,1,0:T(8,128)(2,1)} %bitcast.2, bf16[8,512,512]{2,1,0:T(8,128)(2,1)} %bitcast.3, bf16[2,512,1792]{2,1,0:T(8,128)(2,1)} %refs_0_.1, bf16[2,512,1792]{2,1,0:T(8,128)(2,1)} %refs_1_.1, bf16[2,1792,512]{2,1,0:T(8,128)(2,1)} %refs_2_.1), custom_call_target="tpu_custom_call" | custom-call | flops 127775277056 | bytes 30000000 | tf_op jit(solution)/shard_map/pallas_call | solution.py:304
  278.3 41.9 %shard_map.179 = (bf16[2,512,1792]{2,1,0:T(8,128)(2,1)}, bf16[2,512,1792]{2,1,0:T(8,128)(2,1)}, bf16[2,1792,512]{2,1,0:T(8,128)(2,1)}, f32[2,512,1792]{2,1,0:T(8...) custom-call(bf16[14,512,768]{2,1,0:T(8,128)(2,1)} %shard_map.178.g_r, ...), custom_call_target="tpu_custom_call" | custom-call | flops 1000000000 | bytes 120000000 | tf_op jit(solution)/shard_map/pallas_call | solution.py:281

commit v2 on v1

--- a/solution.py
+++ b/solution.py
@@ -6,6 +6,7 @@
 from jax.experimental import pallas as pl
 from jax.experimental.pallas import tpu as pltpu
 from jax.sharding import PartitionSpec as P
+
 
 TM = 512
 FS = 256
@@ -71,36 +72,31 @@
 
 
 class Ring:
-    def __init__(self, n, rows, own, got, out, g_hbm, send, recv, out_sem):
-        self.n, self.half, self.rows = n, n // 2, rows // n
-        self.own, self.got, self.out, self.g_hbm = own, got, out, g_hbm
+    def __init__(self, n, own, got, out, sums, far, send, recv, out_sem):
+        self.n, self.half, self.rows = n, n // 2, own.shape[2]
+        self.kept = self.half - 2
+        self.sends = self.half + self.kept
+        self.own, self.got, self.out, self.sums, self.far = own, got, out, sums, far
         self.send, self.recv, self.out_sem = send, recv, out_sem
         self.me = lax.axis_index("dp")
         self.to = ({"dp": lax.rem(self.me + n - 1, n)}, {"dp": lax.rem(self.me + 1, n)})
 
-    def part(self, offset, way, halved):
-        owner = lax.rem(self.me + offset + self.n, self.n)
-        size = self.rows // 2 if halved else self.rows
-        start = owner * self.rows + (size if halved and way == 1 else 0)
-        return pl.ds(pl.multiple_of(start, size), size)
-
-    def landing(self, way, halved):
+    def chunk(self, way, offset):
+        return lax.rem(self.me + (offset if way == 0 else -offset) + self.n, self.n)
+
+    def part(self, way, halved):
         size = self.rows // 2 if halved else self.rows
         return pl.ds(size if halved and way == 1 else 0, size)
 
-    def sign(self, way):
-        return 1 if way == 0 else -1
-
     def copy(self, slot, k, way):
         h = self.half
+        rows = self.part(way, k == 0)
+        chunk = self.chunk(way, k - h)
         if k < h:
-            halved = k == 0
-            rows = self.part(self.sign(way) * (k - h), way, halved)
-            src = self.own.at[slot, rows]
-            dst = self.got.at[slot, k, way, self.landing(way, halved)]
+            src = self.own.at[slot, chunk, rows]
+            dst = self.got.at[slot, k, way, rows]
         else:
-            rows = self.part(self.sign(way) * (k - h), way, k == 2 * h - 1)
-            src = dst = self.out.at[slot, rows]
+            src = dst = self.out.at[slot, chunk, rows]
         return pltpu.make_async_remote_copy(
             src_ref=src,
             dst_ref=dst,
@@ -111,44 +107,53 @@
         )
 
     def write_out(self, slot, t):
-        return pltpu.make_async_copy(self.out.at[slot], self.g_hbm.at[t], self.out_sem.at[slot])
+        copies = []
+        for offset in range(-self.kept, self.kept + 1):
+            chunk = self.chunk(0, offset)
+            copies.append((self.out.at[slot, chunk], self.sums.at[t, chunk]))
+        for way in (0, 1):
+            chunk = self.chunk(way, self.kept)
+            for part in (0, 1):
+                copies.append((self.out.at[slot, chunk, self.part(part, True)], self.far[2 * way + part].at[t]))
+        return [pltpu.make_async_copy(a, b, self.out_sem.at[slot, i]) for i, (a, b) in enumerate(copies)]
 
     def event(self, slot, t, k):
         h = self.half
-        if 0 < k <= 2 * h:
+        if 0 < k <= self.sends:
             for way in (0, 1):
                 self.copy(slot, k - 1, way).wait_recv()
         if 0 < k < h:
             for way in (0, 1):
-                rows = self.part(self.sign(way) * (k - h), way, k == 1)
-                came = self.got[slot, k - 1, way, self.landing(way, k == 1)].astype(F32)
-                self.own[slot, rows] = (self.own[slot, rows].astype(F32) + came).astype(BF16)
+                rows, chunk = self.part(way, k == 1), self.chunk(way, k - h)
+                came = self.got[slot, k - 1, way, rows].astype(F32)
+                self.own[slot, chunk, rows] = (self.own[slot, chunk, rows].astype(F32) + came).astype(BF16)
         if k == h:
-            rows = self.part(0, 0, False)
-            total = self.own[slot, rows].astype(F32) + self.got[slot, h - 1, 0].astype(F32) + self.got[slot, h - 1, 1].astype(F32)
-            self.out[slot, rows] = total.astype(BF16)
-        if k < 2 * h:
+            total = self.own[slot, self.me].astype(F32) + self.got[slot, h - 1, 0].astype(F32) + self.got[slot, h - 1, 1].astype(F32)
+            self.out[slot, self.me] = total.astype(BF16)
+        if k < self.sends:
             for way in (0, 1):
                 self.copy(slot, k, way).start()
-        if k == 2 * h:
-            self.write_out(slot, t).start()
-            for sent in range(2 * h):
+        if k == self.sends:
+            for copy in self.write_out(slot, t):
+                copy.start()
+            for sent in range(self.sends):
                 for way in (0, 1):
                     self.copy(slot, sent, way).wait_send()
-        if k == 2 * h + 1:
-            self.write_out(slot, t).wait()
+        if k == self.sends + 1:
+            for copy in self.write_out(slot, t):
+                copy.wait()
 
 
 SLOTS = 4
-EVERY = 3
-
-
-def train_kernel(n, x, dy, wg, wu, wd, g_out, w_gu, w_d, a1, a2, at, dyv, dyt, h1, da, act, acc, own, got, out, sem, wsem, send, recv, out_sem):
+EVERY = 5
+
+
+def train_kernel(n, x, dy, wg, wu, wd, sums, far0, far1, far2, far3, w_gu, w_d, a1, a2, at, dyv, dyt, h1, da, act, acc, own, got, out, sem, wsem, send, recv, out_sem):
     layers, slices = w_gu.shape[:2]
     tiles = x.shape[0]
     total = layers * slices
     barrier = pltpu.get_barrier_semaphore()
-    ring = Ring(n, acc.shape[0], own, got, out, g_out, send, recv, out_sem)
+    ring = Ring(n, own, got, out, sums, (far0, far1, far2, far3), send, recv, out_sem)
     for device in ring.to:
         pl.semaphore_signal(barrier, inc=1, device_id=device, device_id_type=pl.DeviceIdType.MESH)
 
@@ -200,7 +205,7 @@
         c.wait()
     pl.semaphore_wait(barrier, 2)
 
-    offsets = [EVERY * k for k in range(2 * ring.half + 2)]
+    offsets = [EVERY * k for k in range(ring.sends + 1)] + [EVERY * ring.sends + 3]
 
     def events(s, m):
         for k in reversed(range(len(offsets))):
@@ -238,7 +243,10 @@
             return 0
 
         lax.fori_loop(0, tiles, one_tile, 0)
-        own[lax.rem(s, SLOTS)] = acc[...].astype(BF16)
+        slot = lax.rem(s, SLOTS)
+        wide = acc.shape[0] // n
+        own[slot, :, :wide] = acc[:, : 2 * FS].astype(BF16).reshape(n, wide, 2 * FS)
+        own[slot, :, wide:] = acc[:, 2 * FS :].T.astype(BF16).reshape(n, FS // n, -1)
         return 0
 
     lax.fori_loop(0, total, one_slice, 0)
@@ -260,33 +268,49 @@
     return (w - 0.02 * step).astype(BF16), m, v
 
 
-def adam_kernel(g_ref, *refs):
-    ins, outs = refs[:9], refs[9:]
-    for i in range(3):
-        g = g_ref[0, :, i * FS : (i + 1) * FS].astype(F32)
-        if i == 2:
-            g = g.T
-        w, m, v = (ins[k * 3 + i] for k in range(3))
-        new = adam_math(w[0].astype(F32), m[0], v[0], g)
-        for k in range(3):
-            outs[k * 3 + i][0] = new[k]
-
-
-def adam(g, arrays):
-    layers, d, ff = arrays[0].shape
-    slices = ff // FS
-    wide = pl.BlockSpec((1, d, FS), lambda s: (layers - 1 - s // slices, 0, s % slices))
-    tall = pl.BlockSpec((1, FS, d), lambda s: (layers - 1 - s // slices, s % slices, 0))
+def adam_kernel(halves, where, *refs):
+    gs, ins, outs = refs[:halves], refs[halves : halves + 9], refs[-9:]
+    slices = gs[0].shape[0]
+    wide = ins[0].shape[2]
+    for j in range(slices):
+        g = [r[j].reshape(r.shape[-2:]) for r in gs]
+        g = (g[0] if halves == 1 else jnp.concatenate(g, axis=0)).astype(F32)
+        columns = slice(j * FS, (j + 1) * FS)
+        for i, here in ((0, (0, 0, slice(None), columns)), (1, (0, 0, slice(None), columns)), (2, (0, j, 0))):
+            part = (g[:wide, :FS], g[:wide, FS:], g[wide:])[i]
+            w, m, v = (ins[k * 3 + i][here] for k in range(3))
+            new = adam_math(w.astype(F32), m, v, part)
+            for k in range(3):
+                outs[k * 3 + i][here] = new[k]
+
+
+def adam(n, offsets, gs, g_spec, arrays, so_far):
+    layers = arrays[0].shape[0]
+    slices = arrays[2].shape[1]
+    extra = [] if so_far is None else list(so_far)
+    where = lax.axis_index("dp").astype(jnp.int32).reshape(1)
+    step = offsets[1] - offsets[0] if len(offsets) > 1 else 1
+
+    def chunk(o, where):
+        return lax.rem(where[0] + o * step + (offsets[0] + n), n)
+
+    wide = pl.BlockSpec((1, 1) + arrays[0].shape[2:], lambda l, o, where: (l, chunk(o, where), 0, 0))
+    tall = pl.BlockSpec((1, slices, 1) + arrays[2].shape[3:], lambda l, o, where: (l, 0, chunk(o, where), 0, 0))
     specs = [wide, wide, tall] * 3
+    size = sum(a.size * a.dtype.itemsize for a in arrays) * 2 * len(offsets) // n
     return pl.pallas_call(
-        adam_kernel,
-        grid=(layers * slices,),
-        in_specs=[pl.BlockSpec((1, d, 3 * FS), lambda s: (s, 0, 0))] + specs,
-        out_specs=specs,
+        functools.partial(adam_kernel, len(gs)),
+        grid_spec=pltpu.PrefetchScalarGridSpec(
+            num_scalar_prefetch=1,
+            grid=(layers, len(offsets)),
+            in_specs=[g_spec(chunk)] * len(gs) + specs + [pl.BlockSpec(memory_space=pl.ANY)] * len(extra),
+            out_specs=specs,
+        ),
         out_shape=[jax.ShapeDtypeStruct(a.shape, a.dtype) for a in arrays],
+        input_output_aliases={1 + len(gs) + 9 + i: i for i in range(len(extra))},
         compiler_params=pltpu.CompilerParams(vmem_limit_bytes=60_000_000),
-        cost_estimate=pl.CostEstimate(flops=10**9, bytes_accessed=120 * 10**6, transcendentals=0),
-    )(g, *arrays)
+        cost_estimate=pl.CostEstimate(flops=40 * size, bytes_accessed=size, transcendentals=0),
+    )(where, *gs, *arrays, *extra)
 
 
 def solution(mesh):
@@ -299,13 +323,14 @@
         tiles, slices = tokens // TM, ff // FS
         x, dy = x.reshape(tiles, TM, d), dy.reshape(tiles, TM, d)
         hbm = pl.BlockSpec(memory_space=pl.ANY)
-        half = n // 2
+        half, rows = n // 2, (d + FS) // n
         mm = 2 * tokens * d * ff
-        g = pl.pallas_call(
+        sums, *far = pl.pallas_call(
             functools.partial(train_kernel, n),
             in_specs=[hbm] * 5,
-            out_specs=hbm,
-            out_shape=jax.ShapeDtypeStruct((layers * slices, d, 3 * FS), BF16),
+            out_specs=[hbm] * 5,
+            out_shape=[jax.ShapeDtypeStruct((layers * slices, n, rows, d), BF16)]
+            + [jax.ShapeDtypeStruct((layers * slices, rows // 2, d), BF16)] * 4,
             scratch_shapes=[
                 pltpu.VMEM((layers, slices, d, 2 * FS), BF16),
                 pltpu.VMEM((layers, slices, FS, d), BF16),
@@ -318,19 +343,39 @@
                 pltpu.VMEM((tiles, TM, d), F32),
                 pltpu.VMEM((TM, ff), BF16),
                 pltpu.VMEM((d, 3 * FS), F32),
-                pltpu.VMEM((SLOTS, d, 3 * FS), BF16),
-                pltpu.VMEM((SLOTS, half, 2, d // n, 3 * FS), BF16),
-                pltpu.VMEM((SLOTS, d, 3 * FS), BF16),
+                pltpu.VMEM((SLOTS, n, rows, d), BF16),
+                pltpu.VMEM((SLOTS, half, 2, rows, d), BF16),
+                pltpu.VMEM((SLOTS, n, rows, d), BF16),
                 pltpu.SemaphoreType.DMA((tiles + 1,)),
                 pltpu.SemaphoreType.DMA((layers, slices, 3)),
-                pltpu.SemaphoreType.DMA((SLOTS, 2 * half, 2)),
-                pltpu.SemaphoreType.DMA((SLOTS, 2 * half, 2)),
-                pltpu.SemaphoreType.DMA((SLOTS,)),
+                pltpu.SemaphoreType.DMA((SLOTS, 2 * half - 2, 2)),
+                pltpu.SemaphoreType.DMA((SLOTS, 2 * half - 2, 2)),
+                pltpu.SemaphoreType.DMA((SLOTS, n + 1)),
             ],
             compiler_params=pltpu.CompilerParams(vmem_limit_bytes=VMEM_LIMIT, collective_id=0, has_side_effects=True),
             cost_estimate=pl.CostEstimate(flops=17 * mm, bytes_accessed=30 * 10**6, transcendentals=0),
         )(x, dy, wg, wu, wd)
-        return tuple(adam(g, arrays))
+        chunks = [a.reshape(layers, n, d // n, ff) if a.shape[1] == d else a.reshape(layers, slices, n, FS // n, d) for a in arrays]
+        left = [(i, (i + n - 1) % n) for i in range(n)]
+        right = [(i, (i + 1) % n) for i in range(n)]
+
+        def whole(chunk):
+            return pl.BlockSpec((slices, 1, rows, d), lambda l, o, where: (layers - 1 - l, chunk(o, where), 0, 0))
+
+        def halves(chunk):
+            return pl.BlockSpec((slices, rows // 2, d), lambda l, o, where: (layers - 1 - l, 0, 0))
+
+        near = []
+        for i, way in enumerate((left, left, right, right)):
+            near.append(lax.ppermute(far[i], "dp", way))
+        new = adam(n, tuple(range(2 - half, half - 1)), [sums], whole, chunks, None)
+        last = []
+        for i, way in ((0, left), (3, right)):
+            last.append(lax.ppermute(near[i], "dp", way))
+        new = adam(n, (half - 1,), near[:2], halves, chunks, new)
+        new = adam(n, (1 - half,), near[2:], halves, chunks, new)
+        new = adam(n, (half,), last, halves, chunks, new)
+        return tuple(o.reshape(a.shape) for o, a in zip(new, arrays))
 
     return jax.shard_map(
         step,

time: 327 us -> 323 us (0.988)
  the two profiles are of different devices: /device:TPU:21 before, /device:TPU:30 now
where the time goes in v2:
time: 323 us
  Pallas kernels  298 us (92%)
  waiting for transfers between devices  13.1 us (4%)
  starting transfers between devices  8.94 us (3%)
    pallas_call x1, Pallas kernels, step(): pl.pallas_call(functools.partial(train_kernel, n), in_specs=[hbm] * 5, ou...  253 us
    pallas_call x4, Pallas kernels, adam(): pl.pallas_call(functools.partial(adam_kernel, len(gs)), grid_spec=pltpu.P...  45 us
    ppermute x4, waiting for transfers between devices, step(): near.append(lax.ppermute(far[i], 'dp', way))  13.1 us
  transfers between devices with their start and end apart: 6, of which 1 were waited for; matrix products, arithmetic and copies ran while one was open for 0% of the time, Pallas kernels for 12%

profile of v2, /device:TPU:30, one launch (start us, length us, event | category | flops | bytes accessed | tf_op | source)
XLA Modules:
  0.0 322.7 jit_solution(1565209870765376264)
XLA Ops:
  0.6 252.9 %shard_map.178 = (bf16[14,8,96,512]{3,2,1,0:T(8,128)(2,1)}, bf16[14,48,512]{2,1,0:T(8,128)(2,1)}, bf16[14,48,512]{2,1,0:T(8,128)(2,1)}, bf16[14,48,512]{2,1,0:T(8,128)(2,1)}, bf16[14,48,512]{2,1,0:T(8,128)(2,1)}) custom-call(bf16[8,512,512]{2,1,0:T(8,128)(2,1)} %bitcast.66, bf16[8,512,512]{2,1,0:T(8,128)(2,1)} %bitcast.67, bf16[2,512,1792]{2,1,0:T(8,128)(2,1)} %wg.1, ...), custom_call_target="tpu_custom_call" | custom-call | flops 127775277056 | bytes 30000000 | tf_op jit(solution)/shard_map/pallas_call | solution.py:328
  253.5 2.3 collective-permute-start
  255.8 0.0 collective-permute-start.2
  255.8 3.2 %collective-permute-start.5 = (bf16[14,48,512]{2,1,0:T(8,128)(2,1)}, bf16[14,48,512]{2,1,0:T(8,128)(2,1)}, u32[]{:S(2)}, u32[]{:S(2)}) collective-permute-start(bf16[14,48,512]{2,1,0:T(8,128)(2,1)} %get-tuple-element.53), channel_id=1, source_target_pairs={{0,7},{1,0},{2,1},{3,2},{4,3},{5,4},{6,5},{7,6},{8,15},{9,8},{10,9... | collective-permute-start | bytes 2064392 | tf_op jit(solution)/shard_map/ppermute | solution.py:370
  259.1 0.0 collective-permute-start.4
  259.1 13.1 %collective-permute-done.refs_0_ = bf16[14,48,512]{2,1,0:T(8,128)(2,1)S(1)} collective-permute-done((bf16[14,48,512]{2,1,0:T(8,128)(2,1)}, bf16[14,48,512]{2,1,0:T(8,128)(2,1)S(1)}, u32[]{:S(2)}, u32[]{:S(2)}) %collective-permute-start) | collective-permute-done | bytes 688160 | tf_op jit(solution)/shard_map/ppermute | solution.py:370
  272.1 0.0 copy-start
  272.1 3.4 %collective-permute-start.1 = (bf16[14,48,512]{2,1,0:T(8,128)(2,1)S(1)}, bf16[14,48,512]{2,1,0:T(8,128)(2,1)S(1)}, u32[]{:S(2)}, u32[]{:S(2)}) collective-permute-start(bf16[14,48,512]{2,1,0:T(8,128)(2,1)S(1)} %collective-permute-done.refs_0_), channel_id=1, source_target_pairs={{0,7},{1,0},{2,1},{3,2},{4,3},{5,4},{6,5},{7,6},{8,15},{9,8},{10,9... | collective-permute-start | bytes 2064392 | tf_op jit(solution)/shard_map/ppermute | solution.py:374
  275.6 0.0 collective-permute-done.2.refs_1_
  275.6 0.0 copy-start.1
  275.6 0.0 collective-permute-start.3
  275.6 27.0 %shard_map.179 = (bf16[2,8,64,1792]{3,2,1,0:T(8,128)(2,1)}, bf16[2,8,64,1792]{3,2,1,0:T(8,128)(2,1)}, bf16[2,7,8,32,512]{4,3,2,1,0:T(8,128)(2,1)}, f32[2,8,64,17...) custom-call(s32[1]{0:T(128)} %bitcast.where, ...), custom_call_target="tpu_custom_call" | custom-call | flops 2752512000 | bytes 68812800 | tf_op jit(solution)/shard_map/pallas_call | solution.py:301
  302.6 0.0 copy-done
  302.6 0.0 copy-done.1
  302.6 0.0 collective-permute-done.5.refs_1_
  302.6 6.0 %shard_map.180 = (bf16[2,8,64,1792]{3,2,1,0:T(8,128)(2,1)}, bf16[2,8,64,1792]{3,2,1,0:T(8,128)(2,1)}, bf16[2,7,8,32,512]{4,3,2,1,0:T(8,128)(2,1)}, f32[2,8,64,17...) custom-call(s32[1]{0:T(128)} %bitcast.where, ...), custom_call_target="tpu_custom_call", output_to_operand_aliasing={{0}: (12, {}), {1}: (13, {}), {2}: (14, {}), {3}: (15, {}),... | custom-call | flops 550502400 | bytes 13762560 | tf_op jit(solution)/shard_map/pallas_call | solution.py:301
  308.6 0.0 collective-permute-done.4.refs_0_
  308.7 0.0 copy-start.4
  308.7 0.8 copy-done.4
  309.5 6.0 %shard_map.181 = (bf16[2,8,64,1792]{3,2,1,0:T(8,128)(2,1)}, bf16[2,8,64,1792]{3,2,1,0:T(8,128)(2,1)}, bf16[2,7,8,32,512]{4,3,2,1,0:T(8,128)(2,1)}, f32[2,8,64,17...) custom-call(s32[1]{0:T(128)} %bitcast.where, ...), custom_call_target="tpu_custom_call", output_to_operand_aliasing={{0}: (12, {}), {1}: (13, {}), {2}: (14, {}), {3}: (15, {}),... | custom-call | flops 550502400 | bytes 13762560 | tf_op jit(solution)/shard_map/pallas_call | solution.py:301
  315.5 0.0 collective-permute-done.1.refs_0_
  315.5 0.0 copy-start.2
  315.5 0.0 collective-permute-done.3.refs_1_
  315.5 0.0 copy-start.3
  315.5 0.8 copy-done.2
  316.3 0.3 copy-done.3
  316.6 6.0 %shard_map.182 = (bf16[2,8,64,1792]{3,2,1,0:T(8,128)(2,1)}, bf16[2,8,64,1792]{3,2,1,0:T(8,128)(2,1)}, bf16[2,7,8,32,512]{4,3,2,1,0:T(8,128)(2,1)}, f32[2,8,64,17...) custom-call(s32[1]{0:T(128)} %bitcast.where, ...), custom_call_target="tpu_custom_call", output_to_operand_aliasing={{0}: (12, {}), {1}: (13, {}), {2}: (14, {}), {3}: (15, {}),... | custom-call | flops 550502400 | bytes 13762560 | tf_op jit(solution)/shard_map/pallas_call | solution.py:301
Async XLA Ops:
  253.5 18.6 %collective-permute-start = (bf16[14,48,512]{2,1,0:T(8,128)(2,1)}, bf16[14,48,512]{2,1,0:T(8,128)(2,1)S(1)}, u32[]{:S(2)}, u32[]{:S(2)}) collective-permute-start(bf16[14,48,512]{2,1,0:T(8,128)(2,1)} %get-tuple-element.50), channel_id=1, source_target_pairs={{0,7},{1,0},{2,1},{3,2},{4,3},{5,4},{6,5},{7,6},{8,15},{9,8},{10,9... | collective-permute-start | bytes 2064392 | tf_op jit(solution)/shard_map/ppermute | solution.py:370
  255.8 19.7 %collective-permute-start.2 = (bf16[14,48,512]{2,1,0:T(8,128)(2,1)}, bf16[14,48,512]{2,1,0:T(8,128)(2,1)S(1)}, u32[]{:S(2)}, u32[]{:S(2)}) collective-permute-start(bf16[14,48,512]{2,1,0:T(8,128)(2,1)} %get-tuple-element.51), channel_id=1, source_target_pairs={{0,1},{1,2},{2,3},{3,4},{4,5},{5,6},{6,7},{7,0},{8,9},{9,10},{10,1... | collective-permute-start | bytes 2064392 | tf_op jit(solution)/shard_map/ppermute | solution.py:370
  255.8 46.8 %collective-permute-start.5 = (bf16[14,48,512]{2,1,0:T(8,128)(2,1)}, bf16[14,48,512]{2,1,0:T(8,128)(2,1)}, u32[]{:S(2)}, u32[]{:S(2)}) collective-permute-start(bf16[14,48,512]{2,1,0:T(8,128)(2,1)} %get-tuple-element.53), channel_id=1, source_target_pairs={{0,7},{1,0},{2,1},{3,2},{4,3},{5,4},{6,5},{7,6},{8,15},{9,8},{10,9... | collective-permute-start | bytes 2064392 | tf_op jit(solution)/shard_map/ppermute | solution.py:370
  259.1 49.6 %collective-permute-start.4 = (bf16[14,48,512]{2,1,0:T(8,128)(2,1)}, bf16[14,48,512]{2,1,0:T(8,128)(2,1)S(1)}, u32[]{:S(2)}, u32[]{:S(2)}) collective-permute-start(bf16[14,48,512]{2,1,0:T(8,128)(2,1)} %get-tuple-element.52), channel_id=1, source_target_pairs={{0,1},{1,2},{2,3},{3,4},{4,5},{5,6},{6,7},{7,0},{8,9},{9,10},{10,1... | collective-permute-start | bytes 2064392 | tf_op jit(solution)/shard_map/ppermute | solution.py:370
  272.1 30.4 %copy-start = (bf16[14,48,512]{2,1,0:T(8,128)(2,1)}, bf16[14,48,512]{2,1,0:T(8,128)(2,1)S(1)}, u32[]{:S(2)}) copy-start(bf16[14,48,512]{2,1,0:T(8,128)(2,1)S(1)} %collective-permute-done.refs_0_) | copy-start | bytes 2064388
  272.1 43.3 %collective-permute-start.1 = (bf16[14,48,512]{2,1,0:T(8,128)(2,1)S(1)}, bf16[14,48,512]{2,1,0:T(8,128)(2,1)S(1)}, u32[]{:S(2)}, u32[]{:S(2)}) collective-permute-start(bf16[14,48,512]{2,1,0:T(8,128)(2,1)S(1)} %collective-permute-done.refs_0_), channel_id=1, source_target_pairs={{0,7},{1,0},{2,1},{3,2},{4,3},{5,4},{6,5},{7,6},{8,15},{9,8},{10,9... | collective-permute-start | bytes 2064392 | tf_op jit(solution)/shard_map/ppermute | solution.py:374
  275.6 27.0 %copy-start.1 = (bf16[14,48,512]{2,1,0:T(8,128)(2,1)}, bf16[14,48,512]{2,1,0:T(8,128)(2,1)S(1)}, u32[]{:S(2)}) copy-start(bf16[14,48,512]{2,1,0:T(8,128)(2,1)S(1)} %collective-permute-done.2.refs_1_) | copy-start | bytes 2064388
  275.6 39.9 %collective-permute-start.3 = (bf16[14,48,512]{2,1,0:T(8,128)(2,1)S(1)}, bf16[14,48,512]{2,1,0:T(8,128)(2,1)S(1)}, u32[]{:S(2)}, u32[]{:S(2)}) collective-permute-start(bf16[14,48,512]{2,1,0:T(8,128)(2,1)S(1)} %collective-permute-done.2.refs_1_), channel_id=1, source_target_pairs={{0,1},{1,2},{2,3},{3,4},{4,5},{5,6},{6,7},{7,0},{8,9},{9,10},{10,1... | collective-permute-start | bytes 2064392 | tf_op jit(solution)/shard_map/ppermute | solution.py:374
  308.7 0.9 copy-start.4
  315.5 0.9 copy-start.2
  315.5 1.1 copy-start.3

commit v3 on v2

--- a/solution.py
+++ b/solution.py
@@ -35,30 +35,36 @@
     return 0.5 * jnp.tanh(0.5 * g) + 0.5
 
 
-def forward_tile(x, w_gu, w_d, act_ref):
-    slices = w_gu.shape[0]
-    a = normed(x)
-    for j in range(slices):
+def forward_first(h, w_gu, act_ref):
+    a = normed(h)
+    for j in range(w_gu.shape[0]):
         gu = dot(a, w_gu[j])
         g, u = gu[:, :FS], gu[:, FS:]
         act_ref[:, j * FS : (j + 1) * FS] = (g * sigmoid(g) * u).astype(BF16)
+    return a
+
+
+def forward_second(h, w_d, act_ref):
+    slices = w_d.shape[0]
     y = dot(act_ref[...], w_d[...].reshape(slices * FS, -1)).astype(BF16)
-    return a, (x.astype(F32) + y.astype(F32)).astype(BF16)
-
-
-def slice_tile(a, a_t, dy, dy_t, wgu, wd, acc_ref):
+    return (h.astype(F32) + y.astype(F32)).astype(BF16)
+
+
+def slice_first(a, dy, wgu, wd, buf):
     gu = dot(a, wgu)
+    dact = dot_t(dy, wd)
     g, u = gu[:, :FS], gu[:, FS:]
-    dact = dot_t(dy, wd).astype(BF16).astype(F32)
+    dact = dact.astype(BF16).astype(F32)
     s = sigmoid(g)
     silu = g * s
-    act = (silu * u).astype(BF16)
-    du = (dact * silu).astype(BF16)
-    dg = (dact * u * (s + silu * (1.0 - s))).astype(BF16)
-    acc_ref[:, 2 * FS :] += dot(dy_t, act)
-    dgu = jnp.concatenate([dg, du], axis=1)
-    acc_ref[:, : 2 * FS] += dot(a_t, dgu)
-    return dgu
+    buf[:, 2 * FS : 3 * FS] = (silu * u).astype(BF16)
+    buf[:, FS : 2 * FS] = (dact * silu).astype(BF16)
+    buf[:, :FS] = (dact * u * (s + silu * (1.0 - s))).astype(BF16)
+
+
+def slice_second(a_t, dy_t, buf, acc_gu, acc_d):
+    acc_d[...] += dot(dy_t, buf[:, 2 * FS : 3 * FS])
+    acc_gu[...] += dot(a_t, buf[:, : 2 * FS])
 
 
 def norm_back(da, h, dy):
@@ -148,7 +154,7 @@
 EVERY = 5
 
 
-def train_kernel(n, x, dy, wg, wu, wd, sums, far0, far1, far2, far3, w_gu, w_d, a1, a2, at, dyv, dyt, h1, da, act, acc, own, got, out, sem, wsem, send, recv, out_sem):
+def train_kernel(n, x, dy, wg, wu, wd, sums, far0, far1, far2, far3, w_gu, w_d, a1, a2, at, dyv, dyt, h1, da, buf0, buf1, acc_gu, acc_d, own, got, out, sem, wsem, send, recv, out_sem):
     layers, slices = w_gu.shape[:2]
     tiles = x.shape[0]
     total = layers * slices
@@ -169,7 +175,7 @@
         ]
 
     def state(m):
-        return pltpu.make_async_copy(x.at[m], a1.at[m], sem.at[m])
+        return pltpu.make_async_copy(x.at[m], h1.at[m], sem.at[m])
 
     all_dy = pltpu.make_async_copy(dy, dyv, sem.at[tiles])
     state(0).start()
@@ -183,29 +189,34 @@
     for c in weights(0):
         c.wait()
 
-    def forward(m, _):
-        state(m).wait()
-        a, h = forward_tile(a1[m], w_gu.at[0], w_d.at[0], act)
-        a1[m] = a
+    def forward_a(m):
+        a1[m] = forward_first(h1[m], w_gu.at[0], buf0)
+
+    def forward_b(m):
+        h = forward_second(h1[m], w_d.at[0], buf0)
         h1[m] = h
         a = normed(h)
         a2[m] = a
         at[m] = a.T
+        dyt[m] = dyv[m].T
         da[m] = jnp.zeros(da.shape[1:], F32)
 
-        @pl.when(m == 0)
-        def _():
-            all_dy.wait()
-
-        dyt[m] = dyv[m].T
+    def forward(m, _):
+        state(m + 1).wait()
+        forward_b(m)
+        forward_a(m + 1)
         return 0
 
-    lax.fori_loop(0, tiles, forward, 0)
+    state(0).wait()
+    forward_a(0)
+    all_dy.wait()
+    lax.fori_loop(0, tiles - 1, forward, 0)
+    forward_b(tiles - 1)
     for c in weights(1):
         c.wait()
     pl.semaphore_wait(barrier, 2)
 
-    offsets = [EVERY * k for k in range(ring.sends + 1)] + [EVERY * ring.sends + 3]
+    offsets = [1 + EVERY * k for k in range(ring.sends + 1)] + [EVERY * ring.sends + 4]
 
     def events(s, m):
         for k in reversed(range(len(offsets))):
@@ -216,40 +227,67 @@
             def _():
                 ring.event(lax.rem(t, SLOTS), t, k)
 
-    def one_slice(s, _):
-        second = s < slices
-        l = jnp.where(second, 1, 0)
-        j = jnp.where(second, s, s - slices)
-        acc[...] = jnp.zeros_like(acc)
-
-        def one_tile(m, _):
-            events(s, m)
-
-            @pl.when(s == slices)
-            def _():
-                back = norm_back(da[m], h1[m], dyv[m])
-                dyv[m] = back
-                dyt[m] = back.T
-                a = a1[m]
-                a2[m] = a
-                at[m] = a.T
-
-            dgu = slice_tile(a2[m], at[m], dyv[m], dyt[m], w_gu[l, j], w_d[l, j], acc)
-
-            @pl.when(second)
-            def _():
-                da[m] += dot_t(dgu, w_gu[l, j])
-
-            return 0
-
-        lax.fori_loop(0, tiles, one_tile, 0)
+    def finish(s):
         slot = lax.rem(s, SLOTS)
-        wide = acc.shape[0] // n
-        own[slot, :, :wide] = acc[:, : 2 * FS].astype(BF16).reshape(n, wide, 2 * FS)
-        own[slot, :, wide:] = acc[:, 2 * FS :].T.astype(BF16).reshape(n, FS // n, -1)
-        return 0
-
-    lax.fori_loop(0, total, one_slice, 0)
+        wide = acc_gu.shape[0] // n
+        own[slot, :, :wide] = acc_gu[...].astype(BF16).reshape(n, wide, 2 * FS)
+        own[slot, :, wide:] = acc_d[...].T.astype(BF16).reshape(n, FS // n, -1)
+        acc_gu[...] = jnp.zeros_like(acc_gu)
+        acc_d[...] = jnp.zeros_like(acc_d)
+
+    def backward(l, first_s):
+        second = l == layers - 1
+        states = a2 if second else a1
+
+        def turn(m):
+            back = norm_back(da[m], h1[m], dyv[m])
+            dyv[m] = back
+            dyt[m] = back.T
+            at[m] = a1[m].T
+
+        def slice_a(m, j, buf):
+            slice_first(states[m], dyv[m], w_gu[l, j], w_d[l, j], buf)
+
+        def slice_b(m, j, buf):
+            slice_second(at[m], dyt[m], buf, acc_gu, acc_d)
+            if second:
+                da[m] += dot_t(buf[:, : 2 * FS], w_gu[l, j])
+
+        def one_slice(j, _):
+            s = first_s + j
+
+            def pair(i, _):
+                m = 2 * i
+                events(s, m)
+                if not second:
+                    @pl.when(j == 0)
+                    def _():
+                        turn(m)
+                        turn(m + 1)
+
+                slice_a(m, j, buf0)
+                slice_b(lax.rem(m + tiles - 1, tiles), jnp.where(i == 0, lax.rem(j + slices - 1, slices), j), buf1)
+
+                @pl.when((i == 0) & (j > 0))
+                def _():
+                    finish(s - 1)
+
+                events(s, m + 1)
+                slice_a(m + 1, j, buf1)
+                slice_b(m, j, buf0)
+                return 0
+
+            return lax.fori_loop(0, tiles // 2, pair, 0)
+
+        buf1[:, : 3 * FS] = jnp.zeros((TM, 3 * FS), BF16)
+        lax.fori_loop(0, slices, one_slice, 0)
+        slice_b(tiles - 1, slices - 1, buf1)
+        finish(first_s + slices - 1)
+
+    acc_gu[...] = jnp.zeros_like(acc_gu)
+    acc_d[...] = jnp.zeros_like(acc_d)
+    for l in reversed(range(layers)):
+        backward(l, (layers - 1 - l) * slices)
 
     def drain(s, _):
         def one(m, _):
@@ -342,7 +380,9 @@
                 pltpu.VMEM((tiles, TM, d), BF16),
                 pltpu.VMEM((tiles, TM, d), F32),
                 pltpu.VMEM((TM, ff), BF16),
-                pltpu.VMEM((d, 3 * FS), F32),
+                pltpu.VMEM((TM, 3 * FS), BF16),
+                pltpu.VMEM((d, 2 * FS), F32),
+                pltpu.VMEM((d, FS), F32),
                 pltpu.VMEM((SLOTS, n, rows, d), BF16),
                 pltpu.VMEM((SLOTS, half, 2, rows, d), BF16),
                 pltpu.VMEM((SLOTS, n, rows, d), BF16),

time: 323 us -> 308 us (0.954)
  the two profiles are of different devices: /device:TPU:30 before, /device:TPU:22 now
where the time goes in v3:
time: 308 us
  Pallas kernels  283 us (92%)
  waiting for transfers between devices  12.9 us (4%)
  starting transfers between devices  9.34 us (3%)
    pallas_call x1, Pallas kernels, step(): pl.pallas_call(functools.partial(train_kernel, n), in_specs=[hbm] * 5, ou...  238 us
    pallas_call x4, Pallas kernels, adam(): pl.pallas_call(functools.partial(adam_kernel, len(gs)), grid_spec=pltpu.P...  45.2 us
    ppermute x4, waiting for transfers between devices, step(): near.append(lax.ppermute(far[i], 'dp', way))  12.9 us
  transfers between devices with their start and end apart: 6, of which 1 were waited for; matrix products, arithmetic and copies ran while one was open for 0% of the time, Pallas kernels for 13%

profile of v3, /device:TPU:22, one launch (start us, length us, event | category | flops | bytes accessed | tf_op | source)
XLA Modules:
  0.0 308.2 jit_solution(15419196388164491889)
XLA Ops:
  0.6 238.0 %shard_map.178 = (bf16[14,8,96,512]{3,2,1,0:T(8,128)(2,1)}, bf16[14,48,512]{2,1,0:T(8,128)(2,1)}, bf16[14,48,512]{2,1,0:T(8,128)(2,1)}, bf16[14,48,512]{2,1,0:T(8,128)(2,1)}, bf16[14,48,512]{2,1,0:T(8,128)(2,1)}) custom-call(bf16[8,512,512]{2,1,0:T(8,128)(2,1)} %bitcast.66, bf16[8,512,512]{2,1,0:T(8,128)(2,1)} %bitcast.67, bf16[2,512,1792]{2,1,0:T(8,128)(2,1)} %wg.1, ...), custom_call_target="tpu_custom_call" | custom-call | flops 127775277056 | bytes 30000000 | tf_op jit(solution)/shard_map/pallas_call | solution.py:366
  238.6 2.5 collective-permute-start
  241.1 0.0 collective-permute-start.2
  241.1 3.2 %collective-permute-start.5 = (bf16[14,48,512]{2,1,0:T(8,128)(2,1)}, bf16[14,48,512]{2,1,0:T(8,128)(2,1)}, u32[]{:S(2)}, u32[]{:S(2)}) collective-permute-start(bf16[14,48,512]{2,1,0:T(8,128)(2,1)} %get-tuple-element.53), channel_id=1, source_target_pairs={{0,7},{1,0},{2,1},{3,2},{4,3},{5,4},{6,5},{7,6},{8,15},{9,8},{10,9... | collective-permute-start | bytes 2064392 | tf_op jit(solution)/shard_map/ppermute | solution.py:410
  244.4 0.0 collective-permute-start.4
  244.4 12.9 %collective-permute-done.refs_0_ = bf16[14,48,512]{2,1,0:T(8,128)(2,1)S(1)} collective-permute-done((bf16[14,48,512]{2,1,0:T(8,128)(2,1)}, bf16[14,48,512]{2,1,0:T(8,128)(2,1)S(1)}, u32[]{:S(2)}, u32[]{:S(2)}) %collective-permute-start) | collective-permute-done | bytes 688160 | tf_op jit(solution)/shard_map/ppermute | solution.py:410
  257.3 0.0 copy-start
  257.3 3.6 %collective-permute-start.1 = (bf16[14,48,512]{2,1,0:T(8,128)(2,1)S(1)}, bf16[14,48,512]{2,1,0:T(8,128)(2,1)S(1)}, u32[]{:S(2)}, u32[]{:S(2)}) collective-permute-start(bf16[14,48,512]{2,1,0:T(8,128)(2,1)S(1)} %collective-permute-done.refs_0_), channel_id=1, source_target_pairs={{0,7},{1,0},{2,1},{3,2},{4,3},{5,4},{6,5},{7,6},{8,15},{9,8},{10,9... | collective-permute-start | bytes 2064392 | tf_op jit(solution)/shard_map/ppermute | solution.py:414
  260.8 0.0 collective-permute-done.2.refs_1_
  260.8 0.0 copy-start.1
  260.9 0.0 collective-permute-start.3
  260.9 27.2 %shard_map.179 = (bf16[2,8,64,1792]{3,2,1,0:T(8,128)(2,1)}, bf16[2,8,64,1792]{3,2,1,0:T(8,128)(2,1)}, bf16[2,7,8,32,512]{4,3,2,1,0:T(8,128)(2,1)}, f32[2,8,64,17...) custom-call(s32[1]{0:T(128)} %bitcast.where, ...), custom_call_target="tpu_custom_call" | custom-call | flops 2752512000 | bytes 68812800 | tf_op jit(solution)/shard_map/pallas_call | solution.py:339
  288.0 0.0 copy-done
  288.1 0.0 copy-done.1
  288.1 0.0 collective-permute-done.5.refs_1_
  288.1 6.0 %shard_map.180 = (bf16[2,8,64,1792]{3,2,1,0:T(8,128)(2,1)}, bf16[2,8,64,1792]{3,2,1,0:T(8,128)(2,1)}, bf16[2,7,8,32,512]{4,3,2,1,0:T(8,128)(2,1)}, f32[2,8,64,17...) custom-call(s32[1]{0:T(128)} %bitcast.where, ...), custom_call_target="tpu_custom_call", output_to_operand_aliasing={{0}: (12, {}), {1}: (13, {}), {2}: (14, {}), {3}: (15, {}),... | custom-call | flops 550502400 | bytes 13762560 | tf_op jit(solution)/shard_map/pallas_call | solution.py:339
  294.1 0.0 collective-permute-done.4.refs_0_
  294.1 0.0 copy-start.4
  294.1 0.8 copy-done.4
  295.0 6.0 %shard_map.181 = (bf16[2,8,64,1792]{3,2,1,0:T(8,128)(2,1)}, bf16[2,8,64,1792]{3,2,1,0:T(8,128)(2,1)}, bf16[2,7,8,32,512]{4,3,2,1,0:T(8,128)(2,1)}, f32[2,8,64,17...) custom-call(s32[1]{0:T(128)} %bitcast.where, ...), custom_call_target="tpu_custom_call", output_to_operand_aliasing={{0}: (12, {}), {1}: (13, {}), {2}: (14, {}), {3}: (15, {}),... | custom-call | flops 550502400 | bytes 13762560 | tf_op jit(solution)/shard_map/pallas_call | solution.py:339
  301.0 0.0 collective-permute-done.1.refs_0_
  301.0 0.0 copy-start.2
  301.0 0.0 collective-permute-done.3.refs_1_
  301.0 0.0 copy-start.3
  301.0 0.8 copy-done.2
  301.8 0.3 copy-done.3
  302.1 6.0 %shard_map.182 = (bf16[2,8,64,1792]{3,2,1,0:T(8,128)(2,1)}, bf16[2,8,64,1792]{3,2,1,0:T(8,128)(2,1)}, bf16[2,7,8,32,512]{4,3,2,1,0:T(8,128)(2,1)}, f32[2,8,64,17...) custom-call(s32[1]{0:T(128)} %bitcast.where, ...), custom_call_target="tpu_custom_call", output_to_operand_aliasing={{0}: (12, {}), {1}: (13, {}), {2}: (14, {}), {3}: (15, {}),... | custom-call | flops 550502400 | bytes 13762560 | tf_op jit(solution)/shard_map/pallas_call | solution.py:339
Async XLA Ops:
  238.6 18.7 %collective-permute-start = (bf16[14,48,512]{2,1,0:T(8,128)(2,1)}, bf16[14,48,512]{2,1,0:T(8,128)(2,1)S(1)}, u32[]{:S(2)}, u32[]{:S(2)}) collective-permute-start(bf16[14,48,512]{2,1,0:T(8,128)(2,1)} %get-tuple-element.50), channel_id=1, source_target_pairs={{0,7},{1,0},{2,1},{3,2},{4,3},{5,4},{6,5},{7,6},{8,15},{9,8},{10,9... | collective-permute-start | bytes 2064392 | tf_op jit(solution)/shard_map/ppermute | solution.py:410
  241.1 19.7 %collective-permute-start.2 = (bf16[14,48,512]{2,1,0:T(8,128)(2,1)}, bf16[14,48,512]{2,1,0:T(8,128)(2,1)S(1)}, u32[]{:S(2)}, u32[]{:S(2)}) collective-permute-start(bf16[14,48,512]{2,1,0:T(8,128)(2,1)} %get-tuple-element.51), channel_id=1, source_target_pairs={{0,1},{1,2},{2,3},{3,4},{4,5},{5,6},{6,7},{7,0},{8,9},{9,10},{10,1... | collective-permute-start | bytes 2064392 | tf_op jit(solution)/shard_map/ppermute | solution.py:410
  241.1 46.9 %collective-permute-start.5 = (bf16[14,48,512]{2,1,0:T(8,128)(2,1)}, bf16[14,48,512]{2,1,0:T(8,128)(2,1)}, u32[]{:S(2)}, u32[]{:S(2)}) collective-permute-start(bf16[14,48,512]{2,1,0:T(8,128)(2,1)} %get-tuple-element.53), channel_id=1, source_target_pairs={{0,7},{1,0},{2,1},{3,2},{4,3},{5,4},{6,5},{7,6},{8,15},{9,8},{10,9... | collective-permute-start | bytes 2064392 | tf_op jit(solution)/shard_map/ppermute | solution.py:410
  244.4 49.8 %collective-permute-start.4 = (bf16[14,48,512]{2,1,0:T(8,128)(2,1)}, bf16[14,48,512]{2,1,0:T(8,128)(2,1)S(1)}, u32[]{:S(2)}, u32[]{:S(2)}) collective-permute-start(bf16[14,48,512]{2,1,0:T(8,128)(2,1)} %get-tuple-element.52), channel_id=1, source_target_pairs={{0,1},{1,2},{2,3},{3,4},{4,5},{5,6},{6,7},{7,0},{8,9},{9,10},{10,1... | collective-permute-start | bytes 2064392 | tf_op jit(solution)/shard_map/ppermute | solution.py:410
  257.3 30.8 %copy-start = (bf16[14,48,512]{2,1,0:T(8,128)(2,1)}, bf16[14,48,512]{2,1,0:T(8,128)(2,1)S(1)}, u32[]{:S(2)}) copy-start(bf16[14,48,512]{2,1,0:T(8,128)(2,1)S(1)} %collective-permute-done.refs_0_) | copy-start | bytes 2064388
  257.3 43.7 %collective-permute-start.1 = (bf16[14,48,512]{2,1,0:T(8,128)(2,1)S(1)}, bf16[14,48,512]{2,1,0:T(8,128)(2,1)S(1)}, u32[]{:S(2)}, u32[]{:S(2)}) collective-permute-start(bf16[14,48,512]{2,1,0:T(8,128)(2,1)S(1)} %collective-permute-done.refs_0_), channel_id=1, source_target_pairs={{0,7},{1,0},{2,1},{3,2},{4,3},{5,4},{6,5},{7,6},{8,15},{9,8},{10,9... | collective-permute-start | bytes 2064392 | tf_op jit(solution)/shard_map/ppermute | solution.py:414
  260.8 27.2 %copy-start.1 = (bf16[14,48,512]{2,1,0:T(8,128)(2,1)}, bf16[14,48,512]{2,1,0:T(8,128)(2,1)S(1)}, u32[]{:S(2)}) copy-start(bf16[14,48,512]{2,1,0:T(8,128)(2,1)S(1)} %collective-permute-done.2.refs_1_) | copy-start | bytes 2064388
  260.9 40.1 %collective-permute-start.3 = (bf16[14,48,512]{2,1,0:T(8,128)(2,1)S(1)}, bf16[14,48,512]{2,1,0:T(8,128)(2,1)S(1)}, u32[]{:S(2)}, u32[]{:S(2)}) collective-permute-start(bf16[14,48,512]{2,1,0:T(8,128)(2,1)S(1)} %collective-permute-done.2.refs_1_), channel_id=1, source_target_pairs={{0,1},{1,2},{2,3},{3,4},{4,5},{5,6},{6,7},{7,0},{8,9},{9,10},{10,1... | collective-permute-start | bytes 2064392 | tf_op jit(solution)/shard_map/ppermute | solution.py:414
  294.1 0.9 copy-start.4
  301.0 0.9 copy-start.2
  301.0 1.1 copy-start.3

commit v4 on v3

--- a/solution.py
+++ b/solution.py
@@ -35,10 +35,11 @@
     return 0.5 * jnp.tanh(0.5 * g) + 0.5
 
 
-def forward_first(h, w_gu, act_ref):
+def forward_first(h, w_gu, act_ref, ready=lambda j: None):
     a = normed(h)
-    for j in range(w_gu.shape[0]):
-        gu = dot(a, w_gu[j])
+    for j in range(w_gu.shape[1] // (2 * FS)):
+        ready(j)
+        gu = dot(a, w_gu[:, 2 * j * FS : 2 * (j + 1) * FS])
         g, u = gu[:, :FS], gu[:, FS:]
         act_ref[:, j * FS : (j + 1) * FS] = (g * sigmoid(g) * u).astype(BF16)
     return a
@@ -142,20 +143,22 @@
         if k == self.sends:
             for copy in self.write_out(slot, t):
                 copy.start()
-            for sent in range(self.sends):
-                for way in (0, 1):
-                    self.copy(slot, sent, way).wait_send()
+        for sent in range(max(k - 2, 0), k - 1) if k < self.sends else range(k - 2, k) if k == self.sends else ():
+            for way in (0, 1):
+                self.copy(slot, sent, way).wait_send()
         if k == self.sends + 1:
             for copy in self.write_out(slot, t):
                 copy.wait()
 
 
 SLOTS = 4
-EVERY = 5
-
-
-def train_kernel(n, x, dy, wg, wu, wd, sums, far0, far1, far2, far3, w_gu, w_d, a1, a2, at, dyv, dyt, h1, da, buf0, buf1, acc_gu, acc_d, own, got, out, sem, wsem, send, recv, out_sem):
-    layers, slices = w_gu.shape[:2]
+EVERY = 6
+EARLY, SOONER = 2, 5
+
+
+def train_kernel(n, x, dy, wg, wu, wd, sums, far0, far1, far2, far3, dgu, w_gu, w_d, a1, a2, at, dyv, dyt, h1, pulled, act, buf0, buf1,
+                 acc_gu, acc_d, own, got, out, sem, wsem, push_sem, pull_sem, send, recv, out_sem):
+    layers, slices = w_d.shape[:2]
     tiles = x.shape[0]
     total = layers * slices
     barrier = pltpu.get_barrier_semaphore()
@@ -163,43 +166,43 @@
     for device in ring.to:
         pl.semaphore_signal(barrier, inc=1, device_id=device, device_id_type=pl.DeviceIdType.MESH)
 
-    def weights(l):
-        return [
-            copy
-            for j in range(slices)
-            for copy in (
-                pltpu.make_async_copy(wg.at[l, :, pl.ds(j * FS, FS)], w_gu.at[l, j, :, pl.ds(0, FS)], wsem.at[l, j, 0]),
-                pltpu.make_async_copy(wu.at[l, :, pl.ds(j * FS, FS)], w_gu.at[l, j, :, pl.ds(FS, FS)], wsem.at[l, j, 1]),
-                pltpu.make_async_copy(wd.at[l, pl.ds(j * FS, FS), :], w_d.at[l, j], wsem.at[l, j, 2]),
-            )
-        ]
+    def columns(j):
+        return pl.ds(pl.multiple_of(j * (2 * FS), 2 * FS), 2 * FS)
+
+    def weights(l, j):
+        return (
+            pltpu.make_async_copy(wg.at[l, :, pl.ds(j * FS, FS)], w_gu.at[l, :, pl.ds(2 * j * FS, FS)], wsem.at[l, j, 0]),
+            pltpu.make_async_copy(wu.at[l, :, pl.ds(j * FS, FS)], w_gu.at[l, :, pl.ds(2 * j * FS + FS, FS)], wsem.at[l, j, 1]),
+            pltpu.make_async_copy(wd.at[l, pl.ds(j * FS, FS), :], w_d.at[l, j], wsem.at[l, j, 2]),
+        )
 
     def state(m):
         return pltpu.make_async_copy(x.at[m], h1.at[m], sem.at[m])
 
     all_dy = pltpu.make_async_copy(dy, dyv, sem.at[tiles])
     state(0).start()
-    for c in weights(0):
-        c.start()
-    for m in range(1, tiles):
+    for i in (0, 1, 2):
+        for j in range(slices):
+            weights(0, j)[i].start()
+        if i == 1:
+            state(1).start()
+    all_dy.start()
+    for m in range(2, tiles):
         state(m).start()
-    all_dy.start()
-    for c in weights(1):
-        c.start()
-    for c in weights(0):
-        c.wait()
-
-    def forward_a(m):
-        a1[m] = forward_first(h1[m], w_gu.at[0], buf0)
+    for j in range(slices):
+        for c in weights(1, j):
+            c.start()
+
+    def forward_a(m, ready=lambda j: None):
+        a1[m] = forward_first(h1[m], w_gu.at[0], act, ready)
 
     def forward_b(m):
-        h = forward_second(h1[m], w_d.at[0], buf0)
+        h = forward_second(h1[m], w_d.at[0], act)
         h1[m] = h
         a = normed(h)
         a2[m] = a
         at[m] = a.T
         dyt[m] = dyv[m].T
-        da[m] = jnp.zeros(da.shape[1:], F32)
 
     def forward(m, _):
         state(m + 1).wait()
@@ -207,25 +210,46 @@
         forward_a(m + 1)
         return 0
 
+    def ready(j):
+        for first, last in ((0, 2), (2, slices)):
+            if j == first:
+                for here in range(first, last):
+                    for c in weights(0, here)[:2]:
+                        c.wait()
+
     state(0).wait()
-    forward_a(0)
+    forward_a(0, ready)
+    for j in range(slices):
+        weights(0, j)[2].wait()
     all_dy.wait()
     lax.fori_loop(0, tiles - 1, forward, 0)
     forward_b(tiles - 1)
-    for c in weights(1):
-        c.wait()
+    for j in range(slices):
+        for c in weights(1, j):
+            c.wait()
     pl.semaphore_wait(barrier, 2)
 
-    offsets = [1 + EVERY * k for k in range(ring.sends + 1)] + [EVERY * ring.sends + 4]
-
-    def events(s, m):
-        for k in reversed(range(len(offsets))):
-            ago, at_tile = divmod(offsets[k], tiles)
-            t = s - 1 - ago
-
-            @pl.when((m == at_tile) & (t >= 0) & (t < total))
-            def _():
-                ring.event(lax.rem(t, SLOTS), t, k)
+    def offset(k, every):
+        return 1 + every * k if k <= ring.sends else 5 + every * ring.sends
+
+    def events(now, m, odd):
+        for k in reversed(range(ring.sends + 2)):
+            cases = []
+            for every, low, high in ((SOONER, 0, EARLY), (EVERY, EARLY, total)):
+                ago, at_tile = divmod(offset(k, every), tiles)
+                place = now - 1 - ago
+                t = jnp.where(place > slices, place - 1, place)
+                if at_tile % 2 == odd:
+                    cases.append(((m == at_tile) & (place != slices) & (t >= low) & (t < high), t))
+            if cases:
+                here, t = cases[0]
+                for other, u in cases[1:]:
+                    t = jnp.where(other, u, t)
+                    here = here | other
+
+                @pl.when(here)
+                def _():
+                    ring.event(lax.rem(t, SLOTS), t, k)
 
     def finish(s):
         slot = lax.rem(s, SLOTS)
@@ -235,68 +259,93 @@
         acc_gu[...] = jnp.zeros_like(acc_gu)
         acc_d[...] = jnp.zeros_like(acc_d)
 
-    def backward(l, first_s):
+    def push(m, j, i):
+        return pltpu.make_async_copy((buf0, buf1)[i].at[:, pl.ds(0, 2 * FS)], dgu.at[m, :, columns(j)], push_sem.at[i])
+
+    def pull(m):
+        return pltpu.make_async_copy(dgu.at[m], pulled.at[lax.rem(m, 2)], pull_sem.at[lax.rem(m, 2)])
+
+    def backward(l):
         second = l == layers - 1
         states = a2 if second else a1
 
-        def turn(m):
-            back = norm_back(da[m], h1[m], dyv[m])
-            dyv[m] = back
-            dyt[m] = back.T
-            at[m] = a1[m].T
-
         def slice_a(m, j, buf):
-            slice_first(states[m], dyv[m], w_gu[l, j], w_d[l, j], buf)
-
-        def slice_b(m, j, buf):
+            slice_first(states[m], dyv[m], w_gu[l, :, columns(j)], w_d[l, j], buf)
+
+        def slice_b(m, buf):
             slice_second(at[m], dyt[m], buf, acc_gu, acc_d)
-            if second:
-                da[m] += dot_t(buf[:, : 2 * FS], w_gu[l, j])
 
         def one_slice(j, _):
-            s = first_s + j
+            now = j if second else slices + 1 + j
 
             def pair(i, _):
-                m = 2 * i
-                events(s, m)
-                if not second:
-                    @pl.when(j == 0)
-                    def _():
-                        turn(m)
-                        turn(m + 1)
-
-                slice_a(m, j, buf0)
-                slice_b(lax.rem(m + tiles - 1, tiles), jnp.where(i == 0, lax.rem(j + slices - 1, slices), j), buf1)
-
-                @pl.when((i == 0) & (j > 0))
-                def _():
-                    finish(s - 1)
-
-                events(s, m + 1)
-                slice_a(m + 1, j, buf1)
-                slice_b(m, j, buf0)
+                for half, here, there in ((0, buf0, buf1), (1, buf1, buf0)):
+                    m = 2 * i + half
+                    events(now, m, half)
+                    if second:
+                        @pl.when((i > 0) | (j > 0))
+                        def _():
+                            push(m, j, half).wait()
+
+                    slice_a(m, j, here)
+                    slice_b(lax.rem(m + tiles - 1, tiles), there)
+                    if second:
+                        push(m, j, half).start()
+                    if half == 0:
+                        @pl.when((i == 0) & (j > 0))
+                        def _():
+                            finish((0 if second else slices) + j - 1)
+
                 return 0
 
             return lax.fori_loop(0, tiles // 2, pair, 0)
 
-        buf1[:, : 3 * FS] = jnp.zeros((TM, 3 * FS), BF16)
+        buf1[...] = jnp.zeros_like(buf1)
         lax.fori_loop(0, slices, one_slice, 0)
-        slice_b(tiles - 1, slices - 1, buf1)
-        finish(first_s + slices - 1)
+        if second:
+            for m in (0, 1):
+                pull(m).start()
+        slice_b(tiles - 1, buf1)
+        finish((slices if second else total) - 1)
+
+    def turn(m, _):
+        for odd in (0, 1):
+            events(slices, m, odd)
+        pull(m).wait()
+        parts = 2
+        size = TM // parts
+        for part in range(parts):
+            rows = pl.ds(part * size, size)
+            da = dot_t(pulled[lax.rem(m, 2), rows], w_gu[layers - 1])
+            back = norm_back(da, h1[m, rows], dyv[m, rows])
+            dyv[m, rows] = back
+            dyt[m, :, rows] = back.T
+            at[m, :, rows] = a1[m, rows].T
+
+        @pl.when(m + 2 < tiles)
+        def _():
+            pull(m + 2).start()
+
+        return 0
 
     acc_gu[...] = jnp.zeros_like(acc_gu)
     acc_d[...] = jnp.zeros_like(acc_d)
-    for l in reversed(range(layers)):
-        backward(l, (layers - 1 - l) * slices)
-
-    def drain(s, _):
-        def one(m, _):
-            events(s, m)
+    backward(layers - 1)
+    for i in (0, 1):
+        push(i, 0, i).wait()
+    lax.fori_loop(0, tiles, turn, 0)
+    backward(0)
+
+    def drain(now, _):
+        def pair(i, _):
+            for half in (0, 1):
+                events(now, 2 * i + half, half)
             return 0
 
-        return lax.fori_loop(0, tiles, one, 0)
-
-    lax.fori_loop(total, total + 1 + offsets[-1] // tiles, drain, 0)
+        return lax.fori_loop(0, tiles // 2, pair, 0)
+
+    end = total + 1
+    lax.fori_loop(end, end + 1 + offset(ring.sends + 1, EVERY) // tiles, drain, 0)
 
 
 def adam_math(w, m, v, g):
@@ -346,7 +395,7 @@
         ),
         out_shape=[jax.ShapeDtypeStruct(a.shape, a.dtype) for a in arrays],
         input_output_aliases={1 + len(gs) + 9 + i: i for i in range(len(extra))},
-        compiler_params=pltpu.CompilerParams(vmem_limit_bytes=60_000_000),
+        compiler_params=pltpu.CompilerParams(vmem_limit_bytes=32_000_000),
         cost_estimate=pl.CostEstimate(flops=40 * size, bytes_accessed=size, transcendentals=0),
     )(where, *gs, *arrays, *extra)
 
@@ -363,14 +412,15 @@
         hbm = pl.BlockSpec(memory_space=pl.ANY)
         half, rows = n // 2, (d + FS) // n
         mm = 2 * tokens * d * ff
-        sums, *far = pl.pallas_call(
+        sums, *far, _ = pl.pallas_call(
             functools.partial(train_kernel, n),
             in_specs=[hbm] * 5,
-            out_specs=[hbm] * 5,
+            out_specs=[hbm] * 6,
             out_shape=[jax.ShapeDtypeStruct((layers * slices, n, rows, d), BF16)]
-            + [jax.ShapeDtypeStruct((layers * slices, rows // 2, d), BF16)] * 4,
+            + [jax.ShapeDtypeStruct((layers * slices, rows // 2, d), BF16)] * 4
+            + [jax.ShapeDtypeStruct((tiles, TM, 2 * ff), BF16)],
             scratch_shapes=[
-                pltpu.VMEM((layers, slices, d, 2 * FS), BF16),
+                pltpu.VMEM((layers, d, 2 * ff), BF16),
                 pltpu.VMEM((layers, slices, FS, d), BF16),
                 pltpu.VMEM((tiles, TM, d), BF16),
                 pltpu.VMEM((tiles, TM, d), BF16),
@@ -378,8 +428,9 @@
                 pltpu.VMEM((tiles, TM, d), BF16),
                 pltpu.VMEM((tiles, d, TM), BF16),
                 pltpu.VMEM((tiles, TM, d), BF16),
-                pltpu.VMEM((tiles, TM, d), F32),
+                pltpu.VMEM((2, TM, 2 * ff), BF16),
                 pltpu.VMEM((TM, ff), BF16),
+                pltpu.VMEM((TM, 3 * FS), BF16),
                 pltpu.VMEM((TM, 3 * FS), BF16),
                 pltpu.VMEM((d, 2 * FS), F32),
                 pltpu.VMEM((d, FS), F32),
@@ -388,12 +439,14 @@
                 pltpu.VMEM((SLOTS, n, rows, d), BF16),
                 pltpu.SemaphoreType.DMA((tiles + 1,)),
                 pltpu.SemaphoreType.DMA((layers, slices, 3)),
+                pltpu.SemaphoreType.DMA((2,)),
+                pltpu.SemaphoreType.DMA((2,)),
                 pltpu.SemaphoreType.DMA((SLOTS, 2 * half - 2, 2)),
                 pltpu.SemaphoreType.DMA((SLOTS, 2 * half - 2, 2)),
                 pltpu.SemaphoreType.DMA((SLOTS, n + 1)),
             ],
             compiler_params=pltpu.CompilerParams(vmem_limit_bytes=VMEM_LIMIT, collective_id=0, has_side_effects=True),
-            cost_estimate=pl.CostEstimate(flops=17 * mm, bytes_accessed=30 * 10**6, transcendentals=0),
+            cost_estimate=pl.CostEstimate(flops=17 * mm, bytes_accessed=90 * 10**6, transcendentals=0),
         )(x, dy, wg, wu, wd)
         chunks = [a.reshape(layers, n, d // n, ff) if a.shape[1] == d else a.reshape(layers, slices, n, FS // n, d) for a in arrays]
         left = [(i, (i + n - 1) % n) for i in range(n)]

time: 308 us -> 308 us (level)
  Pallas kernels: 283 us -> 275 us
  local copies, waits for them, and re-layouts: 1.93 us -> 9.2 us
    unnamed x10 -> x8, local copies, waits for them, and re-layouts: 1.93 us -> 9.2 us
    pallas_call x1, Pallas kernels: 238 us -> 234 us  [step(): pl.pallas_call(functools.partial(train_kernel, n), in_specs=[hbm] * 5, ou...]
    pallas_call x4, Pallas kernels: 45.2 us -> 41 us  [adam(): pl.pallas_call(functools.partial(adam_kernel, len(gs)), grid_spec=pltpu.P...]
  transfers between devices with their start and end apart: 6 -> 6, of which waited for: 1 -> 1; matrix products, arithmetic and copies ran while one was open for 0% -> 0% of each run, Pallas kernels for 13% -> 12%
where the time goes in v4:
time: 308 us
  Pallas kernels  275 us (89%)
  waiting for transfers between devices  12.9 us (4%)
  starting transfers between devices  10.2 us (3%)
  local copies, waits for them, and re-layouts  9.2 us (3%)
    pallas_call x1, Pallas kernels, step(): pl.pallas_call(functools.partial(train_kernel, n), in_specs=[hbm] * 5, ou...  234 us
    pallas_call x4, Pallas kernels, adam(): pl.pallas_call(functools.partial(adam_kernel, len(gs)), grid_spec=pltpu.P...  41 us
    ppermute x4, waiting for transfers between devices, step(): near.append(lax.ppermute(far[i], 'dp', way))  12.9 us
    unnamed x8, local copies, waits for them, and re-layouts  9.2 us
    ppermute x4, starting transfers between devices, step(): near.append(lax.ppermute(far[i], 'dp', way))  6.59 us
  transfers between devices with their start and end apart: 6, of which 1 were waited for; matrix products, arithmetic and copies ran while one was open for 0% of the time, Pallas kernels for 12%

profile of v4, /device:TPU:22, one launch (start us, length us, event | category | flops | bytes accessed | tf_op | source)
XLA Modules:
  0.0 307.8 jit_solution(8015849076138265341)
XLA Ops:
  0.6 233.6 %shard_map.178 = (bf16[14,8,96,512]{3,2,1,0:T(8,128)(2,1)}, bf16[14,48,512]{2,1,0:T(8,128)(2,1)}, bf16[14,48,512]{2,1,0:T(8,128)(2,1)}, bf16[14,48,512]{2,1,0:T(...) custom-call(bf16[8,512,512]{2,1,0:T(8,128)(2,1)} %bitcast.66, bf16[8,512,512]{2,1,0:T(8,128)(2,1)} %bitcast.67, ...), custom_call_target="tpu_custom_call" | custom-call | flops 127775277056 | bytes 90000000 | tf_op jit(solution)/shard_map/pallas_call | solution.py:415
  234.3 3.4 %collective-permute-start = (bf16[14,48,512]{2,1,0:T(8,128)(2,1)}, bf16[14,48,512]{2,1,0:T(8,128)(2,1)S(1)}, u32[]{:S(2)}, u32[]{:S(2)}) collective-permute-start(bf16[14,48,512]{2,1,0:T(8,128)(2,1)} %get-tuple-element.50), channel_id=1, source_target_pairs={{0,7},{1,0},{2,1},{3,2},{4,3},{5,4},{6,5},{7,6},{8,15},{9,8},{10,9... | collective-permute-start | bytes 2064392 | tf_op jit(solution)/shard_map/ppermute | solution.py:463
  237.6 0.0 collective-permute-start.2
  237.6 3.2 %collective-permute-start.5 = (bf16[14,48,512]{2,1,0:T(8,128)(2,1)}, bf16[14,48,512]{2,1,0:T(8,128)(2,1)}, u32[]{:S(2)}, u32[]{:S(2)}) collective-permute-start(bf16[14,48,512]{2,1,0:T(8,128)(2,1)} %get-tuple-element.53), channel_id=1, source_target_pairs={{0,7},{1,0},{2,1},{3,2},{4,3},{5,4},{6,5},{7,6},{8,15},{9,8},{10,9... | collective-permute-start | bytes 2064392 | tf_op jit(solution)/shard_map/ppermute | solution.py:463
  240.9 0.0 collective-permute-start.4
  240.9 12.9 %collective-permute-done.refs_0_ = bf16[14,48,512]{2,1,0:T(8,128)(2,1)S(1)} collective-permute-done((bf16[14,48,512]{2,1,0:T(8,128)(2,1)}, bf16[14,48,512]{2,1,0:T(8,128)(2,1)S(1)}, u32[]{:S(2)}, u32[]{:S(2)}) %collective-permute-start) | collective-permute-done | bytes 688160 | tf_op jit(solution)/shard_map/ppermute | solution.py:463
  253.8 3.6 %collective-permute-start.1 = (bf16[14,48,512]{2,1,0:T(8,128)(2,1)S(1)}, bf16[14,48,512]{2,1,0:T(8,128)(2,1)S(1)}, u32[]{:S(2)}, u32[]{:S(2)}) collective-permute-start(bf16[14,48,512]{2,1,0:T(8,128)(2,1)S(1)} %collective-permute-done.refs_0_), channel_id=1, source_target_pairs={{0,7},{1,0},{2,1},{3,2},{4,3},{5,4},{6,5},{7,6},{8,15},{9,8},{10,9... | collective-permute-start | bytes 2064392 | tf_op jit(solution)/shard_map/ppermute | solution.py:467
  257.4 0.0 collective-permute-done.2.refs_1_
  257.4 0.0 collective-permute-start.3
  257.4 0.0 copy-start
  257.4 3.1 %copy-done = f32[2,512,1792]{2,1,0:T(8,128)S(1)} copy-done((f32[2,512,1792]{2,1,0:T(8,128)S(1)}, f32[2,512,1792]{2,1,0:T(8,128)}, u32[]{:S(2)}) %copy-start) | copy-done | bytes 7340056
  260.4 0.0 copy-start.1
  260.4 2.0 copy-done.1
  262.5 0.0 copy-start.2
  262.5 2.0 copy-done.2
  264.5 0.0 copy-start.3
  264.5 2.0 copy-done.3
  266.6 25.0 %shard_map.179 = (bf16[2,8,64,1792]{3,2,1,0:T(8,128)(2,1)}, bf16[2,8,64,1792]{3,2,1,0:T(8,128)(2,1)}, bf16[2,7,8,32,512]{4,3,2,1,0:T(8,128)(2,1)}, f32[2,8,64,17...) custom-call(s32[1]{0:T(128)} %bitcast.where, ...), custom_call_target="tpu_custom_call" | custom-call | flops 2752512000 | bytes 68812800 | tf_op jit(solution)/shard_map/pallas_call | solution.py:388
  291.6 0.0 collective-permute-done.5.refs_1_
  291.6 5.4 %shard_map.180 = (bf16[2,8,64,1792]{3,2,1,0:T(8,128)(2,1)}, bf16[2,8,64,1792]{3,2,1,0:T(8,128)(2,1)}, bf16[2,7,8,32,512]{4,3,2,1,0:T(8,128)(2,1)}, f32[2,8,64,17...) custom-call(s32[1]{0:T(128)} %bitcast.where, ...), custom_call_target="tpu_custom_call", output_to_operand_aliasing={{0}: (12, {}), {1}: (13, {}), {2}: (14, {}), {3}: (15, {}),... | custom-call | flops 550502400 | bytes 13762560 | tf_op jit(solution)/shard_map/pallas_call | solution.py:388
  297.0 0.0 collective-permute-done.4.refs_0_
  297.0 5.3 %shard_map.181 = (bf16[2,8,64,1792]{3,2,1,0:T(8,128)(2,1)}, bf16[2,8,64,1792]{3,2,1,0:T(8,128)(2,1)}, bf16[2,7,8,32,512]{4,3,2,1,0:T(8,128)(2,1)}, f32[2,8,64,17...) custom-call(s32[1]{0:T(128)} %bitcast.where, ...), custom_call_target="tpu_custom_call", output_to_operand_aliasing={{0}: (12, {}), {1}: (13, {}), {2}: (14, {}), {3}: (15, {}),... | custom-call | flops 550502400 | bytes 13762560 | tf_op jit(solution)/shard_map/pallas_call | solution.py:388
  302.3 0.0 collective-permute-done.1.refs_0_
  302.3 0.0 collective-permute-done.3.refs_1_
  302.3 5.3 %shard_map.182 = (bf16[2,8,64,1792]{3,2,1,0:T(8,128)(2,1)}, bf16[2,8,64,1792]{3,2,1,0:T(8,128)(2,1)}, bf16[2,7,8,32,512]{4,3,2,1,0:T(8,128)(2,1)}, f32[2,8,64,17...) custom-call(s32[1]{0:T(128)} %bitcast.where, ...), custom_call_target="tpu_custom_call", output_to_operand_aliasing={{0}: (12, {}), {1}: (13, {}), {2}: (14, {}), {3}: (15, {}),... | custom-call | flops 550502400 | bytes 13762560 | tf_op jit(solution)/shard_map/pallas_call | solution.py:388
Async XLA Ops:
  234.3 19.5 %collective-permute-start = (bf16[14,48,512]{2,1,0:T(8,128)(2,1)}, bf16[14,48,512]{2,1,0:T(8,128)(2,1)S(1)}, u32[]{:S(2)}, u32[]{:S(2)}) collective-permute-start(bf16[14,48,512]{2,1,0:T(8,128)(2,1)} %get-tuple-element.50), channel_id=1, source_target_pairs={{0,7},{1,0},{2,1},{3,2},{4,3},{5,4},{6,5},{7,6},{8,15},{9,8},{10,9... | collective-permute-start | bytes 2064392 | tf_op jit(solution)/shard_map/ppermute | solution.py:463
  237.6 19.7 %collective-permute-start.2 = (bf16[14,48,512]{2,1,0:T(8,128)(2,1)}, bf16[14,48,512]{2,1,0:T(8,128)(2,1)S(1)}, u32[]{:S(2)}, u32[]{:S(2)}) collective-permute-start(bf16[14,48,512]{2,1,0:T(8,128)(2,1)} %get-tuple-element.51), channel_id=1, source_target_pairs={{0,1},{1,2},{2,3},{3,4},{4,5},{5,6},{6,7},{7,0},{8,9},{9,10},{10,1... | collective-permute-start | bytes 2064392 | tf_op jit(solution)/shard_map/ppermute | solution.py:463
  237.6 53.9 %collective-permute-start.5 = (bf16[14,48,512]{2,1,0:T(8,128)(2,1)}, bf16[14,48,512]{2,1,0:T(8,128)(2,1)}, u32[]{:S(2)}, u32[]{:S(2)}) collective-permute-start(bf16[14,48,512]{2,1,0:T(8,128)(2,1)} %get-tuple-element.53), channel_id=1, source_target_pairs={{0,7},{1,0},{2,1},{3,2},{4,3},{5,4},{6,5},{7,6},{8,15},{9,8},{10,9... | collective-permute-start | bytes 2064392 | tf_op jit(solution)/shard_map/ppermute | solution.py:463
  240.9 56.1 %collective-permute-start.4 = (bf16[14,48,512]{2,1,0:T(8,128)(2,1)}, bf16[14,48,512]{2,1,0:T(8,128)(2,1)S(1)}, u32[]{:S(2)}, u32[]{:S(2)}) collective-permute-start(bf16[14,48,512]{2,1,0:T(8,128)(2,1)} %get-tuple-element.52), channel_id=1, source_target_pairs={{0,1},{1,2},{2,3},{3,4},{4,5},{5,6},{6,7},{7,0},{8,9},{9,10},{10,1... | collective-permute-start | bytes 2064392 | tf_op jit(solution)/shard_map/ppermute | solution.py:463
  253.8 48.5 %collective-permute-start.1 = (bf16[14,48,512]{2,1,0:T(8,128)(2,1)S(1)}, bf16[14,48,512]{2,1,0:T(8,128)(2,1)S(1)}, u32[]{:S(2)}, u32[]{:S(2)}) collective-permute-start(bf16[14,48,512]{2,1,0:T(8,128)(2,1)S(1)} %collective-permute-done.refs_0_), channel_id=1, source_target_pairs={{0,7},{1,0},{2,1},{3,2},{4,3},{5,4},{6,5},{7,6},{8,15},{9,8},{10,9... | collective-permute-start | bytes 2064392 | tf_op jit(solution)/shard_map/ppermute | solution.py:467
  257.4 45.0 %collective-permute-start.3 = (bf16[14,48,512]{2,1,0:T(8,128)(2,1)S(1)}, bf16[14,48,512]{2,1,0:T(8,128)(2,1)S(1)}, u32[]{:S(2)}, u32[]{:S(2)}) collective-permute-start(bf16[14,48,512]{2,1,0:T(8,128)(2,1)S(1)} %collective-permute-done.2.refs_1_), channel_id=1, source_target_pairs={{0,1},{1,2},{2,3},{3,4},{4,5},{5,6},{6,7},{7,0},{8,9},{9,10},{10,1... | collective-permute-start | bytes 2064392 | tf_op jit(solution)/shard_map/ppermute | solution.py:467
  257.4 3.1 %copy-start = (f32[2,512,1792]{2,1,0:T(8,128)S(1)}, f32[2,512,1792]{2,1,0:T(8,128)}, u32[]{:S(2)}) copy-start(f32[2,512,1792]{2,1,0:T(8,128)} %param.16) | copy-start | bytes 22020100
  260.4 2.0 copy-start.1
  262.5 2.0 copy-start.2
  264.5 2.0 copy-start.3

commit v5 on v4

--- a/solution.py
+++ b/solution.py
@@ -9,6 +9,7 @@
 
 
 TM = 512
+PAIR = 2
 FS = 256
 F32, BF16 = jnp.float32, jnp.bfloat16
 VMEM_LIMIT = 67_000_000
@@ -58,14 +59,15 @@
     dact = dact.astype(BF16).astype(F32)
     s = sigmoid(g)
     silu = g * s
-    buf[:, 2 * FS : 3 * FS] = (silu * u).astype(BF16)
-    buf[:, FS : 2 * FS] = (dact * silu).astype(BF16)
-    buf[:, :FS] = (dact * u * (s + silu * (1.0 - s))).astype(BF16)
+    shape = buf.shape[:2] + (FS,)
+    buf[:, :, 2 * FS : 3 * FS] = (silu * u).astype(BF16).reshape(shape)
+    buf[:, :, FS : 2 * FS] = (dact * silu).astype(BF16).reshape(shape)
+    buf[:, :, :FS] = (dact * u * (s + silu * (1.0 - s))).astype(BF16).reshape(shape)
 
 
 def slice_second(a_t, dy_t, buf, acc_gu, acc_d):
-    acc_d[...] += dot(dy_t, buf[:, 2 * FS : 3 * FS])
-    acc_gu[...] += dot(a_t, buf[:, : 2 * FS])
+    acc_d[...] += sum(dot(dy_t[i], buf[i, :, 2 * FS : 3 * FS]) for i in range(PAIR))
+    acc_gu[...] += sum(dot(a_t[i], buf[i, :, : 2 * FS]) for i in range(PAIR))
 
 
 def norm_back(da, h, dy):
@@ -143,7 +145,7 @@
         if k == self.sends:
             for copy in self.write_out(slot, t):
                 copy.start()
-        for sent in range(max(k - 2, 0), k - 1) if k < self.sends else range(k - 2, k) if k == self.sends else ():
+        for sent in range(h) if k == h else range(h, self.sends) if k == self.sends else ():
             for way in (0, 1):
                 self.copy(slot, sent, way).wait_send()
         if k == self.sends + 1:
@@ -152,8 +154,7 @@
 
 
 SLOTS = 4
-EVERY = 6
-EARLY, SOONER = 2, 5
+EVERY = 3
 
 
 def train_kernel(n, x, dy, wg, wu, wd, sums, far0, far1, far2, far3, dgu, w_gu, w_d, a1, a2, at, dyv, dyt, h1, pulled, act, buf0, buf1,
@@ -181,11 +182,12 @@
 
     all_dy = pltpu.make_async_copy(dy, dyv, sem.at[tiles])
     state(0).start()
-    for i in (0, 1, 2):
-        for j in range(slices):
-            weights(0, j)[i].start()
-        if i == 1:
-            state(1).start()
+    for j in range(slices):
+        for c in weights(0, j)[:2]:
+            c.start()
+    state(1).start()
+    for j in range(slices):
+        weights(0, j)[2].start()
     all_dy.start()
     for m in range(2, tiles):
         state(m).start()
@@ -229,27 +231,29 @@
             c.wait()
     pl.semaphore_wait(barrier, 2)
 
-    def offset(k, every):
-        return 1 + every * k if k <= ring.sends else 5 + every * ring.sends
-
-    def events(now, m, odd):
-        for k in reversed(range(ring.sends + 2)):
-            cases = []
-            for every, low, high in ((SOONER, 0, EARLY), (EVERY, EARLY, total)):
-                ago, at_tile = divmod(offset(k, every), tiles)
-                place = now - 1 - ago
-                t = jnp.where(place > slices, place - 1, place)
-                if at_tile % 2 == odd:
-                    cases.append(((m == at_tile) & (place != slices) & (t >= low) & (t < high), t))
-            if cases:
-                here, t = cases[0]
-                for other, u in cases[1:]:
-                    t = jnp.where(other, u, t)
-                    here = here | other
-
-                @pl.when(here)
-                def _():
-                    ring.event(lax.rem(t, SLOTS), t, k)
+    steps = tiles // PAIR
+    turns = tiles // steps
+    offsets = [1 + EVERY * k for k in range(ring.sends + 1)] + [3 + EVERY * ring.sends]
+
+    def round_of(now):
+        found = []
+        for ago in range(1 + offsets[-1] // steps):
+            place = now - 1 - ago
+            t = jnp.where(place >= slices, place - turns, place)
+            there = (place >= 0) & (t < total) & ((place < slices) | (t >= slices))
+            found.append((there, t, lax.rem(t + SLOTS, SLOTS)))
+        return found
+
+    def events(found, u, odd=None):
+        for k in reversed(range(len(offsets))):
+            ago, at_step = divmod(offsets[k], steps)
+            if odd is not None and at_step % 2 != odd:
+                continue
+            there, t, slot = found[ago]
+
+            @pl.when((u == at_step) & there)
+            def _():
+                ring.event(slot, t, k)
 
     def finish(s):
         slot = lax.rem(s, SLOTS)
@@ -259,8 +263,10 @@
         acc_gu[...] = jnp.zeros_like(acc_gu)
         acc_d[...] = jnp.zeros_like(acc_d)
 
-    def push(m, j, i):
-        return pltpu.make_async_copy((buf0, buf1)[i].at[:, pl.ds(0, 2 * FS)], dgu.at[m, :, columns(j)], push_sem.at[i])
+    def push(u, j, i):
+        return pltpu.make_async_copy(
+            (buf0, buf1)[i].at[:, :, pl.ds(0, 2 * FS)], dgu.at[pl.ds(u * PAIR, PAIR), :, columns(j)], push_sem.at[i]
+        )
 
     def pull(m):
         return pltpu.make_async_copy(dgu.at[m], pulled.at[lax.rem(m, 2)], pull_sem.at[lax.rem(m, 2)])
@@ -269,28 +275,31 @@
         second = l == layers - 1
         states = a2 if second else a1
 
-        def slice_a(m, j, buf):
-            slice_first(states[m], dyv[m], w_gu[l, :, columns(j)], w_d[l, j], buf)
-
-        def slice_b(m, buf):
-            slice_second(at[m], dyt[m], buf, acc_gu, acc_d)
+        def slice_a(u, j, buf):
+            here = pl.ds(u * PAIR, PAIR)
+            rows = (PAIR * TM, dyv.shape[-1])
+            slice_first(states[here].reshape(rows), dyv[here].reshape(rows), w_gu[l, :, columns(j)], w_d[l, j], buf)
+
+        def slice_b(u, buf):
+            here = pl.ds(u * PAIR, PAIR)
+            slice_second(at.at[here], dyt.at[here], buf, acc_gu, acc_d)
 
         def one_slice(j, _):
-            now = j if second else slices + 1 + j
-
-            def pair(i, _):
+            found = round_of(j if second else slices + turns + j)
+
+            def two_steps(i, _):
                 for half, here, there in ((0, buf0, buf1), (1, buf1, buf0)):
-                    m = 2 * i + half
-                    events(now, m, half)
+                    u = 2 * i + half
+                    events(found, u, half)
                     if second:
                         @pl.when((i > 0) | (j > 0))
                         def _():
-                            push(m, j, half).wait()
-
-                    slice_a(m, j, here)
-                    slice_b(lax.rem(m + tiles - 1, tiles), there)
+                            push(u, j, half).wait()
+
+                    slice_a(u, j, here)
+                    slice_b(lax.rem(u + steps - 1, steps), there)
                     if second:
-                        push(m, j, half).start()
+                        push(u, j, half).start()
                     if half == 0:
                         @pl.when((i == 0) & (j > 0))
                         def _():
@@ -298,19 +307,18 @@
 
                 return 0
 
-            return lax.fori_loop(0, tiles // 2, pair, 0)
+            return lax.fori_loop(0, steps // 2, two_steps, 0)
 
         buf1[...] = jnp.zeros_like(buf1)
         lax.fori_loop(0, slices, one_slice, 0)
         if second:
             for m in (0, 1):
                 pull(m).start()
-        slice_b(tiles - 1, buf1)
+        slice_b(steps - 1, buf1)
         finish((slices if second else total) - 1)
 
     def turn(m, _):
-        for odd in (0, 1):
-            events(slices, m, odd)
+        events(round_of(slices + m // steps), lax.rem(m, steps))
         pull(m).wait()
         parts = 2
         size = TM // parts
@@ -337,15 +345,16 @@
     backward(0)
 
     def drain(now, _):
-        def pair(i, _):
-            for half in (0, 1):
-                events(now, 2 * i + half, half)
+        found = round_of(now)
+
+        def one(u, _):
+            events(found, u)
             return 0
 
-        return lax.fori_loop(0, tiles // 2, pair, 0)
-
-    end = total + 1
-    lax.fori_loop(end, end + 1 + offset(ring.sends + 1, EVERY) // tiles, drain, 0)
+        return lax.fori_loop(0, steps, one, 0)
+
+    end = total + turns
+    lax.fori_loop(end, end + 1 + offsets[-1] // steps, drain, 0)
 
 
 def adam_math(w, m, v, g):
@@ -395,7 +404,7 @@
         ),
         out_shape=[jax.ShapeDtypeStruct(a.shape, a.dtype) for a in arrays],
         input_output_aliases={1 + len(gs) + 9 + i: i for i in range(len(extra))},
-        compiler_params=pltpu.CompilerParams(vmem_limit_bytes=32_000_000),
+        compiler_params=pltpu.CompilerParams(vmem_limit_bytes=60_000_000),
         cost_estimate=pl.CostEstimate(flops=40 * size, bytes_accessed=size, transcendentals=0),
     )(where, *gs, *arrays, *extra)
 
@@ -430,8 +439,8 @@
                 pltpu.VMEM((tiles, TM, d), BF16),
                 pltpu.VMEM((2, TM, 2 * ff), BF16),
                 pltpu.VMEM((TM, ff), BF16),
-                pltpu.VMEM((TM, 3 * FS), BF16),
-                pltpu.VMEM((TM, 3 * FS), BF16),
+                pltpu.VMEM((PAIR, TM, 3 * FS), BF16),
+                pltpu.VMEM((PAIR, TM, 3 * FS), BF16),
                 pltpu.VMEM((d, 2 * FS), F32),
                 pltpu.VMEM((d, FS), F32),
                 pltpu.VMEM((SLOTS, n, rows, d), BF16),

time: 308 us -> 299 us (0.971)
  local copies, waits for them, and re-layouts: 9.2 us -> 1.94 us
    unnamed x8 -> x10, local copies, waits for them, and re-layouts: 9.2 us -> 1.94 us
    pallas_call x1, Pallas kernels: 234 us -> 228 us  [step(): pl.pallas_call(functools.partial(train_kernel, n), in_specs=[hbm] * 5, ou...]
    pallas_call x4, Pallas kernels: 41 us -> 45 us  [adam(): pl.pallas_call(functools.partial(adam_kernel, len(gs)), grid_spec=pltpu.P...]
  transfers between devices with their start and end apart: 6 -> 6, of which waited for: 1 -> 1; matrix products, arithmetic and copies ran while one was open for 0% -> 0% of each run, Pallas kernels for 12% -> 13%
where the time goes in v5:
time: 299 us
  Pallas kernels  273 us (91%)
  waiting for transfers between devices  12.9 us (4%)
  starting transfers between devices  9.73 us (3%)
    pallas_call x1, Pallas kernels, step(): pl.pallas_call(functools.partial(train_kernel, n), in_specs=[hbm] * 5, ou...  228 us
    pallas_call x4, Pallas kernels, adam(): pl.pallas_call(functools.partial(adam_kernel, len(gs)), grid_spec=pltpu.P...  45 us
    ppermute x4, waiting for transfers between devices, step(): near.append(lax.ppermute(far[i], 'dp', way))  12.9 us
    ppermute x4, starting transfers between devices, step(): near.append(lax.ppermute(far[i], 'dp', way))  6.14 us
  transfers between devices with their start and end apart: 6, of which 1 were waited for; matrix products, arithmetic and copies ran while one was open for 0% of the time, Pallas kernels for 13%

profile of v5, /device:TPU:22, one launch (start us, length us, event | category | flops | bytes accessed | tf_op | source)
XLA Modules:
  0.0 298.7 jit_solution(2819869377339195024)
XLA Ops:
  0.6 228.2 %shard_map.178 = (bf16[14,8,96,512]{3,2,1,0:T(8,128)(2,1)}, bf16[14,48,512]{2,1,0:T(8,128)(2,1)}, bf16[14,48,512]{2,1,0:T(8,128)(2,1)}, bf16[14,48,512]{2,1,0:T(...) custom-call(bf16[8,512,512]{2,1,0:T(8,128)(2,1)} %bitcast.66, bf16[8,512,512]{2,1,0:T(8,128)(2,1)} %bitcast.67, ...), custom_call_target="tpu_custom_call" | custom-call | flops 127775277056 | bytes 90000000 | tf_op jit(solution)/shard_map/pallas_call | solution.py:424
  228.9 2.9 collective-permute-start
  231.8 0.0 collective-permute-start.2
  231.8 3.2 %collective-permute-start.5 = (bf16[14,48,512]{2,1,0:T(8,128)(2,1)}, bf16[14,48,512]{2,1,0:T(8,128)(2,1)}, u32[]{:S(2)}, u32[]{:S(2)}) collective-permute-start(bf16[14,48,512]{2,1,0:T(8,128)(2,1)} %get-tuple-element.53), channel_id=1, source_target_pairs={{0,7},{1,0},{2,1},{3,2},{4,3},{5,4},{6,5},{7,6},{8,15},{9,8},{10,9... | collective-permute-start | bytes 2064392 | tf_op jit(solution)/shard_map/ppermute | solution.py:472
  235.0 0.0 collective-permute-start.4
  235.0 12.9 %collective-permute-done.refs_0_ = bf16[14,48,512]{2,1,0:T(8,128)(2,1)S(1)} collective-permute-done((bf16[14,48,512]{2,1,0:T(8,128)(2,1)}, bf16[14,48,512]{2,1,0:T(8,128)(2,1)S(1)}, u32[]{:S(2)}, u32[]{:S(2)}) %collective-permute-start) | collective-permute-done | bytes 688160 | tf_op jit(solution)/shard_map/ppermute | solution.py:472
  247.9 0.0 copy-start
  247.9 3.6 %collective-permute-start.1 = (bf16[14,48,512]{2,1,0:T(8,128)(2,1)S(1)}, bf16[14,48,512]{2,1,0:T(8,128)(2,1)S(1)}, u32[]{:S(2)}, u32[]{:S(2)}) collective-permute-start(bf16[14,48,512]{2,1,0:T(8,128)(2,1)S(1)} %collective-permute-done.refs_0_), channel_id=1, source_target_pairs={{0,7},{1,0},{2,1},{3,2},{4,3},{5,4},{6,5},{7,6},{8,15},{9,8},{10,9... | collective-permute-start | bytes 2064392 | tf_op jit(solution)/shard_map/ppermute | solution.py:476
  251.5 0.0 collective-permute-done.2.refs_1_
  251.5 0.0 copy-start.1
  251.5 0.0 collective-permute-start.3
  251.5 27.0 %shard_map.179 = (bf16[2,8,64,1792]{3,2,1,0:T(8,128)(2,1)}, bf16[2,8,64,1792]{3,2,1,0:T(8,128)(2,1)}, bf16[2,7,8,32,512]{4,3,2,1,0:T(8,128)(2,1)}, f32[2,8,64,17...) custom-call(s32[1]{0:T(128)} %bitcast.where, ...), custom_call_target="tpu_custom_call" | custom-call | flops 2752512000 | bytes 68812800 | tf_op jit(solution)/shard_map/pallas_call | solution.py:397
  278.5 0.0 copy-done
  278.6 0.0 copy-done.1
  278.6 0.0 collective-permute-done.5.refs_1_
  278.6 6.0 %shard_map.180 = (bf16[2,8,64,1792]{3,2,1,0:T(8,128)(2,1)}, bf16[2,8,64,1792]{3,2,1,0:T(8,128)(2,1)}, bf16[2,7,8,32,512]{4,3,2,1,0:T(8,128)(2,1)}, f32[2,8,64,17...) custom-call(s32[1]{0:T(128)} %bitcast.where, ...), custom_call_target="tpu_custom_call", output_to_operand_aliasing={{0}: (12, {}), {1}: (13, {}), {2}: (14, {}), {3}: (15, {}),... | custom-call | flops 550502400 | bytes 13762560 | tf_op jit(solution)/shard_map/pallas_call | solution.py:397
  284.6 0.0 collective-permute-done.4.refs_0_
  284.6 0.0 copy-start.4
  284.6 0.8 copy-done.4
  285.5 6.0 %shard_map.181 = (bf16[2,8,64,1792]{3,2,1,0:T(8,128)(2,1)}, bf16[2,8,64,1792]{3,2,1,0:T(8,128)(2,1)}, bf16[2,7,8,32,512]{4,3,2,1,0:T(8,128)(2,1)}, f32[2,8,64,17...) custom-call(s32[1]{0:T(128)} %bitcast.where, ...), custom_call_target="tpu_custom_call", output_to_operand_aliasing={{0}: (12, {}), {1}: (13, {}), {2}: (14, {}), {3}: (15, {}),... | custom-call | flops 550502400 | bytes 13762560 | tf_op jit(solution)/shard_map/pallas_call | solution.py:397
  291.5 0.0 collective-permute-done.1.refs_0_
  291.5 0.0 copy-start.2
  291.5 0.0 collective-permute-done.3.refs_1_
  291.5 0.0 copy-start.3
  291.5 0.8 copy-done.2
  292.3 0.3 copy-done.3
  292.6 6.0 %shard_map.182 = (bf16[2,8,64,1792]{3,2,1,0:T(8,128)(2,1)}, bf16[2,8,64,1792]{3,2,1,0:T(8,128)(2,1)}, bf16[2,7,8,32,512]{4,3,2,1,0:T(8,128)(2,1)}, f32[2,8,64,17...) custom-call(s32[1]{0:T(128)} %bitcast.where, ...), custom_call_target="tpu_custom_call", output_to_operand_aliasing={{0}: (12, {}), {1}: (13, {}), {2}: (14, {}), {3}: (15, {}),... | custom-call | flops 550502400 | bytes 13762560 | tf_op jit(solution)/shard_map/pallas_call | solution.py:397
Async XLA Ops:
  228.9 19.0 %collective-permute-start = (bf16[14,48,512]{2,1,0:T(8,128)(2,1)}, bf16[14,48,512]{2,1,0:T(8,128)(2,1)S(1)}, u32[]{:S(2)}, u32[]{:S(2)}) collective-permute-start(bf16[14,48,512]{2,1,0:T(8,128)(2,1)} %get-tuple-element.50), channel_id=1, source_target_pairs={{0,7},{1,0},{2,1},{3,2},{4,3},{5,4},{6,5},{7,6},{8,15},{9,8},{10,9... | collective-permute-start | bytes 2064392 | tf_op jit(solution)/shard_map/ppermute | solution.py:472
  231.8 19.7 %collective-permute-start.2 = (bf16[14,48,512]{2,1,0:T(8,128)(2,1)}, bf16[14,48,512]{2,1,0:T(8,128)(2,1)S(1)}, u32[]{:S(2)}, u32[]{:S(2)}) collective-permute-start(bf16[14,48,512]{2,1,0:T(8,128)(2,1)} %get-tuple-element.51), channel_id=1, source_target_pairs={{0,1},{1,2},{2,3},{3,4},{4,5},{5,6},{6,7},{7,0},{8,9},{9,10},{10,1... | collective-permute-start | bytes 2064392 | tf_op jit(solution)/shard_map/ppermute | solution.py:472
  231.8 46.8 %collective-permute-start.5 = (bf16[14,48,512]{2,1,0:T(8,128)(2,1)}, bf16[14,48,512]{2,1,0:T(8,128)(2,1)}, u32[]{:S(2)}, u32[]{:S(2)}) collective-permute-start(bf16[14,48,512]{2,1,0:T(8,128)(2,1)} %get-tuple-element.53), channel_id=1, source_target_pairs={{0,7},{1,0},{2,1},{3,2},{4,3},{5,4},{6,5},{7,6},{8,15},{9,8},{10,9... | collective-permute-start | bytes 2064392 | tf_op jit(solution)/shard_map/ppermute | solution.py:472
  235.0 49.6 %collective-permute-start.4 = (bf16[14,48,512]{2,1,0:T(8,128)(2,1)}, bf16[14,48,512]{2,1,0:T(8,128)(2,1)S(1)}, u32[]{:S(2)}, u32[]{:S(2)}) collective-permute-start(bf16[14,48,512]{2,1,0:T(8,128)(2,1)} %get-tuple-element.52), channel_id=1, source_target_pairs={{0,1},{1,2},{2,3},{3,4},{4,5},{5,6},{6,7},{7,0},{8,9},{9,10},{10,1... | collective-permute-start | bytes 2064392 | tf_op jit(solution)/shard_map/ppermute | solution.py:472
  247.9 30.6 %copy-start = (bf16[14,48,512]{2,1,0:T(8,128)(2,1)}, bf16[14,48,512]{2,1,0:T(8,128)(2,1)S(1)}, u32[]{:S(2)}) copy-start(bf16[14,48,512]{2,1,0:T(8,128)(2,1)S(1)} %collective-permute-done.refs_0_) | copy-start | bytes 2064388
  247.9 43.5 %collective-permute-start.1 = (bf16[14,48,512]{2,1,0:T(8,128)(2,1)S(1)}, bf16[14,48,512]{2,1,0:T(8,128)(2,1)S(1)}, u32[]{:S(2)}, u32[]{:S(2)}) collective-permute-start(bf16[14,48,512]{2,1,0:T(8,128)(2,1)S(1)} %collective-permute-done.refs_0_), channel_id=1, source_target_pairs={{0,7},{1,0},{2,1},{3,2},{4,3},{5,4},{6,5},{7,6},{8,15},{9,8},{10,9... | collective-permute-start | bytes 2064392 | tf_op jit(solution)/shard_map/ppermute | solution.py:476
  251.5 27.0 %copy-start.1 = (bf16[14,48,512]{2,1,0:T(8,128)(2,1)}, bf16[14,48,512]{2,1,0:T(8,128)(2,1)S(1)}, u32[]{:S(2)}) copy-start(bf16[14,48,512]{2,1,0:T(8,128)(2,1)S(1)} %collective-permute-done.2.refs_1_) | copy-start | bytes 2064388
  251.5 39.9 %collective-permute-start.3 = (bf16[14,48,512]{2,1,0:T(8,128)(2,1)S(1)}, bf16[14,48,512]{2,1,0:T(8,128)(2,1)S(1)}, u32[]{:S(2)}, u32[]{:S(2)}) collective-permute-start(bf16[14,48,512]{2,1,0:T(8,128)(2,1)S(1)} %collective-permute-done.2.refs_1_), channel_id=1, source_target_pairs={{0,1},{1,2},{2,3},{3,4},{4,5},{5,6},{6,7},{7,0},{8,9},{9,10},{10,1... | collective-permute-start | bytes 2064392 | tf_op jit(solution)/shard_map/ppermute | solution.py:476
  284.6 0.9 copy-start.4
  291.5 0.9 copy-start.2
  291.5 1.1 copy-start.3

commit v6 on v5

--- a/solution.py
+++ b/solution.py
@@ -81,12 +81,14 @@
 
 
 class Ring:
-    def __init__(self, n, own, got, out, sums, far, send, recv, out_sem):
+    def __init__(self, n, slices, own, got, out, sums, far, send, recv, out_sem, leaf_send, leaf_recv):
         self.n, self.half, self.rows = n, n // 2, own.shape[2]
         self.kept = self.half - 2
         self.sends = self.half + self.kept
+        self.slices = slices
         self.own, self.got, self.out, self.sums, self.far = own, got, out, sums, far
         self.send, self.recv, self.out_sem = send, recv, out_sem
+        self.leaf_send, self.leaf_recv = leaf_send, leaf_recv
         self.me = lax.axis_index("dp")
         self.to = ({"dp": lax.rem(self.me + n - 1, n)}, {"dp": lax.rem(self.me + 1, n)})
 
@@ -116,15 +118,34 @@
         )
 
     def write_out(self, slot, t):
+        chunks = [self.chunk(0, offset) for offset in range(-self.kept, self.kept + 1)]
+        return [
+            pltpu.make_async_copy(self.out.at[slot, chunk], self.sums.at[t, chunk], self.out_sem.at[slot, i])
+            for i, chunk in enumerate(chunks)
+        ]
+
+    def write_far(self, slot, t, first):
         copies = []
-        for offset in range(-self.kept, self.kept + 1):
-            chunk = self.chunk(0, offset)
-            copies.append((self.out.at[slot, chunk], self.sums.at[t, chunk]))
         for way in (0, 1):
             chunk = self.chunk(way, self.kept)
-            for part in (0, 1):
-                copies.append((self.out.at[slot, chunk, self.part(part, True)], self.far[2 * way + part].at[t]))
-        return [pltpu.make_async_copy(a, b, self.out_sem.at[slot, i]) for i, (a, b) in enumerate(copies)]
+            for place, part in ((0, way), (1, 1 - way)) if first else ((2, 1 - way),):
+                to = self.far[way].at[place, t - self.slices if first else t]
+                copies.append((self.out.at[slot, chunk, self.part(part, True)], to))
+        i = 2 * self.kept + 1
+        return [pltpu.make_async_copy(a, b, self.out_sem.at[slot, i + j]) for j, (a, b) in enumerate(copies)]
+
+    def leaf(self, slot, t):
+        return [
+            pltpu.make_async_remote_copy(
+                src_ref=self.out.at[slot, self.chunk(way, self.kept), self.part(way, True)],
+                dst_ref=self.far[way].at[3, t],
+                send_sem=self.leaf_send.at[slot, way],
+                recv_sem=self.leaf_recv.at[slot, way],
+                device_id=self.to[way],
+                device_id_type=pl.DeviceIdType.MESH,
+            )
+            for way in (0, 1)
+        ]
 
     def event(self, slot, t, k):
         h = self.half
@@ -142,28 +163,37 @@
         if k < self.sends:
             for way in (0, 1):
                 self.copy(slot, k, way).start()
-        if k == self.sends:
+        if k >= self.sends:
+            start = k == self.sends
+
+            @pl.when(t < self.slices)
+            def _():
+                for copy in self.leaf(slot, t) + self.write_far(slot, t, False):
+                    copy.start() if start else copy.wait()
+
+            @pl.when(t >= self.slices)
+            def _():
+                for copy in self.write_far(slot, t, True):
+                    copy.start() if start else copy.wait()
+
             for copy in self.write_out(slot, t):
-                copy.start()
+                copy.start() if start else copy.wait()
         for sent in range(h) if k == h else range(h, self.sends) if k == self.sends else ():
             for way in (0, 1):
                 self.copy(slot, sent, way).wait_send()
-        if k == self.sends + 1:
-            for copy in self.write_out(slot, t):
-                copy.wait()
 
 
 SLOTS = 4
 EVERY = 3
 
 
-def train_kernel(n, x, dy, wg, wu, wd, sums, far0, far1, far2, far3, dgu, w_gu, w_d, a1, a2, at, dyv, dyt, h1, pulled, act, buf0, buf1,
-                 acc_gu, acc_d, own, got, out, sem, wsem, push_sem, pull_sem, send, recv, out_sem):
+def train_kernel(n, x, dy, wg, wu, wd, sums, far0, far1, dgu, w_gu, w_d, a1, a2, at, dyv, dyt, h1, pulled, act, buf0, buf1,
+                 acc_gu, acc_d, own, got, out, sem, wsem, push_sem, pull_sem, send, recv, out_sem, leaf_send, leaf_recv):
     layers, slices = w_d.shape[:2]
     tiles = x.shape[0]
     total = layers * slices
     barrier = pltpu.get_barrier_semaphore()
-    ring = Ring(n, own, got, out, sums, (far0, far1, far2, far3), send, recv, out_sem)
+    ring = Ring(n, slices, own, got, out, sums, (far0, far1), send, recv, out_sem, leaf_send, leaf_recv)
     for device in ring.to:
         pl.semaphore_signal(barrier, inc=1, device_id=device, device_id_type=pl.DeviceIdType.MESH)
 
@@ -257,9 +287,13 @@
 
     def finish(s):
         slot = lax.rem(s, SLOTS)
-        wide = acc_gu.shape[0] // n
-        own[slot, :, :wide] = acc_gu[...].astype(BF16).reshape(n, wide, 2 * FS)
-        own[slot, :, wide:] = acc_d[...].T.astype(BF16).reshape(n, FS // n, -1)
+        wide, tall = acc_gu.shape[0] // n // 2, FS // n // 2
+        gu = acc_gu[...].astype(BF16).reshape(n, 2, wide, 2 * FS)
+        down = acc_d[...].T.astype(BF16).reshape(n, 2, tall, acc_d.shape[0])
+        for half in (0, 1):
+            start = half * (wide + tall)
+            own[slot, :, start : start + wide] = gu[:, half]
+            own[slot, :, start + wide : start + wide + tall] = down[:, half]
         acc_gu[...] = jnp.zeros_like(acc_gu)
         acc_d[...] = jnp.zeros_like(acc_d)
 
@@ -364,13 +398,15 @@
     return (w - 0.02 * step).astype(BF16), m, v
 
 
-def adam_kernel(halves, where, *refs):
-    gs, ins, outs = refs[:halves], refs[halves : halves + 9], refs[-9:]
-    slices = gs[0].shape[0]
-    wide = ins[0].shape[2]
+def adam_kernel(sources, table, me, *refs):
+    gs, ins, outs = refs[:sources], refs[sources : sources + 9], refs[-9:]
+    source = table[pl.program_id(0), 3]
+    slices, wide = ins[2].shape[1], ins[0].shape[2]
     for j in range(slices):
-        g = [r[j].reshape(r.shape[-2:]) for r in gs]
-        g = (g[0] if halves == 1 else jnp.concatenate(g, axis=0)).astype(F32)
+        g = None
+        for i, ref in enumerate(gs):
+            here = (ref[j, 0] if ref.shape[0] == slices else ref[0, j]).astype(F32)
+            g = here if g is None else jnp.where(source == i, here, g)
         columns = slice(j * FS, (j + 1) * FS)
         for i, here in ((0, (0, 0, slice(None), columns)), (1, (0, 0, slice(None), columns)), (2, (0, j, 0))):
             part = (g[:wide, :FS], g[:wide, FS:], g[wide:])[i]
@@ -380,33 +416,52 @@
                 outs[k * 3 + i][here] = new[k]
 
 
-def adam(n, offsets, gs, g_spec, arrays, so_far):
-    layers = arrays[0].shape[0]
-    slices = arrays[2].shape[1]
+def adam(n, steps, gs, arrays, so_far, vmem):
+    layers, slices = arrays[0].shape[0], arrays[2].shape[1]
+    rows, d = gs[0].shape[-2:]
+    half_rows = rows if gs[0].shape[1] == slices else rows // 2
+    blocks = [0] * len(gs)
+    table = []
+    for layer, offset, half, source, block in steps:
+        blocks[source] = block
+        table.append([layer, offset + n, half, source] + blocks)
+    table = jnp.array(table, jnp.int32)
+    me = lax.axis_index("dp").astype(jnp.int32).reshape(1)
+
+    def chunk(s, table, me):
+        return lax.rem(me[0] + table[s, 1], n)
+
+    def source(i, g):
+        if g.shape[1] == slices:
+            return pl.BlockSpec((1, slices, half_rows, d), lambda s, table, me: (table[s, 4 + i], 0, 0, 0))
+
+        def whole(s, table, me):
+            return layers - 1 - table[s, 0], lax.rem(me[0] + table[s, 4 + i], n), table[s, 2], 0
+
+        return pl.BlockSpec((slices, 1, half_rows, d), whole)
+
+    wide = pl.BlockSpec(
+        (1, 1, arrays[0].shape[2] // 2, arrays[0].shape[3]), lambda s, table, me: (table[s, 0], chunk(s, table, me), table[s, 2], 0)
+    )
+    tall = pl.BlockSpec(
+        (1, slices, 1, arrays[2].shape[3] // 2, d), lambda s, table, me: (table[s, 0], 0, chunk(s, table, me), table[s, 2], 0)
+    )
+    specs = [wide, wide, tall] * 3
     extra = [] if so_far is None else list(so_far)
-    where = lax.axis_index("dp").astype(jnp.int32).reshape(1)
-    step = offsets[1] - offsets[0] if len(offsets) > 1 else 1
-
-    def chunk(o, where):
-        return lax.rem(where[0] + o * step + (offsets[0] + n), n)
-
-    wide = pl.BlockSpec((1, 1) + arrays[0].shape[2:], lambda l, o, where: (l, chunk(o, where), 0, 0))
-    tall = pl.BlockSpec((1, slices, 1) + arrays[2].shape[3:], lambda l, o, where: (l, 0, chunk(o, where), 0, 0))
-    specs = [wide, wide, tall] * 3
-    size = sum(a.size * a.dtype.itemsize for a in arrays) * 2 * len(offsets) // n
+    size = sum(a.size * a.dtype.itemsize for a in arrays) * len(steps) // (n * layers)
     return pl.pallas_call(
         functools.partial(adam_kernel, len(gs)),
         grid_spec=pltpu.PrefetchScalarGridSpec(
-            num_scalar_prefetch=1,
-            grid=(layers, len(offsets)),
-            in_specs=[g_spec(chunk)] * len(gs) + specs + [pl.BlockSpec(memory_space=pl.ANY)] * len(extra),
+            num_scalar_prefetch=2,
+            grid=(len(steps),),
+            in_specs=[source(i, g) for i, g in enumerate(gs)] + specs + [pl.BlockSpec(memory_space=pl.ANY)] * len(extra),
             out_specs=specs,
         ),
         out_shape=[jax.ShapeDtypeStruct(a.shape, a.dtype) for a in arrays],
-        input_output_aliases={1 + len(gs) + 9 + i: i for i in range(len(extra))},
-        compiler_params=pltpu.CompilerParams(vmem_limit_bytes=60_000_000),
+        input_output_aliases={2 + len(gs) + 9 + i: i for i in range(len(extra))},
+        compiler_params=pltpu.CompilerParams(vmem_limit_bytes=vmem),
         cost_estimate=pl.CostEstimate(flops=40 * size, bytes_accessed=size, transcendentals=0),
-    )(where, *gs, *arrays, *extra)
+    )(table, me, *gs, *arrays, *extra)
 
 
 def solution(mesh):
@@ -424,9 +479,9 @@
         sums, *far, _ = pl.pallas_call(
             functools.partial(train_kernel, n),
             in_specs=[hbm] * 5,
-            out_specs=[hbm] * 6,
+            out_specs=[hbm] * 4,
             out_shape=[jax.ShapeDtypeStruct((layers * slices, n, rows, d), BF16)]
-            + [jax.ShapeDtypeStruct((layers * slices, rows // 2, d), BF16)] * 4
+            + [jax.ShapeDtypeStruct((4, slices, rows // 2, d), BF16)] * 2
             + [jax.ShapeDtypeStruct((tiles, TM, 2 * ff), BF16)],
             scratch_shapes=[
                 pltpu.VMEM((layers, d, 2 * ff), BF16),
@@ -453,30 +508,32 @@
                 pltpu.SemaphoreType.DMA((SLOTS, 2 * half - 2, 2)),
                 pltpu.SemaphoreType.DMA((SLOTS, 2 * half - 2, 2)),
                 pltpu.SemaphoreType.DMA((SLOTS, n + 1)),
+                pltpu.SemaphoreType.DMA((SLOTS, 2)),
+                pltpu.SemaphoreType.DMA((SLOTS, 2)),
             ],
             compiler_params=pltpu.CompilerParams(vmem_limit_bytes=VMEM_LIMIT, collective_id=0, has_side_effects=True),
             cost_estimate=pl.CostEstimate(flops=17 * mm, bytes_accessed=90 * 10**6, transcendentals=0),
         )(x, dy, wg, wu, wd)
         chunks = [a.reshape(layers, n, d // n, ff) if a.shape[1] == d else a.reshape(layers, slices, n, FS // n, d) for a in arrays]
-        left = [(i, (i + n - 1) % n) for i in range(n)]
-        right = [(i, (i + 1) % n) for i in range(n)]
-
-        def whole(chunk):
-            return pl.BlockSpec((slices, 1, rows, d), lambda l, o, where: (layers - 1 - l, chunk(o, where), 0, 0))
-
-        def halves(chunk):
-            return pl.BlockSpec((slices, rows // 2, d), lambda l, o, where: (layers - 1 - l, 0, 0))
-
-        near = []
-        for i, way in enumerate((left, left, right, right)):
-            near.append(lax.ppermute(far[i], "dp", way))
-        new = adam(n, tuple(range(2 - half, half - 1)), [sums], whole, chunks, None)
-        last = []
-        for i, way in ((0, left), (3, right)):
-            last.append(lax.ppermute(near[i], "dp", way))
-        new = adam(n, (half - 1,), near[:2], halves, chunks, new)
-        new = adam(n, (1 - half,), near[2:], halves, chunks, new)
-        new = adam(n, (half,), last, halves, chunks, new)
+        ways = ([(i, (i + n - 1) % n) for i in range(n)], [(i, (i + 1) % n) for i in range(n)])
+        first, second = range(layers)
+        kept = half - 2
+        here = {
+            l: [(l, offset, part, 0, offset + n) for offset in range(-kept, kept + 1) for part in (0, 1)] for l in (first, second)
+        }
+        near, last = [], []
+        for way in (0, 1):
+            near.append(lax.ppermute(far[way], "dp", ways[way]))
+        steps = here[second] + [(second, kept + 1, 0, 1, 3), (second, -kept - 1, 1, 2, 3)] + here[first]
+        new = adam(n, steps, [sums, *far], chunks, None, 60_000_000)
+        for way in (0, 1):
+            last.append(lax.ppermute(near[way][0], "dp", ways[way]))
+        steps = []
+        for way, sign in ((0, 1), (1, -1)):
+            steps += [(first, sign * (kept + 1), way, way, 0), (first, sign * (kept + 1), 1 - way, way, 1)]
+            steps += [(second, sign * (kept + 1), 1 - way, way, 2), (second, sign * half, way, way, 3)]
+        new = adam(n, steps, near, chunks, new, 52_000_000)
+        new = adam(n, [(first, half, 0, 0, 0), (first, -half, 1, 1, 0)], [a[None] for a in last], chunks, new, 60_000_000)
         return tuple(o.reshape(a.shape) for o, a in zip(new, arrays))
 
     return jax.shard_map(

time: 299 us -> 322 us (1.077)
  the two profiles are of different devices: /device:TPU:22 before, /device:TPU:21 now
where the time goes in v6:
time: 322 us; the launch traced here: 317 us
  Pallas kernels  284 us (88%)
  waiting for transfers between devices  27.2 us (8%)
  starting transfers between devices  4.63 us (1%)
    pallas_call x1, Pallas kernels, step(): pl.pallas_call(functools.partial(train_kernel, n), in_specs=[hbm] * 5, ou...  232 us
    pallas_call x3, Pallas kernels, adam(): pl.pallas_call(functools.partial(adam_kernel, len(gs)), grid_spec=pltpu.P...  51.9 us
    ppermute x2, waiting for transfers between devices, step(): near.append(lax.ppermute(far[way], 'dp', ways[way]))  27.2 us
  transfers between devices with their start and end apart: 4, of which 1 were waited for; matrix products, arithmetic and copies ran while one was open for 0% of the time, Pallas kernels for 15%

profile of v6, /device:TPU:21, one launch (start us, length us, event | category | flops | bytes accessed | tf_op | source)
XLA Modules:
  0.0 317.5 jit_solution(15664152971084877634)
XLA Ops:
  0.6 232.0 %shard_map.205 = (bf16[14,8,96,512]{3,2,1,0:T(8,128)(2,1)}, bf16[4,7,48,512]{3,2,1,0:T(8,128)(2,1)}, bf16[4,7,48,512]{3,2,1,0:T(8,128)(2,1)}, bf16[8,512,3584]{2,1,0:T(8,128)(2,1)}) custom-call(bf16[8,512,512]{2,1,0:T(8,128)(2,1)} %bitcast.65, bf16[8,512,512]{2,1,0:T(8,128)(2,1)} %bitcast.66, bf16[2,512,1792]{2,1,0:T(8,128)(2,1)} %wg.1, ...), custom_call_target="tpu_custom_call" | custom-call | flops 127775277056 | bytes 90000000 | tf_op jit(solution)/shard_map/pallas_call | solution.py:479
  232.6 2.0 collective-permute-start
  234.7 0.0 collective-permute-start.2
  234.7 27.2 %collective-permute-done.refs_0_ = bf16[4,7,48,512]{3,2,1,0:T(8,128)(2,1)S(1)} collective-permute-done((bf16[4,7,48,512]{3,2,1,0:T(8,128)(2,1)}, bf16[4,7,48,512]{3,2,1,0:T(8,128)(2,1)S(1)}, u32[]{:S(2)}, u32[]{:S(2)}) %collective-permute-start) | collective-permute-done | bytes 1376288 | tf_op jit(solution)/shard_map/ppermute | solution.py:526
  261.9 2.5 collective-permute-start.1
  264.4 0.0 collective-permute-done.2.refs_1_
  264.4 0.1 collective-permute-start.3
  264.6 0.0 copy-start
  264.6 32.9 %shard_map.206 = (bf16[2,8,64,1792]{3,2,1,0:T(8,128)(2,1)}, bf16[2,8,64,1792]{3,2,1,0:T(8,128)(2,1)}, bf16[2,7,8,32,512]{4,3,2,1,0:T(8,128)(2,1)}, f32[2,8,64,17...) custom-call(s32[22,7]{1,0:T(8,128)} %constant.10.clone.table, ...), custom_call_target="tpu_custom_call" | custom-call | flops 3027763200 | bytes 75694080 | tf_op jit(solution)/shard_map/pallas_call | solution.py:452
  297.4 0.0 copy-done
  297.5 13.8 %shard_map.207 = (bf16[2,8,64,1792]{3,2,1,0:T(8,128)(2,1)}, bf16[2,8,64,1792]{3,2,1,0:T(8,128)(2,1)}, bf16[2,7,8,32,512]{4,3,2,1,0:T(8,128)(2,1)}, f32[2,8,64,17...) custom-call(s32[8,6]{1,0:T(8,128)S(1)} %copy-done, ...), custom_call_target="tpu_custom_call", output_to_operand_aliasing={{0}: (13, {}), {1}: (14, {}), {2}: (15, {}), {3}: (16, {}),... | custom-call | flops 1101004800 | bytes 27525120 | tf_op jit(solution)/shard_map/pallas_call | solution.py:452
  311.3 0.0 collective-permute-done.1
  311.3 0.0 copy-start.1
  311.3 0.0 collective-permute-done.3
  311.3 0.0 copy-start.2
  311.3 0.7 copy-done.1
  312.0 0.1 copy-done.2
  312.1 5.2 %shard_map.208 = (bf16[2,8,64,1792]{3,2,1,0:T(8,128)(2,1)}, bf16[2,8,64,1792]{3,2,1,0:T(8,128)(2,1)}, bf16[2,7,8,32,512]{4,3,2,1,0:T(8,128)(2,1)}, f32[2,8,64,17...) custom-call(s32[2,6]{1,0:T(2,128)} %constant.12.clone.table, ...), custom_call_target="tpu_custom_call", output_to_operand_aliasing={{0}: (13, {}), {1}: (14, {}), {2}: (15, {}), {3}: (16, {}),... | custom-call | flops 275251200 | bytes 6881280 | tf_op jit(solution)/shard_map/pallas_call | solution.py:452
  (2 shorter events, 0.0 us)
Async XLA Ops:
  232.6 29.3 %collective-permute-start = (bf16[4,7,48,512]{3,2,1,0:T(8,128)(2,1)}, bf16[4,7,48,512]{3,2,1,0:T(8,128)(2,1)S(1)}, u32[]{:S(2)}, u32[]{:S(2)}) collective-permute-start(bf16[4,7,48,512]{3,2,1,0:T(8,128)(2,1)} %get-tuple-element.39.refs_1_), channel_id=1, source_target_pairs={{0,7},{1,0},{2,1},{3,2},{4,3},{5,4},{6,5},{7,6},{8,15},{9,8},{10,9... | collective-permute-start | bytes 4128776 | tf_op jit(solution)/shard_map/ppermute | solution.py:526
  234.7 29.8 %collective-permute-start.2 = (bf16[4,7,48,512]{3,2,1,0:T(8,128)(2,1)}, bf16[4,7,48,512]{3,2,1,0:T(8,128)(2,1)S(1)}, u32[]{:S(2)}, u32[]{:S(2)}) collective-permute-start(bf16[4,7,48,512]{3,2,1,0:T(8,128)(2,1)} %get-tuple-element.40.refs_2_), channel_id=1, source_target_pairs={{0,1},{1,2},{2,3},{3,4},{4,5},{5,6},{6,7},{7,0},{8,9},{9,10},{10,1... | collective-permute-start | bytes 4128776 | tf_op jit(solution)/shard_map/ppermute | solution.py:526
  261.9 49.4 %collective-permute-start.1 = (bf16[7,48,512]{2,1,0:T(8,128)(2,1)S(1)}, bf16[7,48,512]{2,1,0:T(8,128)(2,1)S(1)}, u32[]{:S(2)}, u32[]{:S(2)}) collective-permute-start(bf16[7,48,512]{2,1,0:T(8,128)(2,1)S(1)} %slice_bitcast_fusion.1), channel_id=1, source_target_pairs={{0,7},{1,0},{2,1},{3,2},{4,3},{5,4},{6,5},{7,6},{8,15},{9,8},{10,9... | collective-permute-start | bytes 1032200 | tf_op jit(solution)/shard_map/ppermute | solution.py:530
  264.4 46.9 %collective-permute-start.3 = (bf16[7,48,512]{2,1,0:T(8,128)(2,1)S(1)}, bf16[7,48,512]{2,1,0:T(8,128)(2,1)S(1)}, u32[]{:S(2)}, u32[]{:S(2)}) collective-permute-start(bf16[7,48,512]{2,1,0:T(8,128)(2,1)S(1)} %slice_bitcast_fusion), channel_id=1, source_target_pairs={{0,1},{1,2},{2,3},{3,4},{4,5},{5,6},{6,7},{7,0},{8,9},{9,10},{10,1... | collective-permute-start | bytes 1032200 | tf_op jit(solution)/shard_map/ppermute | solution.py:530
  264.6 32.9 %copy-start = (s32[8,6]{1,0:T(8,128)S(1)}, s32[8,6]{1,0:T(8,128)}, u32[]{:S(2)}) copy-start(s32[8,6]{1,0:T(8,128)} %constant.11.clone.table) | copy-start | bytes 580
  311.3 0.7 copy-start.1
  311.3 0.8 copy-start.2

commit v7 on v5

--- a/solution.py
+++ b/solution.py
@@ -180,7 +180,9 @@
     def state(m):
         return pltpu.make_async_copy(x.at[m], h1.at[m], sem.at[m])
 
-    all_dy = pltpu.make_async_copy(dy, dyv, sem.at[tiles])
+    def cotangent(m):
+        return pltpu.make_async_copy(dy.at[m], dyv.at[m], sem.at[tiles + m])
+
     state(0).start()
     for j in range(slices):
         for c in weights(0, j)[:2]:
@@ -188,9 +190,11 @@
     state(1).start()
     for j in range(slices):
         weights(0, j)[2].start()
-    all_dy.start()
+    cotangent(0).start()
     for m in range(2, tiles):
         state(m).start()
+        cotangent(m - 1).start()
+    cotangent(tiles - 1).start()
     for j in range(slices):
         for c in weights(1, j):
             c.start()
@@ -208,6 +212,7 @@
 
     def forward(m, _):
         state(m + 1).wait()
+        cotangent(m).wait()
         forward_b(m)
         forward_a(m + 1)
         return 0
@@ -223,8 +228,8 @@
     forward_a(0, ready)
     for j in range(slices):
         weights(0, j)[2].wait()
-    all_dy.wait()
     lax.fori_loop(0, tiles - 1, forward, 0)
+    cotangent(tiles - 1).wait()
     forward_b(tiles - 1)
     for j in range(slices):
         for c in weights(1, j):
@@ -364,13 +369,18 @@
     return (w - 0.02 * step).astype(BF16), m, v
 
 
-def adam_kernel(halves, where, *refs):
-    gs, ins, outs = refs[:halves], refs[halves : halves + 9], refs[-9:]
-    slices = gs[0].shape[0]
-    wide = ins[0].shape[2]
+def adam_kernel(sources, table, me, *refs):
+    count = sum(sources)
+    gs, ins, outs = list(refs[:count]), refs[count : count + 9], refs[-9:]
+    which = table[pl.program_id(0), 2]
+    slices, wide = ins[2].shape[1], ins[0].shape[2]
     for j in range(slices):
-        g = [r[j].reshape(r.shape[-2:]) for r in gs]
-        g = (g[0] if halves == 1 else jnp.concatenate(g, axis=0)).astype(F32)
+        g, place = None, 0
+        for i, pieces in enumerate(sources):
+            here = [r[j].reshape(r.shape[-2:]) for r in gs[place : place + pieces]]
+            here = (here[0] if pieces == 1 else jnp.concatenate(here, axis=0)).astype(F32)
+            g = here if g is None else jnp.where(which == i, here, g)
+            place += pieces
         columns = slice(j * FS, (j + 1) * FS)
         for i, here in ((0, (0, 0, slice(None), columns)), (1, (0, 0, slice(None), columns)), (2, (0, j, 0))):
             part = (g[:wide, :FS], g[:wide, FS:], g[wide:])[i]
@@ -380,33 +390,45 @@
                 outs[k * 3 + i][here] = new[k]
 
 
-def adam(n, offsets, gs, g_spec, arrays, so_far):
-    layers = arrays[0].shape[0]
-    slices = arrays[2].shape[1]
+def adam(n, steps, sources, arrays, so_far, vmem):
+    layers, slices = arrays[0].shape[0], arrays[2].shape[1]
+    blocks = [layers - 1 - steps[0][0]] * len(sources)
+    table = []
+    for layer, offset, source in steps:
+        blocks[source] = layers - 1 - layer
+        table.append([layer, offset + n, source] + blocks)
+    table = jnp.array(table, jnp.int32)
+    me = lax.axis_index("dp").astype(jnp.int32).reshape(1)
+
+    def chunk(s, table, me):
+        return lax.rem(me[0] + table[s, 1], n)
+
+    def spec(i, g):
+        if g.ndim == 3:
+            return pl.BlockSpec((slices,) + g.shape[1:], lambda s, table, me: (table[s, 3 + i], 0, 0))
+        return pl.BlockSpec((slices, 1) + g.shape[2:], lambda s, table, me: (table[s, 3 + i], chunk(s, table, me), 0, 0))
+
+    wide = pl.BlockSpec((1, 1) + arrays[0].shape[2:], lambda s, table, me: (table[s, 0], chunk(s, table, me), 0, 0))
+    tall = pl.BlockSpec((1, slices, 1) + arrays[2].shape[3:], lambda s, table, me: (table[s, 0], 0, chunk(s, table, me), 0, 0))
+    specs = [wide, wide, tall] * 3
+    gs = [g for source in sources for g in source]
     extra = [] if so_far is None else list(so_far)
-    where = lax.axis_index("dp").astype(jnp.int32).reshape(1)
-    step = offsets[1] - offsets[0] if len(offsets) > 1 else 1
-
-    def chunk(o, where):
-        return lax.rem(where[0] + o * step + (offsets[0] + n), n)
-
-    wide = pl.BlockSpec((1, 1) + arrays[0].shape[2:], lambda l, o, where: (l, chunk(o, where), 0, 0))
-    tall = pl.BlockSpec((1, slices, 1) + arrays[2].shape[3:], lambda l, o, where: (l, 0, chunk(o, where), 0, 0))
-    specs = [wide, wide, tall] * 3
-    size = sum(a.size * a.dtype.itemsize for a in arrays) * 2 * len(offsets) // n
+    size = 2 * sum(a.size * a.dtype.itemsize for a in arrays) * len(steps) // (n * layers)
     return pl.pallas_call(
-        functools.partial(adam_kernel, len(gs)),
+        functools.partial(adam_kernel, [len(source) for source in sources]),
         grid_spec=pltpu.PrefetchScalarGridSpec(
-            num_scalar_prefetch=1,
-            grid=(layers, len(offsets)),
-            in_specs=[g_spec(chunk)] * len(gs) + specs + [pl.BlockSpec(memory_space=pl.ANY)] * len(extra),
+            num_scalar_prefetch=2,
+            grid=(len(steps),),
+            in_specs=[spec(i, g) for i, source in enumerate(sources) for g in source]
+            + specs
+            + [pl.BlockSpec(memory_space=pl.ANY)] * len(extra),
             out_specs=specs,
         ),
         out_shape=[jax.ShapeDtypeStruct(a.shape, a.dtype) for a in arrays],
-        input_output_aliases={1 + len(gs) + 9 + i: i for i in range(len(extra))},
-        compiler_params=pltpu.CompilerParams(vmem_limit_bytes=60_000_000),
+        input_output_aliases={2 + len(gs) + 9 + i: i for i in range(len(extra))},
+        compiler_params=pltpu.CompilerParams(vmem_limit_bytes=vmem),
         cost_estimate=pl.CostEstimate(flops=40 * size, bytes_accessed=size, transcendentals=0),
-    )(where, *gs, *arrays, *extra)
+    )(table, me, *gs, *arrays, *extra)
 
 
 def solution(mesh):
@@ -446,7 +468,7 @@
                 pltpu.VMEM((SLOTS, n, rows, d), BF16),
                 pltpu.VMEM((SLOTS, half, 2, rows, d), BF16),
                 pltpu.VMEM((SLOTS, n, rows, d), BF16),
-                pltpu.SemaphoreType.DMA((tiles + 1,)),
+                pltpu.SemaphoreType.DMA((2 * tiles,)),
                 pltpu.SemaphoreType.DMA((layers, slices, 3)),
                 pltpu.SemaphoreType.DMA((2,)),
                 pltpu.SemaphoreType.DMA((2,)),
@@ -461,22 +483,19 @@
         left = [(i, (i + n - 1) % n) for i in range(n)]
         right = [(i, (i + 1) % n) for i in range(n)]
 
-        def whole(chunk):
-            return pl.BlockSpec((slices, 1, rows, d), lambda l, o, where: (layers - 1 - l, chunk(o, where), 0, 0))
-
-        def halves(chunk):
-            return pl.BlockSpec((slices, rows // 2, d), lambda l, o, where: (layers - 1 - l, 0, 0))
-
-        near = []
-        for i, way in enumerate((left, left, right, right)):
-            near.append(lax.ppermute(far[i], "dp", way))
-        new = adam(n, tuple(range(2 - half, half - 1)), [sums], whole, chunks, None)
-        last = []
+        first, second = range(layers)
+        kept = half - 2
+        big, small = 60_000_000, 52_000_000
+        near, last = [None] * 4, []
+        for i, way in ((0, left), (3, right), (1, left), (2, right)):
+            near[i] = lax.ppermute(far[i], "dp", way)
+        new = adam(n, [(second, o, 0) for o in range(-kept, kept + 1)], [[sums]], chunks, None, big)
         for i, way in ((0, left), (3, right)):
             last.append(lax.ppermute(near[i], "dp", way))
-        new = adam(n, (half - 1,), near[:2], halves, chunks, new)
-        new = adam(n, (1 - half,), near[2:], halves, chunks, new)
-        new = adam(n, (half,), last, halves, chunks, new)
+        new = adam(n, [(first, o, 0) for o in range(-kept, kept + 1)], [[sums]], chunks, new, big)
+        steps = [(l, sign * (kept + 1), way) for way, sign in ((0, 1), (1, -1)) for l in (second, first)]
+        new = adam(n, steps, [near[:2], near[2:]], chunks, new, small)
+        new = adam(n, [(second, half, 0), (first, half, 0)], [last], chunks, new, big)
         return tuple(o.reshape(a.shape) for o, a in zip(new, arrays))
 
     return jax.shard_map(

time: 299 us -> 304 us (1.017)
  Pallas kernels: 273 us -> 279 us
    pallas_call x4, Pallas kernels: 45 us -> 51.3 us  [adam(): pl.pallas_call(functools.partial(adam_kernel, [len(source) for source in...]
  transfers between devices with their start and end apart: 6 -> 6, of which waited for: 1 -> 1; matrix products, arithmetic and copies ran while one was open for 0% -> 0% of each run, Pallas kernels for 13% -> 15%
where the time goes in v7:
time: 304 us
  Pallas kernels  279 us (92%)
  waiting for transfers between devices  12.9 us (4%)
  starting transfers between devices  9.73 us (3%)
    pallas_call x1, Pallas kernels, step(): pl.pallas_call(functools.partial(train_kernel, n), in_specs=[hbm] * 5, ou...  228 us
    pallas_call x4, Pallas kernels, adam(): pl.pallas_call(functools.partial(adam_kernel, [len(source) for source in...  51.3 us
    ppermute x4, waiting for transfers between devices, step(): near[i] = lax.ppermute(far[i], 'dp', way)  12.9 us
    ppermute x4, starting transfers between devices, step(): near[i] = lax.ppermute(far[i], 'dp', way)  6.14 us
  transfers between devices with their start and end apart: 6, of which 1 were waited for; matrix products, arithmetic and copies ran while one was open for 0% of the time, Pallas kernels for 15%

profile of v7, /device:TPU:22, one launch (start us, length us, event | category | flops | bytes accessed | tf_op | source)
XLA Modules:
  0.0 303.5 jit_solution(4387229432227542318)
XLA Ops:
  0.6 227.8 %shard_map.214 = (bf16[14,8,96,512]{3,2,1,0:T(8,128)(2,1)}, bf16[14,48,512]{2,1,0:T(8,128)(2,1)}, bf16[14,48,512]{2,1,0:T(8,128)(2,1)}, bf16[14,48,512]{2,1,0:T(...) custom-call(bf16[8,512,512]{2,1,0:T(8,128)(2,1)} %bitcast.66, bf16[8,512,512]{2,1,0:T(8,128)(2,1)} %bitcast.67, ...), custom_call_target="tpu_custom_call" | custom-call | flops 127775277056 | bytes 90000000 | tf_op jit(solution)/shard_map/pallas_call | solution.py:446
  228.4 2.9 collective-permute-start
  231.3 0.0 collective-permute-start.2
  231.3 3.2 %collective-permute-start.4 = (bf16[14,48,512]{2,1,0:T(8,128)(2,1)}, bf16[14,48,512]{2,1,0:T(8,128)(2,1)S(1)}, u32[]{:S(2)}, u32[]{:S(2)}) collective-permute-start(bf16[14,48,512]{2,1,0:T(8,128)(2,1)} %get-tuple-element.52), channel_id=1, source_target_pairs={{0,7},{1,0},{2,1},{3,2},{4,3},{5,4},{6,5},{7,6},{8,15},{9,8},{10,9... | collective-permute-start | bytes 2064392 | tf_op jit(solution)/shard_map/ppermute | solution.py:491
  234.6 0.0 collective-permute-start.5
  234.6 12.9 %collective-permute-done.refs_0_ = bf16[14,48,512]{2,1,0:T(8,128)(2,1)S(1)} collective-permute-done((bf16[14,48,512]{2,1,0:T(8,128)(2,1)}, bf16[14,48,512]{2,1,0:T(8,128)(2,1)S(1)}, u32[]{:S(2)}, u32[]{:S(2)}) %collective-permute-start) | collective-permute-done | bytes 688160 | tf_op jit(solution)/shard_map/ppermute | solution.py:491
  247.5 3.6 %collective-permute-start.1 = (bf16[14,48,512]{2,1,0:T(8,128)(2,1)S(1)}, bf16[14,48,512]{2,1,0:T(8,128)(2,1)S(1)}, u32[]{:S(2)}, u32[]{:S(2)}) collective-permute-start(bf16[14,48,512]{2,1,0:T(8,128)(2,1)S(1)} %collective-permute-done.refs_0_), channel_id=1, source_target_pairs={{0,7},{1,0},{2,1},{3,2},{4,3},{5,4},{6,5},{7,6},{8,15},{9,8},{10,9... | collective-permute-start | bytes 2064392 | tf_op jit(solution)/shard_map/ppermute | solution.py:494
  251.1 0.0 collective-permute-done.2.refs_3_
  251.1 0.0 collective-permute-start.3
  251.1 16.3 %shard_map.215 = (bf16[2,8,64,1792]{3,2,1,0:T(8,128)(2,1)}, bf16[2,8,64,1792]{3,2,1,0:T(8,128)(2,1)}, bf16[2,7,8,32,512]{4,3,2,1,0:T(8,128)(2,1)}, f32[2,8,64,17...) custom-call(s32[5,4]{1,0:T(8,128)} %constant.12.clone.table, ...), custom_call_target="tpu_custom_call" | custom-call | flops 1376256000 | bytes 34406400 | tf_op jit(solution)/shard_map/pallas_call | solution.py:417
  267.4 0.0 copy-start
  267.4 16.1 %shard_map.216 = (bf16[2,8,64,1792]{3,2,1,0:T(8,128)(2,1)}, bf16[2,8,64,1792]{3,2,1,0:T(8,128)(2,1)}, bf16[2,7,8,32,512]{4,3,2,1,0:T(8,128)(2,1)}, f32[2,8,64,17...) custom-call(s32[5,4]{1,0:T(8,128)} %constant.13.clone.table, ...), custom_call_target="tpu_custom_call", output_to_operand_aliasing={{0}: (12, {}), {1}: (13, {}), {2}: (14, {}), {3}: (15, {}),... | custom-call | flops 1376256000 | bytes 34406400 | tf_op jit(solution)/shard_map/pallas_call | solution.py:417
  283.4 0.0 collective-permute-done.4.refs_1_
  283.5 0.0 collective-permute-done.5.refs_2_
  283.5 0.0 copy-done
  283.5 12.1 %shard_map.217 = (bf16[2,8,64,1792]{3,2,1,0:T(8,128)(2,1)}, bf16[2,8,64,1792]{3,2,1,0:T(8,128)(2,1)}, bf16[2,7,8,32,512]{4,3,2,1,0:T(8,128)(2,1)}, f32[2,8,64,17...) custom-call(s32[4,5]{1,0:T(4,128)S(1)} %copy-done, ...), custom_call_target="tpu_custom_call", output_to_operand_aliasing={{0}: (15, {}), {1}: (16, {}), {2}: (17, {}), {3}: (18, {}),... | custom-call | flops 1101004800 | bytes 27525120 | tf_op jit(solution)/shard_map/pallas_call | solution.py:417
  295.6 0.0 collective-permute-done.1.refs_0_
  295.6 0.0 copy-start.1
  295.6 0.0 collective-permute-done.3.refs_1_
  295.7 0.9 copy-done.1
  296.5 6.8 %shard_map.218 = (bf16[2,8,64,1792]{3,2,1,0:T(8,128)(2,1)}, bf16[2,8,64,1792]{3,2,1,0:T(8,128)(2,1)}, bf16[2,7,8,32,512]{4,3,2,1,0:T(8,128)(2,1)}, f32[2,8,64,17...) custom-call(s32[2,4]{1,0:T(2,128)} %constant.15.clone.table, ...), custom_call_target="tpu_custom_call", output_to_operand_aliasing={{0}: (13, {}), {1}: (14, {}), {2}: (15, {}), {3}: (16, {}),... | custom-call | flops 550502400 | bytes 13762560 | tf_op jit(solution)/shard_map/pallas_call | solution.py:417
Async XLA Ops:
  228.4 19.0 %collective-permute-start = (bf16[14,48,512]{2,1,0:T(8,128)(2,1)}, bf16[14,48,512]{2,1,0:T(8,128)(2,1)S(1)}, u32[]{:S(2)}, u32[]{:S(2)}) collective-permute-start(bf16[14,48,512]{2,1,0:T(8,128)(2,1)} %get-tuple-element.50), channel_id=1, source_target_pairs={{0,7},{1,0},{2,1},{3,2},{4,3},{5,4},{6,5},{7,6},{8,15},{9,8},{10,9... | collective-permute-start | bytes 2064392 | tf_op jit(solution)/shard_map/ppermute | solution.py:491
  231.3 19.7 %collective-permute-start.2 = (bf16[14,48,512]{2,1,0:T(8,128)(2,1)}, bf16[14,48,512]{2,1,0:T(8,128)(2,1)S(1)}, u32[]{:S(2)}, u32[]{:S(2)}) collective-permute-start(bf16[14,48,512]{2,1,0:T(8,128)(2,1)} %get-tuple-element.51), channel_id=1, source_target_pairs={{0,1},{1,2},{2,3},{3,4},{4,5},{5,6},{6,7},{7,0},{8,9},{9,10},{10,1... | collective-permute-start | bytes 2064392 | tf_op jit(solution)/shard_map/ppermute | solution.py:491
  231.3 52.1 %collective-permute-start.4 = (bf16[14,48,512]{2,1,0:T(8,128)(2,1)}, bf16[14,48,512]{2,1,0:T(8,128)(2,1)S(1)}, u32[]{:S(2)}, u32[]{:S(2)}) collective-permute-start(bf16[14,48,512]{2,1,0:T(8,128)(2,1)} %get-tuple-element.52), channel_id=1, source_target_pairs={{0,7},{1,0},{2,1},{3,2},{4,3},{5,4},{6,5},{7,6},{8,15},{9,8},{10,9... | collective-permute-start | bytes 2064392 | tf_op jit(solution)/shard_map/ppermute | solution.py:491
  234.6 48.9 %collective-permute-start.5 = (bf16[14,48,512]{2,1,0:T(8,128)(2,1)}, bf16[14,48,512]{2,1,0:T(8,128)(2,1)S(1)}, u32[]{:S(2)}, u32[]{:S(2)}) collective-permute-start(bf16[14,48,512]{2,1,0:T(8,128)(2,1)} %get-tuple-element.53), channel_id=1, source_target_pairs={{0,1},{1,2},{2,3},{3,4},{4,5},{5,6},{6,7},{7,0},{8,9},{9,10},{10,1... | collective-permute-start | bytes 2064392 | tf_op jit(solution)/shard_map/ppermute | solution.py:491
  247.5 48.2 %collective-permute-start.1 = (bf16[14,48,512]{2,1,0:T(8,128)(2,1)S(1)}, bf16[14,48,512]{2,1,0:T(8,128)(2,1)S(1)}, u32[]{:S(2)}, u32[]{:S(2)}) collective-permute-start(bf16[14,48,512]{2,1,0:T(8,128)(2,1)S(1)} %collective-permute-done.refs_0_), channel_id=1, source_target_pairs={{0,7},{1,0},{2,1},{3,2},{4,3},{5,4},{6,5},{7,6},{8,15},{9,8},{10,9... | collective-permute-start | bytes 2064392 | tf_op jit(solution)/shard_map/ppermute | solution.py:494
  251.1 44.6 %collective-permute-start.3 = (bf16[14,48,512]{2,1,0:T(8,128)(2,1)S(1)}, bf16[14,48,512]{2,1,0:T(8,128)(2,1)}, u32[]{:S(2)}, u32[]{:S(2)}) collective-permute-start(bf16[14,48,512]{2,1,0:T(8,128)(2,1)S(1)} %collective-permute-done.2.refs_3_), channel_id=1, source_target_pairs={{0,1},{1,2},{2,3},{3,4},{4,5},{5,6},{6,7},{7,0},{8,9},{9,10},{10,1... | collective-permute-start | bytes 2064392 | tf_op jit(solution)/shard_map/ppermute | solution.py:494
  267.4 16.1 %copy-start = (s32[4,5]{1,0:T(4,128)S(1)}, s32[4,5]{1,0:T(4,128)}, u32[]{:S(2)}) copy-start(s32[4,5]{1,0:T(4,128)} %constant.14.clone.table) | copy-start | bytes 244
  295.6 0.9 copy-start.1

commit v8 on v7

--- a/solution.py
+++ b/solution.py
@@ -122,8 +122,8 @@
             copies.append((self.out.at[slot, chunk], self.sums.at[t, chunk]))
         for way in (0, 1):
             chunk = self.chunk(way, self.kept)
-            for part in (0, 1):
-                copies.append((self.out.at[slot, chunk, self.part(part, True)], self.far[2 * way + part].at[t]))
+            for place, part in ((0, way), (1, 1 - way)):
+                copies.append((self.out.at[slot, chunk, self.part(part, True)], self.far[way].at[place, t]))
         return [pltpu.make_async_copy(a, b, self.out_sem.at[slot, i]) for i, (a, b) in enumerate(copies)]
 
     def event(self, slot, t, k):
@@ -157,13 +157,13 @@
 EVERY = 3
 
 
-def train_kernel(n, x, dy, wg, wu, wd, sums, far0, far1, far2, far3, dgu, w_gu, w_d, a1, a2, at, dyv, dyt, h1, pulled, act, buf0, buf1,
+def train_kernel(n, x, dy, wg, wu, wd, sums, far0, far1, dgu, w_gu, w_d, a1, a2, at, dyv, dyt, h1, pulled, act, buf0, buf1,
                  acc_gu, acc_d, own, got, out, sem, wsem, push_sem, pull_sem, send, recv, out_sem):
     layers, slices = w_d.shape[:2]
     tiles = x.shape[0]
     total = layers * slices
     barrier = pltpu.get_barrier_semaphore()
-    ring = Ring(n, own, got, out, sums, (far0, far1, far2, far3), send, recv, out_sem)
+    ring = Ring(n, own, got, out, sums, (far0, far1), send, recv, out_sem)
     for device in ring.to:
         pl.semaphore_signal(barrier, inc=1, device_id=device, device_id_type=pl.DeviceIdType.MESH)
 
@@ -349,17 +349,36 @@
     lax.fori_loop(0, tiles, turn, 0)
     backward(0)
 
-    def drain(now, _):
-        found = round_of(now)
-
-        def one(u, _):
-            events(found, u)
-            return 0
-
-        return lax.fori_loop(0, steps, one, 0)
-
-    end = total + turns
-    lax.fori_loop(end, end + 1 + offsets[-1] // steps, drain, 0)
+    left = {}
+    for t in range(total):
+        start = steps * (t + 1 + (turns if t >= slices else 0))
+        late = [(k, start + offset - steps * (total + turns)) for k, offset in enumerate(offsets)]
+        late = [(k, at) for k, at in late if at >= 0]
+        if late:
+            left[t] = late[0]
+    for t, k in drain_order(left, ring.half, ring.sends):
+        ring.event(t % SLOTS, t, k)
+
+
+def drain_order(left, half, sends):
+    step, beyond, now, wire, order = 0.92, 1.3, 0.0, 1.0, []
+    ready = {t: 0.0 if k == 0 else max(0.0, (at - EVERY) * step + 1 + beyond) for t, (k, at) in left.items()}
+    todo = {t: k for t, (k, _) in left.items()}
+    while todo:
+        can = [t for t, k in todo.items() if k < half - 1 or t - SLOTS not in todo]
+        rank = {t: (todo[t] if todo[t] <= sends else -1 if t + SLOTS in todo else sends + 1, -t) for t in can}
+        arrived = [t for t in can if ready[t] <= now]
+        t = min(arrived, key=lambda t: rank[t]) if arrived else min(can, key=lambda t: (ready[t], rank[t]))
+        k = todo[t]
+        now = max(now, ready[t]) + 0.05
+        order.append((t, k))
+        if k < sends:
+            wire = max(wire, now) + (0.5 if k == 0 else 1.0)
+        ready[t] = wire + beyond if k < sends else now + 0.5
+        todo[t] = k + 1
+        if k > sends:
+            del todo[t]
+    return order
 
 
 def adam_math(w, m, v, g):
@@ -369,18 +388,14 @@
     return (w - 0.02 * step).astype(BF16), m, v
 
 
-def adam_kernel(sources, table, me, *refs):
-    count = sum(sources)
-    gs, ins, outs = list(refs[:count]), refs[count : count + 9], refs[-9:]
-    which = table[pl.program_id(0), 2]
+def adam_kernel(pieces, me, *refs):
+    gs, ins, outs = refs[:pieces], refs[pieces : pieces + 9], refs[-9:]
     slices, wide = ins[2].shape[1], ins[0].shape[2]
     for j in range(slices):
-        g, place = None, 0
-        for i, pieces in enumerate(sources):
-            here = [r[j].reshape(r.shape[-2:]) for r in gs[place : place + pieces]]
-            here = (here[0] if pieces == 1 else jnp.concatenate(here, axis=0)).astype(F32)
-            g = here if g is None else jnp.where(which == i, here, g)
-            place += pieces
+        g = [(r[j] if r.shape[0] == slices else r[0, j]).reshape(r.shape[-2:]) for r in gs]
+        g = [g[0] if pieces == 1 else jnp.concatenate(g[i : i + 2], axis=0) for i in range(0, pieces, 2)]
+        g = [part.astype(F32) for part in g]
+        g = g[0] if len(g) == 1 else jnp.where(pl.program_id(1) == 0, g[0], g[1])
         columns = slice(j * FS, (j + 1) * FS)
         for i, here in ((0, (0, 0, slice(None), columns)), (1, (0, 0, slice(None), columns)), (2, (0, j, 0))):
             part = (g[:wide, :FS], g[:wide, FS:], g[wide:])[i]
@@ -390,45 +405,38 @@
                 outs[k * 3 + i][here] = new[k]
 
 
-def adam(n, steps, sources, arrays, so_far, vmem):
+def adam(n, first, stride, count, gs, arrays, so_far, vmem):
     layers, slices = arrays[0].shape[0], arrays[2].shape[1]
-    blocks = [layers - 1 - steps[0][0]] * len(sources)
-    table = []
-    for layer, offset, source in steps:
-        blocks[source] = layers - 1 - layer
-        table.append([layer, offset + n, source] + blocks)
-    table = jnp.array(table, jnp.int32)
     me = lax.axis_index("dp").astype(jnp.int32).reshape(1)
 
-    def chunk(s, table, me):
-        return lax.rem(me[0] + table[s, 1], n)
-
-    def spec(i, g):
+    def chunk(o, me):
+        return lax.rem(me[0] + o * stride + (first + n), n)
+
+    def spec(g, place):
+        if g.shape[1] == n:
+            return pl.BlockSpec((slices, 1) + g.shape[2:], lambda l, o, me: (layers - 1 - l, chunk(o, me), 0, 0))
         if g.ndim == 3:
-            return pl.BlockSpec((slices,) + g.shape[1:], lambda s, table, me: (table[s, 3 + i], 0, 0))
-        return pl.BlockSpec((slices, 1) + g.shape[2:], lambda s, table, me: (table[s, 3 + i], chunk(s, table, me), 0, 0))
-
-    wide = pl.BlockSpec((1, 1) + arrays[0].shape[2:], lambda s, table, me: (table[s, 0], chunk(s, table, me), 0, 0))
-    tall = pl.BlockSpec((1, slices, 1) + arrays[2].shape[3:], lambda s, table, me: (table[s, 0], 0, chunk(s, table, me), 0, 0))
+            return pl.BlockSpec((slices,) + g.shape[1:], lambda l, o, me: (layers - 1 - l, 0, 0))
+        return pl.BlockSpec((1, slices) + g.shape[2:], lambda l, o, me: (place, layers - 1 - l, 0, 0))
+
+    wide = pl.BlockSpec((1, 1) + arrays[0].shape[2:], lambda l, o, me: (l, chunk(o, me), 0, 0))
+    tall = pl.BlockSpec((1, slices, 1) + arrays[2].shape[3:], lambda l, o, me: (l, 0, chunk(o, me), 0, 0))
     specs = [wide, wide, tall] * 3
-    gs = [g for source in sources for g in source]
     extra = [] if so_far is None else list(so_far)
-    size = 2 * sum(a.size * a.dtype.itemsize for a in arrays) * len(steps) // (n * layers)
+    size = 2 * sum(a.size * a.dtype.itemsize for a in arrays) * count // n
     return pl.pallas_call(
-        functools.partial(adam_kernel, [len(source) for source in sources]),
+        functools.partial(adam_kernel, len(gs)),
         grid_spec=pltpu.PrefetchScalarGridSpec(
-            num_scalar_prefetch=2,
-            grid=(len(steps),),
-            in_specs=[spec(i, g) for i, source in enumerate(sources) for g in source]
-            + specs
-            + [pl.BlockSpec(memory_space=pl.ANY)] * len(extra),
+            num_scalar_prefetch=1,
+            grid=(layers, count),
+            in_specs=[spec(g, place) for g, place in gs] + specs + [pl.BlockSpec(memory_space=pl.ANY)] * len(extra),
             out_specs=specs,
         ),
         out_shape=[jax.ShapeDtypeStruct(a.shape, a.dtype) for a in arrays],
-        input_output_aliases={2 + len(gs) + 9 + i: i for i in range(len(extra))},
+        input_output_aliases={1 + len(gs) + 9 + i: i for i in range(len(extra))},
         compiler_params=pltpu.CompilerParams(vmem_limit_bytes=vmem),
         cost_estimate=pl.CostEstimate(flops=40 * size, bytes_accessed=size, transcendentals=0),
-    )(table, me, *gs, *arrays, *extra)
+    )(me, *[g for g, _ in gs], *arrays, *extra)
 
 
 def solution(mesh):
@@ -446,9 +454,9 @@
         sums, *far, _ = pl.pallas_call(
             functools.partial(train_kernel, n),
             in_specs=[hbm] * 5,
-            out_specs=[hbm] * 6,
+            out_specs=[hbm] * 4,
             out_shape=[jax.ShapeDtypeStruct((layers * slices, n, rows, d), BF16)]
-            + [jax.ShapeDtypeStruct((layers * slices, rows // 2, d), BF16)] * 4
+            + [jax.ShapeDtypeStruct((2, layers * slices, rows // 2, d), BF16)] * 2
             + [jax.ShapeDtypeStruct((tiles, TM, 2 * ff), BF16)],
             scratch_shapes=[
                 pltpu.VMEM((layers, d, 2 * ff), BF16),
@@ -483,19 +491,16 @@
         left = [(i, (i + n - 1) % n) for i in range(n)]
         right = [(i, (i + 1) % n) for i in range(n)]
 
-        first, second = range(layers)
         kept = half - 2
-        big, small = 60_000_000, 52_000_000
-        near, last = [None] * 4, []
-        for i, way in ((0, left), (3, right), (1, left), (2, right)):
-            near[i] = lax.ppermute(far[i], "dp", way)
-        new = adam(n, [(second, o, 0) for o in range(-kept, kept + 1)], [[sums]], chunks, None, big)
-        for i, way in ((0, left), (3, right)):
-            last.append(lax.ppermute(near[i], "dp", way))
-        new = adam(n, [(first, o, 0) for o in range(-kept, kept + 1)], [[sums]], chunks, new, big)
-        steps = [(l, sign * (kept + 1), way) for way, sign in ((0, 1), (1, -1)) for l in (second, first)]
-        new = adam(n, steps, [near[:2], near[2:]], chunks, new, small)
-        new = adam(n, [(second, half, 0), (first, half, 0)], [last], chunks, new, big)
+        near, last = [], []
+        for i, way in enumerate((left, right)):
+            near.append(lax.ppermute(far[i], "dp", way))
+        new = adam(n, -kept, 1, 2 * kept + 1, [(sums, 0)], chunks, None, 60_000_000)
+        for i, way in enumerate((left, right)):
+            last.append(lax.ppermute(near[i][0], "dp", way))
+        sides = [(near[0], 0), (near[0], 1), (near[1], 1), (near[1], 0)]
+        new = adam(n, kept + 1, -2 * (kept + 1), 2, sides, chunks, new, 52_000_000)
+        new = adam(n, half, 1, 1, [(a, 0) for a in last], chunks, new, 60_000_000)
         return tuple(o.reshape(a.shape) for o, a in zip(new, arrays))
 
     return jax.shard_map(

time: 304 us -> 306 us (level)
  the two profiles are of different devices: /device:TPU:22 before, /device:TPU:21 now
where the time goes in v8:
time: 306 us; the launch traced here: 303 us
  Pallas kernels  270 us (88%)
  waiting for transfers between devices  28 us (9%)
  starting transfers between devices  3.12 us (1%)
    pallas_call x1, Pallas kernels, step(): pl.pallas_call(functools.partial(train_kernel, n), in_specs=[hbm] * 5, ou...  226 us
    pallas_call x3, Pallas kernels, adam(): pl.pallas_call(functools.partial(adam_kernel, len(gs)), grid_spec=pltpu.P...  44.3 us
    ppermute x2, waiting for transfers between devices, step(): near.append(lax.ppermute(far[i], 'dp', way))  28 us
  transfers between devices with their start and end apart: 4, of which 1 were waited for; matrix products, arithmetic and copies ran while one was open for 0% of the time, Pallas kernels for 13%

profile of v8, /device:TPU:21, one launch (start us, length us, event | category | flops | bytes accessed | tf_op | source)
XLA Modules:
  0.0 303.0 jit_solution(11488601080098074575)
XLA Ops:
  0.6 225.8 %shard_map.178 = (bf16[14,8,96,512]{3,2,1,0:T(8,128)(2,1)}, bf16[2,14,48,512]{3,2,1,0:T(8,128)(2,1)}, bf16[2,14,48,512]{3,2,1,0:T(8,128)(2,1)}, bf16[8,512,3584]{2,1,0:T(8,128)(2,1)}) custom-call(bf16[8,512,512]{2,1,0:T(8,128)(2,1)} %bitcast.61, bf16[8,512,512]{2,1,0:T(8,128)(2,1)} %bitcast.62, bf16[2,512,1792]{2,1,0:T(8,128)(2,1)} %wg.1, ...), custom_call_target="tpu_custom_call" | custom-call | flops 127775277056 | bytes 90000000 | tf_op jit(solution)/shard_map/pallas_call | solution.py:454
  226.5 1.1 collective-permute-start
  227.6 0.5 collective-permute-start.2
  228.0 28.0 %collective-permute-done.refs_0_.refs_1_ = bf16[2,14,48,512]{3,2,1,0:T(8,128)(2,1)S(1)} collective-permute-done((bf16[2,14,48,512]{3,2,1,0:T(8,128)(2,1)}, bf16[2,14,48,512]{3,2,1,0:T(8,128)(2,1)S(1)}, u32[]{:S(2)}, u32[]{:S(2)}) %collective-permute-start) | collective-permute-done | bytes 1376288 | tf_op jit(solution)/shard_map/ppermute | solution.py:497
  256.1 1.3 collective-permute-start.1
  257.4 0.0 collective-permute-done.2.refs_2_.refs_3_
  257.4 0.9 slice_bitcast_fusion
  258.3 0.2 collective-permute-start.3
  258.6 26.9 %shard_map.179 = (bf16[2,8,64,1792]{3,2,1,0:T(8,128)(2,1)}, bf16[2,8,64,1792]{3,2,1,0:T(8,128)(2,1)}, bf16[2,7,8,32,512]{4,3,2,1,0:T(8,128)(2,1)}, f32[2,8,64,17...) custom-call(s32[1]{0:T(128)} %bitcast.me, ...), custom_call_target="tpu_custom_call" | custom-call | flops 2752512000 | bytes 68812800 | tf_op jit(solution)/shard_map/pallas_call | solution.py:427
  285.5 11.3 %shard_map.180 = (bf16[2,8,64,1792]{3,2,1,0:T(8,128)(2,1)}, bf16[2,8,64,1792]{3,2,1,0:T(8,128)(2,1)}, bf16[2,7,8,32,512]{4,3,2,1,0:T(8,128)(2,1)}, f32[2,8,64,17...) custom-call(s32[1]{0:T(128)} %bitcast.me, ...), custom_call_target="tpu_custom_call", output_to_operand_aliasing={{0}: (14, {}), {1}: (15, {}), {2}: (16, {}), {3}: (17, {}),... | custom-call | flops 1101004800 | bytes 27525120 | tf_op jit(solution)/shard_map/pallas_call | solution.py:427
  296.8 0.0 collective-permute-done.1.refs_0_
  296.8 0.0 collective-permute-done.3.refs_1_
  296.8 6.0 %shard_map.181 = (bf16[2,8,64,1792]{3,2,1,0:T(8,128)(2,1)}, bf16[2,8,64,1792]{3,2,1,0:T(8,128)(2,1)}, bf16[2,7,8,32,512]{4,3,2,1,0:T(8,128)(2,1)}, f32[2,8,64,17...) custom-call(s32[1]{0:T(128)} %bitcast.me, ...), custom_call_target="tpu_custom_call", output_to_operand_aliasing={{0}: (12, {}), {1}: (13, {}), {2}: (14, {}), {3}: (15, {}),... | custom-call | flops 550502400 | bytes 13762560 | tf_op jit(solution)/shard_map/pallas_call | solution.py:427
  (1 shorter events, 0.0 us)
Async XLA Ops:
  226.5 29.6 %collective-permute-start = (bf16[2,14,48,512]{3,2,1,0:T(8,128)(2,1)}, bf16[2,14,48,512]{3,2,1,0:T(8,128)(2,1)S(1)}, u32[]{:S(2)}, u32[]{:S(2)}) collective-permute-start(bf16[2,14,48,512]{3,2,1,0:T(8,128)(2,1)} %get-tuple-element.39), channel_id=1, source_target_pairs={{0,7},{1,0},{2,1},{3,2},{4,3},{5,4},{6,5},{7,6},{8,15},{9,8},{10,9... | collective-permute-start | bytes 4128776 | tf_op jit(solution)/shard_map/ppermute | solution.py:497
  227.6 29.9 %collective-permute-start.2 = (bf16[2,14,48,512]{3,2,1,0:T(8,128)(2,1)}, bf16[2,14,48,512]{3,2,1,0:T(8,128)(2,1)S(1)}, u32[]{:S(2)}, u32[]{:S(2)}) collective-permute-start(bf16[2,14,48,512]{3,2,1,0:T(8,128)(2,1)} %get-tuple-element.40), channel_id=1, source_target_pairs={{0,1},{1,2},{2,3},{3,4},{4,5},{5,6},{6,7},{7,0},{8,9},{9,10},{10,1... | collective-permute-start | bytes 4128776 | tf_op jit(solution)/shard_map/ppermute | solution.py:497
  256.1 40.7 %collective-permute-start.1 = (bf16[14,48,512]{2,1,0:T(8,128)(2,1)S(1)}, bf16[14,48,512]{2,1,0:T(8,128)(2,1)}, u32[]{:S(2)}, u32[]{:S(2)}) collective-permute-start(bf16[14,48,512]{2,1,0:T(8,128)(2,1)S(1)} %slice_bitcast_fusion.1), channel_id=1, source_target_pairs={{0,7},{1,0},{2,1},{3,2},{4,3},{5,4},{6,5},{7,6},{8,15},{9,8},{10,9... | collective-permute-start | bytes 2064392 | tf_op jit(solution)/shard_map/ppermute | solution.py:500
  258.3 38.5 %collective-permute-start.3 = (bf16[14,48,512]{2,1,0:T(8,128)(2,1)}, bf16[14,48,512]{2,1,0:T(8,128)(2,1)}, u32[]{:S(2)}, u32[]{:S(2)}) collective-permute-start(bf16[14,48,512]{2,1,0:T(8,128)(2,1)} %slice_bitcast_fusion), channel_id=1, source_target_pairs={{0,1},{1,2},{2,3},{3,4},{4,5},{5,6},{6,7},{7,0},{8,9},{9,10},{10,1... | collective-permute-start | bytes 2064392 | tf_op jit(solution)/shard_map/ppermute | solution.py:500

commit v9 on v8

--- a/solution.py
+++ b/solution.py
@@ -155,6 +155,7 @@
 
 SLOTS = 4
 EVERY = 3
+STARTS = (5, 9, 13, 20, 26, 27, 31, 41, 45, 49, 53, 63, 64, 65)
 
 
 def train_kernel(n, x, dy, wg, wu, wd, sums, far0, far1, dgu, w_gu, w_d, a1, a2, at, dyv, dyt, h1, pulled, act, buf0, buf1,
@@ -237,28 +238,41 @@
     pl.semaphore_wait(barrier, 2)
 
     steps = tiles // PAIR
-    turns = tiles // steps
-    offsets = [1 + EVERY * k for k in range(ring.sends + 1)] + [3 + EVERY * ring.sends]
-
-    def round_of(now):
-        found = []
-        for ago in range(1 + offsets[-1] // steps):
-            place = now - 1 - ago
-            t = jnp.where(place >= slices, place - turns, place)
-            there = (place >= 0) & (t < total) & ((place < slices) | (t >= slices))
-            found.append((there, t, lax.rem(t + SLOTS, SLOTS)))
-        return found
-
-    def events(found, u, odd=None):
-        for k in reversed(range(len(offsets))):
-            ago, at_step = divmod(offsets[k], steps)
-            if odd is not None and at_step % 2 != odd:
-                continue
-            there, t, slot = found[ago]
-
-            @pl.when((u == at_step) & there)
-            def _():
-                ring.event(slot, t, k)
+    turn_at, first_at, end_at = slices * steps, slices * steps + tiles, total * steps + tiles
+    soonest = [steps * (t + 1) + (tiles if t >= slices else 0) + 1 for t in range(total)]
+    starts = STARTS if len(STARTS) == total and all(a >= b for a, b in zip(STARTS, soonest)) else soonest
+    plan, left = {}, {}
+    for t, start in enumerate(starts):
+        for k in range(ring.sends + 2):
+            due = start + EVERY * k if k <= ring.sends else start + EVERY * ring.sends + 2
+            if due < end_at:
+                plan.setdefault(due, []).append((t, k))
+            elif t not in left:
+                left[t] = (k, due - end_at)
+    most, kinds, base = max(len(some) for some in plan.values()), ring.sends + 2, total * (ring.sends + 2) + 1
+
+    def events(step, low, high):
+        held = jnp.int32(0)
+        for due in range(low, high):
+            number = 0
+            for t, k in sorted(plan.get(due, ()), key=lambda e: e[1]):
+                number = number * base + t * kinds + k + 1
+            if number:
+                held = jnp.where(step == due, number, held)
+
+        def one(_, held):
+            here = lax.rem(held, base)
+            t = lax.div(lax.max(here - 1, 0), kinds)
+            which = here - 1 - t * kinds
+            for k in range(kinds):
+
+                @pl.when((here > 0) & (which == k))
+                def _():
+                    ring.event(lax.rem(t, SLOTS), t, k)
+
+            return lax.div(held, base)
+
+        lax.fori_loop(0, most, one, held)
 
     def finish(s):
         slot = lax.rem(s, SLOTS)
@@ -290,12 +304,10 @@
             slice_second(at.at[here], dyt.at[here], buf, acc_gu, acc_d)
 
         def one_slice(j, _):
-            found = round_of(j if second else slices + turns + j)
-
             def two_steps(i, _):
                 for half, here, there in ((0, buf0, buf1), (1, buf1, buf0)):
                     u = 2 * i + half
-                    events(found, u, half)
+                    events((0 if second else first_at) + j * steps + u, *((0, turn_at) if second else (first_at, end_at)))
                     if second:
                         @pl.when((i > 0) | (j > 0))
                         def _():
@@ -323,7 +335,7 @@
         finish((slices if second else total) - 1)
 
     def turn(m, _):
-        events(round_of(slices + m // steps), lax.rem(m, steps))
+        events(turn_at + m, turn_at, first_at)
         pull(m).wait()
         parts = 2
         size = TM // parts
@@ -349,13 +361,6 @@
     lax.fori_loop(0, tiles, turn, 0)
     backward(0)
 
-    left = {}
-    for t in range(total):
-        start = steps * (t + 1 + (turns if t >= slices else 0))
-        late = [(k, start + offset - steps * (total + turns)) for k, offset in enumerate(offsets)]
-        late = [(k, at) for k, at in late if at >= 0]
-        if late:
-            left[t] = late[0]
     for t, k in drain_order(left, ring.half, ring.sends):
         ring.event(t % SLOTS, t, k)
 
@@ -500,7 +505,7 @@
             last.append(lax.ppermute(near[i][0], "dp", way))
         sides = [(near[0], 0), (near[0], 1), (near[1], 1), (near[1], 0)]
         new = adam(n, kept + 1, -2 * (kept + 1), 2, sides, chunks, new, 52_000_000)
-        new = adam(n, half, 1, 1, [(a, 0) for a in last], chunks, new, 60_000_000)
+        new = adam(n, half, 1, 1, [(a, 0) for a in last], chunks, new, 52_000_000)
         return tuple(o.reshape(a.shape) for o, a in zip(new, arrays))
 
     return jax.shard_map(

time: 306 us -> 314 us (1.026)
  Pallas kernels: 270 us -> 277 us
    pallas_call x1, Pallas kernels: 226 us -> 233 us  [step(): pl.pallas_call(functools.partial(train_kernel, n), in_specs=[hbm] * 5, ou...]
  transfers between devices with their start and end apart: 4 -> 4, of which waited for: 1 -> 1; matrix products, arithmetic and copies ran while one was open for 0% -> 1% of each run, Pallas kernels for 13% -> 12%
where the time goes in v9:
time: 314 us; the launch traced here: 312 us
  Pallas kernels  277 us (88%)
  waiting for transfers between devices  29.3 us (9%)
    pallas_call x1, Pallas kernels, step(): pl.pallas_call(functools.partial(train_kernel, n), in_specs=[hbm] * 5, ou...  233 us
    pallas_call x3, Pallas kernels, adam(): pl.pallas_call(functools.partial(adam_kernel, len(gs)), grid_spec=pltpu.P...  44.1 us
    ppermute x2, waiting for transfers between devices, step(): near.append(lax.ppermute(far[i], 'dp', way))  29.3 us
  transfers between devices with their start and end apart: 4, of which 1 were waited for; matrix products, arithmetic and copies ran while one was open for 1% of the time, Pallas kernels for 12%

profile of v9, /device:TPU:21, one launch (start us, length us, event | category | flops | bytes accessed | tf_op | source)
XLA Modules:
  0.0 312.3 jit_solution(2767522827694117679)
XLA Ops:
  0.6 233.2 %shard_map.178 = (bf16[14,8,96,512]{3,2,1,0:T(8,128)(2,1)}, bf16[2,14,48,512]{3,2,1,0:T(8,128)(2,1)}, bf16[2,14,48,512]{3,2,1,0:T(8,128)(2,1)}, bf16[8,512,3584]{2,1,0:T(8,128)(2,1)}) custom-call(bf16[8,512,512]{2,1,0:T(8,128)(2,1)} %bitcast.61, bf16[8,512,512]{2,1,0:T(8,128)(2,1)} %bitcast.62, bf16[2,512,1792]{2,1,0:T(8,128)(2,1)} %wg.1, ...), custom_call_target="tpu_custom_call" | custom-call | flops 127775277056 | bytes 90000000 | tf_op jit(solution)/shard_map/pallas_call | solution.py:459
  233.9 0.3 collective-permute-start
  234.2 1.2 collective-permute-start.2
  235.4 29.2 %collective-permute-done.refs_0_.refs_1_ = bf16[2,14,48,512]{3,2,1,0:T(8,128)(2,1)S(1)} collective-permute-done((bf16[2,14,48,512]{3,2,1,0:T(8,128)(2,1)}, bf16[2,14,48,512]{3,2,1,0:T(8,128)(2,1)S(1)}, u32[]{:S(2)}, u32[]{:S(2)}) %collective-permute-start) | collective-permute-done | bytes 1376288 | tf_op jit(solution)/shard_map/ppermute | solution.py:502
  264.7 0.9 slice_bitcast_fusion.1
  265.6 0.6 collective-permute-start.1
  266.2 0.0 collective-permute-done.2.refs_2_.refs_3_
  266.2 0.9 slice_bitcast_fusion
  267.1 0.8 collective-permute-start.3
  268.0 26.9 %shard_map.179 = (bf16[2,8,64,1792]{3,2,1,0:T(8,128)(2,1)}, bf16[2,8,64,1792]{3,2,1,0:T(8,128)(2,1)}, bf16[2,7,8,32,512]{4,3,2,1,0:T(8,128)(2,1)}, f32[2,8,64,17...) custom-call(s32[1]{0:T(128)} %bitcast.me, ...), custom_call_target="tpu_custom_call" | custom-call | flops 2752512000 | bytes 68812800 | tf_op jit(solution)/shard_map/pallas_call | solution.py:432
  294.9 11.3 %shard_map.180 = (bf16[2,8,64,1792]{3,2,1,0:T(8,128)(2,1)}, bf16[2,8,64,1792]{3,2,1,0:T(8,128)(2,1)}, bf16[2,7,8,32,512]{4,3,2,1,0:T(8,128)(2,1)}, f32[2,8,64,17...) custom-call(s32[1]{0:T(128)} %bitcast.me, ...), custom_call_target="tpu_custom_call", output_to_operand_aliasing={{0}: (14, {}), {1}: (15, {}), {2}: (16, {}), {3}: (17, {}),... | custom-call | flops 1101004800 | bytes 27525120 | tf_op jit(solution)/shard_map/pallas_call | solution.py:432
  306.2 0.0 collective-permute-done.1.refs_0_
  306.2 0.0 collective-permute-done.3.refs_1_
  306.2 5.9 %shard_map.181 = (bf16[2,8,64,1792]{3,2,1,0:T(8,128)(2,1)}, bf16[2,8,64,1792]{3,2,1,0:T(8,128)(2,1)}, bf16[2,7,8,32,512]{4,3,2,1,0:T(8,128)(2,1)}, f32[2,8,64,17...) custom-call(s32[1]{0:T(128)} %bitcast.me, ...), custom_call_target="tpu_custom_call", output_to_operand_aliasing={{0}: (12, {}), {1}: (13, {}), {2}: (14, {}), {3}: (15, {}),... | custom-call | flops 550502400 | bytes 13762560 | tf_op jit(solution)/shard_map/pallas_call | solution.py:432
Async XLA Ops:
  233.9 30.8 %collective-permute-start = (bf16[2,14,48,512]{3,2,1,0:T(8,128)(2,1)}, bf16[2,14,48,512]{3,2,1,0:T(8,128)(2,1)S(1)}, u32[]{:S(2)}, u32[]{:S(2)}) collective-permute-start(bf16[2,14,48,512]{3,2,1,0:T(8,128)(2,1)} %get-tuple-element.39), channel_id=1, source_target_pairs={{0,7},{1,0},{2,1},{3,2},{4,3},{5,4},{6,5},{7,6},{8,15},{9,8},{10,9... | collective-permute-start | bytes 4128776 | tf_op jit(solution)/shard_map/ppermute | solution.py:502
  234.2 32.0 %collective-permute-start.2 = (bf16[2,14,48,512]{3,2,1,0:T(8,128)(2,1)}, bf16[2,14,48,512]{3,2,1,0:T(8,128)(2,1)S(1)}, u32[]{:S(2)}, u32[]{:S(2)}) collective-permute-start(bf16[2,14,48,512]{3,2,1,0:T(8,128)(2,1)} %get-tuple-element.40), channel_id=1, source_target_pairs={{0,1},{1,2},{2,3},{3,4},{4,5},{5,6},{6,7},{7,0},{8,9},{9,10},{10,1... | collective-permute-start | bytes 4128776 | tf_op jit(solution)/shard_map/ppermute | solution.py:502
  265.6 40.6 %collective-permute-start.1 = (bf16[14,48,512]{2,1,0:T(8,128)(2,1)}, bf16[14,48,512]{2,1,0:T(8,128)(2,1)S(1)}, u32[]{:S(2)}, u32[]{:S(2)}) collective-permute-start(bf16[14,48,512]{2,1,0:T(8,128)(2,1)} %slice_bitcast_fusion.1), channel_id=1, source_target_pairs={{0,7},{1,0},{2,1},{3,2},{4,3},{5,4},{6,5},{7,6},{8,15},{9,8},{10,9... | collective-permute-start | bytes 2064392 | tf_op jit(solution)/shard_map/ppermute | solution.py:505
  267.1 39.1 %collective-permute-start.3 = (bf16[14,48,512]{2,1,0:T(8,128)(2,1)}, bf16[14,48,512]{2,1,0:T(8,128)(2,1)}, u32[]{:S(2)}, u32[]{:S(2)}) collective-permute-start(bf16[14,48,512]{2,1,0:T(8,128)(2,1)} %slice_bitcast_fusion), channel_id=1, source_target_pairs={{0,1},{1,2},{2,3},{3,4},{4,5},{5,6},{6,7},{7,0},{8,9},{9,10},{10,1... | collective-permute-start | bytes 2064392 | tf_op jit(solution)/shard_map/ppermute | solution.py:505

commit v10 on v8

--- a/solution.py
+++ b/solution.py
@@ -187,17 +187,6 @@
     for j in range(slices):
         for c in weights(0, j)[:2]:
             c.start()
-    state(1).start()
-    for j in range(slices):
-        weights(0, j)[2].start()
-    cotangent(0).start()
-    for m in range(2, tiles):
-        state(m).start()
-        cotangent(m - 1).start()
-    cotangent(tiles - 1).start()
-    for j in range(slices):
-        for c in weights(1, j):
-            c.start()
 
     def forward_a(m, ready=lambda j: None):
         a1[m] = forward_first(h1[m], w_gu.at[0], act, ready)
@@ -218,11 +207,24 @@
         return 0
 
     def ready(j):
-        for first, last in ((0, 2), (2, slices)):
+        for first, last in ((0, 1), (1, slices)):
             if j == first:
                 for here in range(first, last):
                     for c in weights(0, here)[:2]:
                         c.wait()
+                if last < slices:
+                    for here in range(slices):
+                        weights(0, here)[2].start()
+                    state(1).start()
+                    cotangent(0).start()
+                else:
+                    for m in range(2, tiles):
+                        state(m).start()
+                        cotangent(m - 1).start()
+                    cotangent(tiles - 1).start()
+                    for here in range(slices):
+                        for c in weights(1, here):
+                            c.start()
 
     state(0).wait()
     forward_a(0, ready)
@@ -250,7 +252,7 @@
         return found
 
     def events(found, u, odd=None):
-        for k in reversed(range(len(offsets))):
+        for k in range(len(offsets)):
             ago, at_step = divmod(offsets[k], steps)
             if odd is not None and at_step % 2 != odd:
                 continue
@@ -500,7 +502,7 @@
             last.append(lax.ppermute(near[i][0], "dp", way))
         sides = [(near[0], 0), (near[0], 1), (near[1], 1), (near[1], 0)]
         new = adam(n, kept + 1, -2 * (kept + 1), 2, sides, chunks, new, 52_000_000)
-        new = adam(n, half, 1, 1, [(a, 0) for a in last], chunks, new, 60_000_000)
+        new = adam(n, half, 1, 1, [(a, 0) for a in last], chunks, new, 52_000_000)
         return tuple(o.reshape(a.shape) for o, a in zip(new, arrays))
 
     return jax.shard_map(

time: 306 us -> 305 us (level)
  transfers between devices with their start and end apart: 4 -> 4, of which waited for: 1 -> 1; matrix products, arithmetic and copies ran while one was open for 0% -> 1% of each run, Pallas kernels for 13% -> 13%
where the time goes in v10:
time: 305 us; the launch traced here: 303 us
  Pallas kernels  269 us (88%)
  waiting for transfers between devices  28.3 us (9%)
    pallas_call x1, Pallas kernels, step(): pl.pallas_call(functools.partial(train_kernel, n), in_specs=[hbm] * 5, ou...  225 us
    pallas_call x3, Pallas kernels, adam(): pl.pallas_call(functools.partial(adam_kernel, len(gs)), grid_spec=pltpu.P...  44.1 us
    ppermute x2, waiting for transfers between devices, step(): near.append(lax.ppermute(far[i], 'dp', way))  28.3 us
  transfers between devices with their start and end apart: 4, of which 1 were waited for; matrix products, arithmetic and copies ran while one was open for 1% of the time, Pallas kernels for 13%

profile of v10, /device:TPU:21, one launch (start us, length us, event | category | flops | bytes accessed | tf_op | source)
XLA Modules:
  0.0 302.6 jit_solution(13315053720084997967)
XLA Ops:
  0.6 224.6 %shard_map.178 = (bf16[14,8,96,512]{3,2,1,0:T(8,128)(2,1)}, bf16[2,14,48,512]{3,2,1,0:T(8,128)(2,1)}, bf16[2,14,48,512]{3,2,1,0:T(8,128)(2,1)}, bf16[8,512,3584]{2,1,0:T(8,128)(2,1)}) custom-call(bf16[8,512,512]{2,1,0:T(8,128)(2,1)} %bitcast.61, bf16[8,512,512]{2,1,0:T(8,128)(2,1)} %bitcast.62, bf16[2,512,1792]{2,1,0:T(8,128)(2,1)} %wg.1, ...), custom_call_target="tpu_custom_call" | custom-call | flops 127775277056 | bytes 90000000 | tf_op jit(solution)/shard_map/pallas_call | solution.py:456
  225.2 0.9 collective-permute-start
  226.2 0.6 collective-permute-start.2
  226.8 28.3 %collective-permute-done.refs_0_.refs_1_ = bf16[2,14,48,512]{3,2,1,0:T(8,128)(2,1)S(1)} collective-permute-done((bf16[2,14,48,512]{3,2,1,0:T(8,128)(2,1)}, bf16[2,14,48,512]{3,2,1,0:T(8,128)(2,1)S(1)}, u32[]{:S(2)}, u32[]{:S(2)}) %collective-permute-start) | collective-permute-done | bytes 1376288 | tf_op jit(solution)/shard_map/ppermute | solution.py:499
  255.0 0.9 slice_bitcast_fusion.1
  255.9 0.7 collective-permute-start.1
  256.7 0.0 collective-permute-done.2.refs_2_.refs_3_
  256.7 0.9 slice_bitcast_fusion
  257.6 0.7 collective-permute-start.3
  258.3 26.9 %shard_map.179 = (bf16[2,8,64,1792]{3,2,1,0:T(8,128)(2,1)}, bf16[2,8,64,1792]{3,2,1,0:T(8,128)(2,1)}, bf16[2,7,8,32,512]{4,3,2,1,0:T(8,128)(2,1)}, f32[2,8,64,17...) custom-call(s32[1]{0:T(128)} %bitcast.me, ...), custom_call_target="tpu_custom_call" | custom-call | flops 2752512000 | bytes 68812800 | tf_op jit(solution)/shard_map/pallas_call | solution.py:429
  285.3 11.3 %shard_map.180 = (bf16[2,8,64,1792]{3,2,1,0:T(8,128)(2,1)}, bf16[2,8,64,1792]{3,2,1,0:T(8,128)(2,1)}, bf16[2,7,8,32,512]{4,3,2,1,0:T(8,128)(2,1)}, f32[2,8,64,17...) custom-call(s32[1]{0:T(128)} %bitcast.me, ...), custom_call_target="tpu_custom_call", output_to_operand_aliasing={{0}: (14, {}), {1}: (15, {}), {2}: (16, {}), {3}: (17, {}),... | custom-call | flops 1101004800 | bytes 27525120 | tf_op jit(solution)/shard_map/pallas_call | solution.py:429
  296.5 0.0 collective-permute-done.1.refs_0_
  296.5 0.0 collective-permute-done.3.refs_1_
  296.6 5.9 %shard_map.181 = (bf16[2,8,64,1792]{3,2,1,0:T(8,128)(2,1)}, bf16[2,8,64,1792]{3,2,1,0:T(8,128)(2,1)}, bf16[2,7,8,32,512]{4,3,2,1,0:T(8,128)(2,1)}, f32[2,8,64,17...) custom-call(s32[1]{0:T(128)} %bitcast.me, ...), custom_call_target="tpu_custom_call", output_to_operand_aliasing={{0}: (12, {}), {1}: (13, {}), {2}: (14, {}), {3}: (15, {}),... | custom-call | flops 550502400 | bytes 13762560 | tf_op jit(solution)/shard_map/pallas_call | solution.py:429
Async XLA Ops:
  225.2 29.8 %collective-permute-start = (bf16[2,14,48,512]{3,2,1,0:T(8,128)(2,1)}, bf16[2,14,48,512]{3,2,1,0:T(8,128)(2,1)S(1)}, u32[]{:S(2)}, u32[]{:S(2)}) collective-permute-start(bf16[2,14,48,512]{3,2,1,0:T(8,128)(2,1)} %get-tuple-element.39), channel_id=1, source_target_pairs={{0,7},{1,0},{2,1},{3,2},{4,3},{5,4},{6,5},{7,6},{8,15},{9,8},{10,9... | collective-permute-start | bytes 4128776 | tf_op jit(solution)/shard_map/ppermute | solution.py:499
  226.2 30.5 %collective-permute-start.2 = (bf16[2,14,48,512]{3,2,1,0:T(8,128)(2,1)}, bf16[2,14,48,512]{3,2,1,0:T(8,128)(2,1)S(1)}, u32[]{:S(2)}, u32[]{:S(2)}) collective-permute-start(bf16[2,14,48,512]{3,2,1,0:T(8,128)(2,1)} %get-tuple-element.40), channel_id=1, source_target_pairs={{0,1},{1,2},{2,3},{3,4},{4,5},{5,6},{6,7},{7,0},{8,9},{9,10},{10,1... | collective-permute-start | bytes 4128776 | tf_op jit(solution)/shard_map/ppermute | solution.py:499
  255.9 40.6 %collective-permute-start.1 = (bf16[14,48,512]{2,1,0:T(8,128)(2,1)}, bf16[14,48,512]{2,1,0:T(8,128)(2,1)S(1)}, u32[]{:S(2)}, u32[]{:S(2)}) collective-permute-start(bf16[14,48,512]{2,1,0:T(8,128)(2,1)} %slice_bitcast_fusion.1), channel_id=1, source_target_pairs={{0,7},{1,0},{2,1},{3,2},{4,3},{5,4},{6,5},{7,6},{8,15},{9,8},{10,9... | collective-permute-start | bytes 2064392 | tf_op jit(solution)/shard_map/ppermute | solution.py:502
  257.6 39.0 %collective-permute-start.3 = (bf16[14,48,512]{2,1,0:T(8,128)(2,1)}, bf16[14,48,512]{2,1,0:T(8,128)(2,1)}, u32[]{:S(2)}, u32[]{:S(2)}) collective-permute-start(bf16[14,48,512]{2,1,0:T(8,128)(2,1)} %slice_bitcast_fusion), channel_id=1, source_target_pairs={{0,1},{1,2},{2,3},{3,4},{4,5},{5,6},{6,7},{7,0},{8,9},{9,10},{10,1... | collective-permute-start | bytes 2064392 | tf_op jit(solution)/shard_map/ppermute | solution.py:502
